TPU v7x, 32 devices: a whole 2x2x4 slice. The times are simulated.
32 devices in a mesh: base: 4 (over y, x), slab: 8 (over z, core).
Axes of the slice: x: 2, y: 2, z: 4, core: 2. Of those that a mesh axis runs over, the one named last changes fastest.
Arguments:
- residual: float32 [4096, 2, 128], P(('base', 'slab')), may hold values from -6 to 6
- position: float32 [4096, 2, 128], P(('base', 'slab')), may hold values from 4 to 124
- owner: int32 [4096, 1], P(('base', 'slab')), may hold values from 0 to 31; in each aligned block of 128 rows (0 to 127, 128 to 255, ...) at most 8 rows name the same one
- tile_local: int32 [4096], P(('base', 'slab')), may hold values from 0 to 127
- xi: float32 [4096, 4096], P(('base', 'slab')), may hold values from -6 to 6
- amplitude: float32 [4096, 4096], P(('base', 'slab')), may hold values from 0.05 to 0.5
Outputs:
- gradient: float32 [4096, 4096], P(('base', 'slab'))
Inputs may be any that keep to these rules, and one draw needn't show every extreme that they name: Among the blocks of one device no owner region is named by more than 8 blocks, a bound that some owner region reaches on some device.
All inputs are finite; a program needn't handle non-finite values.
Results may differ from a plain program's by a relative error of at most 0.00065.
Values sent between devices are 32-bit elements; how exact they have to be, the bound alone decides.
A program may use at most 128 MiB of HBM per device.

v0:
```python
import functools
import math

import jax
import jax.numpy as jnp
import numpy as np
from jax import lax
from jax.experimental import pallas as pl
from jax.experimental.pallas import tpu as pltpu
from jax.sharding import PartitionSpec as P

G = 8192
TILE = 128
both = ("base", "slab")
fine = lax.Precision.HIGHEST


def trig(product, modulus):
    angle = (product % modulus).astype(np.float64) * (2.0 * np.pi / modulus)
    return np.cos(angle), np.sin(angle)


def column_table(n, size):
    depth = size // n
    half = depth // 2
    i = np.arange(half)[None, :]
    j = np.arange(n)[:, None]
    low = n * i + j
    high = (-low) % size
    high[0, 0] = size // 2
    return np.concatenate([low, high], axis=1)


def row_tables(n, size):
    depth = size // n
    cols = column_table(n, size)
    oc, osn = trig(np.arange(n)[:, None] * np.arange(n)[None, :], n)
    outer = np.stack([oc, osn], axis=1)
    prod = np.arange(depth)[None, :, None] * cols[:, None, :]
    c, s = trig(prod, size)
    sign = np.where(np.arange(depth) < depth // 2, 1.0, -1.0)[None, None, :]
    inner = np.stack([c + s, sign * (c - s)], axis=1)
    return outer.astype(np.float32), inner.astype(np.float32)


def grid_row_tables(n, size):
    depth = G // n
    cols = column_table(n, size)
    half = cols.shape[1] // 2
    oc, osn = trig(np.arange(n)[:, None] * np.arange(n)[None, :], n)
    outer = np.stack([np.stack([oc, osn], 1), np.stack([-osn, oc], 1)], 0)
    low = cols[:, :half]
    high = cols[(-np.arange(n)) % n, half:]
    a = np.arange(depth)[None, :, None]
    out = []
    for part in (low, high):
        c, s = trig(a * (part[:, None, :] + G // 4), G)
        out.append(np.stack([np.concatenate([c, s], 2), np.concatenate([-s, c], 2)], 1))
    return outer.astype(np.float32), np.concatenate(out, axis=3).astype(np.float32)


def taps(cells, offsets):
    scaled = (cells - offsets) * 0.25
    kept = jnp.maximum(1.0 - scaled * scaled, 0.0)
    return kept * kept * kept


def split_three(x):
    high = x.astype(jnp.bfloat16)
    rest = x - high.astype(jnp.float32)
    middle = rest.astype(jnp.bfloat16)
    return high, middle, (rest - middle.astype(jnp.float32)).astype(jnp.bfloat16)


def grid_kernel(rows, info_ref, list_ref, data_ref, out_ref):
    count = info_ref[0]
    first = info_ref[1].astype(jnp.float32)
    out_ref[...] = jnp.zeros_like(out_ref)
    row_cells = lax.broadcasted_iota(jnp.int32, (rows, TILE), 0).astype(jnp.float32) + first
    col_cells = lax.broadcasted_iota(jnp.int32, (TILE, TILE), 0).astype(jnp.float32)

    def step(k, carry):
        packed = list_ref[k]
        index = packed // 256
        col = (packed // 2) % 128
        flip = (packed % 2).astype(jnp.float32)
        sign = 1.0 - 2.0 * flip
        start = 128.0 * flip
        block = data_ref[index]
        value = block[0:2, :]
        place = block[2:4, :]
        row_taps = taps(row_cells * sign + start, place[0:1, :])
        col_taps = taps(col_cells * sign + start, place[1:2, :])
        weighted = jnp.concatenate(
            [col_taps * value[0:1, :], col_taps * (value[1:2, :] * sign)], axis=0
        )
        rh, rm, rl = split_three(row_taps)
        wh, wm, wl = split_three(weighted)
        left = jnp.concatenate([rh, rh, rh, rm, rm, rl], axis=1)
        right = jnp.concatenate([wh, wm, wl, wh, wm, wh], axis=1)
        sub = lax.dot_general(
            left, right, (((1,), (1,)), ((), ())), preferred_element_type=jnp.float32
        )
        out_ref[0, col] += sub[:, :TILE]
        out_ref[1, col] += sub[:, TILE:]
        return carry

    lax.fori_loop(0, count, step, 0)


def grid_rows(info, table, gathered, rows):
    tiles = G // TILE
    smem = pl.BlockSpec(memory_space=pltpu.SMEM)
    vmem = pl.BlockSpec(memory_space=pltpu.VMEM)
    return pl.pallas_call(
        functools.partial(grid_kernel, rows),
        out_shape=jax.ShapeDtypeStruct((2, tiles, rows, TILE), jnp.float32),
        in_specs=[smem, smem, vmem],
        out_specs=vmem,
        compiler_params=pltpu.CompilerParams(vmem_limit_bytes=56 * 1024 * 1024),
        cost_estimate=pl.CostEstimate(
            flops=2 * 10**10, bytes_accessed=16 * 2**20, transcendentals=0
        ),
        name="grid_rows",
    )(info, table, gathered)


def einsum(form, *args, precision=lax.Precision.HIGH):
    return jnp.einsum(form, *args, precision=precision, preferred_element_type=jnp.float32)


def general(residual, position, owner, tile_local, xi, amplitude):
    n = lax.axis_size(both)
    n_base = lax.axis_size("base")
    n_slab = lax.axis_size("slab")
    me = lax.axis_index(both)
    rows, size = xi.shape
    depth = size // n
    half = depth // 2
    tiles = G // TILE

    region_rows = G // n_slab // TILE
    region_cols = G // n_base // TILE
    target = owner[:, 0]
    tile_row = (target % n_slab) * region_rows + tile_local // region_cols
    tile_col = (target // n_slab) * region_cols + tile_local % region_cols
    flip = tile_row >= tiles // 2
    tile_row = jnp.where(flip, tiles - 1 - tile_row, tile_row)
    tile_col = jnp.where(flip, tiles - 1 - tile_col, tile_col)
    code = tile_row * 256 + tile_col * 2 + flip.astype(jnp.int32)
    codes = lax.all_gather(code, both, axis=0, tiled=True)
    payload = jnp.concatenate([residual, position], axis=1)
    codes, payload = lax.optimization_barrier((codes, payload))
    gathered = lax.all_gather(payload, both, axis=0, tiled=True)
    blocks = codes.shape[0]
    grid_depth = G // 2 // n
    first_row = me * grid_depth
    mine = (codes // 256 == first_row // TILE).astype(jnp.int32)
    rank = jnp.where(mine == 1, jnp.cumsum(mine) - 1, -1)
    packed = lax.broadcasted_iota(jnp.int32, (blocks,), 0) * 256 + codes % 256
    spots = lax.broadcasted_iota(jnp.int32, (blocks, blocks), 0)
    table = jnp.sum(jnp.where(spots == rank[None, :], packed[None, :], 0), axis=1)
    info = jnp.stack([jnp.sum(mine), first_row % TILE]).astype(jnp.int32)

    outer, inner = row_tables(n, size)
    spectrum = (amplitude * xi).reshape(rows, n, depth)
    mid = einsum("rba,bqc->qcra", spectrum, outer)
    sent = einsum("cra,cae->cre", mid[0], inner[:, 0]) + einsum("cra,cae->cre", mid[1], inner[:, 1])
    sent, gathered = lax.optimization_barrier((sent, gathered))
    field = lax.all_to_all(sent, both, split_axis=0, concat_axis=0, tiled=True)
    field = field.reshape(size, depth)
    lane = lax.broadcasted_iota(jnp.int32, (1, depth), 1)
    still = (me == 0) & (lane % half == 0)

    def mirror(x):
        return jnp.where(still, x, jnp.roll(x, half, axis=-1))

    c_len = 128
    d_len = size // c_len
    bc, bs = (x.astype(np.float32) for x in trig(np.arange(c_len)[:, None] * np.arange(c_len)[None, :], c_len))
    shape = (c_len, d_len, depth)
    n0 = c_len * np.arange(d_len)[None, :] + np.arange(c_len)[:, None]
    ic, isn = (x.astype(np.float32) for x in trig(n0[:, :, None] * np.arange(d_len)[None, None, :], size))
    pair = jnp.stack([field.reshape(shape), mirror(field).reshape(shape)])
    first = np.stack([np.stack([bc, bs], 1), np.stack([bs, -bc], 1)], 0)
    turned = einsum("qbal,qbsc->csal", pair, first)
    second = np.stack([ic, -isn], axis=2)
    power = einsum("csal,cdsa->cdl", turned, second)
    sky = jnp.exp(power / size)

    grid = grid_rows(info, table, gathered, grid_depth)
    outer_g, inner_g = grid_row_tables(n, size)
    parts = tiles // n if tiles >= n else 1
    inner_len = G // n
    if inner_len >= TILE:
        view = grid.reshape(2, n, inner_len // TILE, grid_depth, TILE)
    else:
        flat = grid.transpose(0, 2, 1, 3).reshape(2, grid_depth, n, inner_len)
        view = flat.transpose(0, 2, 1, 3)[:, :, None]
        parts = 1
    lanes = view.shape[-1]
    stage = einsum("qbpra,qbsc->cspra", view, outer_g, precision=fine)
    inner_g = inner_g.reshape(n, 2, parts, lanes, 2 * depth)
    halves = einsum("cspra,cspae->cre", stage, inner_g, precision=fine)
    high = halves[:, :, depth:]
    high = jnp.concatenate([high[:1], jnp.flip(high[1:], axis=0)], axis=0)
    halves = jnp.concatenate([halves[:, :, :depth], high], axis=2)
    got = lax.all_to_all(halves, both, split_axis=0, concat_axis=0, tiled=True)
    got = got.reshape(size, 2 * depth)
    real = jnp.concatenate([got[:, :half], got[:, depth : depth + half]], axis=1)
    imag = jnp.concatenate([got[:, half:depth], got[:, depth + half :]], axis=1)
    wide = G // c_len
    deep = size // wide
    gc, gs = (x.astype(np.float32) for x in trig(np.arange(deep)[:, None] * np.arange(c_len)[None, :], c_len))
    first_g = np.stack([np.stack([gc, gs], 1), np.stack([-gs, gc], 1)], 0)
    whole = jnp.stack([real.reshape(deep, wide, depth), imag.reshape(deep, wide, depth)])
    turned_g = einsum("qbal,qbsc->csal", whole, first_g, precision=fine)
    ac, asn = trig((n0 + G // 4)[:, :, None] * np.arange(wide)[None, None, :], G)
    second_g = (np.stack([ac, -asn], axis=2) / G).astype(np.float32)
    back = einsum("csal,cdsa->cdl", turned_g, second_g, precision=fine)

    z = sky * back
    pz = einsum("cdl,cda->cal", z, ic)
    qz = einsum("cdl,cda->cal", z, isn)
    joined = jnp.stack([pz + mirror(qz), mirror(pz) - qz])
    fold = einsum("qcal,qcb->bal", joined, np.stack([bc, bs]))
    folded = lax.all_to_all(
        fold.reshape(n, rows, depth), both, split_axis=0, concat_axis=0, tiled=True
    )
    ends = einsum("jre,jqae->qjra", folded, inner)
    final = einsum("qjra,bqj->rba", ends, outer)
    return amplitude * final.reshape(rows, size) / size


MESH = pl.DeviceIdType.MESH
parts = ("base", "half", "quad")


def exchange_kernel(nb, ns, send_ref, out_ref, bsend, brecv, usend, dsend, lrecv, hrecv, psend, precv, lsem):
    quads = ns // 2
    nz = ns // 2
    base = lax.axis_index("base")
    slab = lax.axis_index("half") * quads + lax.axis_index("quad")
    z = slab // 2
    core = slab % 2

    def at(b, s):
        return (b, s // quads, s % quads)

    def copy(source, target, here, there, device):
        return pltpu.make_async_remote_copy(
            src_ref=source, dst_ref=target, send_sem=here, recv_sem=there, device_id=device, device_id_type=MESH
        )

    def crossing(k):
        other = (base + k) % nb
        return copy(send_ref.at[other], out_ref.at[slab, base], bsend.at[k], brecv.at[k], at(other, slab))

    def arriving(k):
        from_base = (base - k + nb) % nb
        return copy(send_ref.at[base], out_ref.at[slab, from_base], bsend.at[k], brecv.at[k], at(from_base, slab))

    def block(origin, k):
        return out_ref.at[2 * origin + core, (base - k + nb) % nb]

    def upward(s, k):
        part = block(z - s, k)
        return copy(part, part, usend.at[s, k], lrecv.at[s + 1, k], at(base, slab + 2))

    def downward(s, k):
        part = block(z + s, k)
        return copy(part, part, dsend.at[s, k], hrecv.at[s + 1, k], at(base, slab - 2))

    def from_below(s, k):
        part = block(z - s, k)
        return copy(part, part, usend.at[s, k], lrecv.at[s, k], at(base, slab - 2))

    def from_above(s, k):
        part = block(z + s, k)
        return copy(part, part, dsend.at[s, k], hrecv.at[s, k], at(base, slab + 2))

    def across(origin, k):
        part = block(origin, k)
        return copy(part, part, psend.at[origin, k], precv.at[origin, k], at(base, slab + 1 - 2 * core))

    def from_partner(origin, k):
        part = out_ref.at[2 * origin + 1 - core, (base - k + nb) % nb]
        return copy(part, part, psend.at[origin, k], precv.at[origin, k], at(base, slab + 1 - 2 * core))

    barrier = pltpu.get_barrier_semaphore()
    for k in range(1, nb):
        pl.semaphore_signal(barrier, inc=1, device_id=at((base + k) % nb, slab), device_id_type=MESH)
    pl.semaphore_signal(barrier, inc=1, device_id=at(base, slab + 1 - 2 * core), device_id_type=MESH)

    @pl.when(z < nz - 1)
    def _():
        pl.semaphore_signal(barrier, inc=1, device_id=at(base, slab + 2), device_id_type=MESH)

    @pl.when(z > 0)
    def _():
        pl.semaphore_signal(barrier, inc=1, device_id=at(base, slab - 2), device_id_type=MESH)

    pl.semaphore_wait(barrier, nb + jnp.where(z < nz - 1, 1, 0) + jnp.where(z > 0, 1, 0))

    for k in range(1, nb):
        crossing(k).start()
    own = pltpu.make_async_copy(send_ref.at[base], out_ref.at[slab, base], lsem)
    own.start()

    def pass_on(s, k, ascending, descending):
        if ascending:
            @pl.when((z - s >= 0) & (z < nz - 1))
            def _():
                upward(s, k).start()

        if descending:
            @pl.when((z + s < nz) & (z > 0))
            def _():
                downward(s, k).start()

    for k in range(nb):
        if k == 0:
            own.wait()
        else:
            arriving(k).wait_recv()
        pass_on(0, k, True, True)
        across(z, k).start()
    for s in range(1, nz):
        for k in range(nb):
            @pl.when(z - s >= 0)
            def _():
                from_below(s, k).wait_recv()
                if s < nz - 1:
                    pass_on(s, k, True, False)
                across(z - s, k).start()

            @pl.when(z + s < nz)
            def _():
                from_above(s, k).wait_recv()
                if s < nz - 1:
                    pass_on(s, k, False, True)
                across(z + s, k).start()

    for origin in range(nz):
        for k in range(nb):
            from_partner(origin, k).wait_recv()
    for k in range(1, nb):
        crossing(k).wait_send()
    for s in range(nz - 1):
        for k in range(nb):
            @pl.when((z - s >= 0) & (z < nz - 1))
            def _():
                upward(s, k).wait_send()

            @pl.when((z + s < nz) & (z > 0))
            def _():
                downward(s, k).wait_send()

    for origin in range(nz):
        for k in range(nb):
            across(origin, k).wait_send()


def exchange(sent, ns):
    nb = sent.shape[0]
    nz = ns // 2
    dma = pltpu.SemaphoreType.DMA
    vmem = pl.BlockSpec(memory_space=pltpu.VMEM)
    return pl.pallas_call(
        functools.partial(exchange_kernel, nb, ns),
        out_shape=jax.ShapeDtypeStruct((ns,) + sent.shape, jnp.float32),
        in_specs=[vmem],
        out_specs=vmem,
        scratch_shapes=[
            dma((nb,)), dma((nb,)), dma((nz, nb)), dma((nz, nb)), dma((nz, nb)), dma((nz, nb)),
            dma((nz, nb)), dma((nz, nb)), dma,
        ],
        compiler_params=pltpu.CompilerParams(collective_id=0, has_side_effects=True, vmem_limit_bytes=16 << 20),
        name="exchange",
    )(sent)


def two_parts(x):
    high = x.astype(jnp.bfloat16)
    return high, (x - high.astype(jnp.float32)).astype(jnp.bfloat16)


def times(x, c, s):
    return x[0] * c - x[1] * s, x[0] * s + x[1] * c


def turn(x, angle):
    c, s = math.cos(angle), math.sin(angle)
    return times(x, c, s)


def add(x, y):
    return x[0] + y[0], x[1] + y[1]


def sub(x, y):
    return x[0] - y[0], x[1] - y[1]


def four(x):
    s0, d0, s1, d1 = add(x[0], x[2]), sub(x[0], x[2]), add(x[1], x[3]), sub(x[1], x[3])
    i1 = (-d1[1], d1[0])
    return [add(s0, s1), add(d0, i1), sub(s0, s1), sub(d0, i1)]


def sixteen(x):
    rows = []
    for b0 in range(4):
        y = four([x[4 * b1 + b0] for b1 in range(4)])
        rows.append([y[a0] if a0 * b0 == 0 else turn(y[a0], 2 * math.pi * a0 * b0 / 16) for a0 in range(4)])
    out = [None] * 16
    for a0 in range(4):
        y = four([rows[b0][a0] for b0 in range(4)])
        for a1 in range(4):
            out[a0 + 4 * a1] = y[a1]
    return out


def grid_rows_kernel(info_ref, list_ref, first_ref, data_ref, turn_ref, undo_ref, weight_ref, out_ref, grid_ref):
    count = info_ref[0]
    parity = info_ref[1]
    grid_ref[...] = jnp.zeros_like(grid_ref)
    cells = lax.broadcasted_iota(jnp.int32, (TILE, TILE), 0).astype(jnp.float32) * 0.25
    half = grid_ref.shape[1]

    def bump(offsets):
        d = cells - offsets
        kept = jnp.maximum(1.0 - d * d, 0.0)
        return kept * kept * kept

    def steps(offsets):
        offsets = offsets * 0.25
        return bump(offsets) - bump(offsets - 0.25)

    def one(k):
        packed = list_ref[k]
        col = packed % 64
        rest = packed // 64
        odd = jnp.where(col >= half, parity, 0)
        sign = jnp.where(k < count, 1 - 2 * odd, 0).astype(jnp.float32)
        block = data_ref[rest // 2]
        value = block[0:2, :] * sign
        row_taps = steps(block[2:3, :])
        col_taps = steps(block[3:4, :])
        weighted = jnp.concatenate([col_taps * value[0:1, :], col_taps * value[1:2, :]], axis=0)
        rh, rl = two_parts(row_taps)
        wh, wl = two_parts(weighted)
        left = jnp.concatenate([rh, rh, rl], axis=1)
        right = jnp.concatenate([wh, wl, wh], axis=1)
        made = lax.dot_general(left, right, (((1,), (1,)), ((), ())), preferred_element_type=jnp.float32)
        return made, jnp.where(col >= half, col - half, col), pl.multiple_of((rest % 2) * TILE, TILE)

    def step(k, carry):
        made = [one(2 * k + u) for u in range(2)]
        for sub_grid, col, start in made:
            grid_ref[0, col, pl.ds(start, TILE), :] += sub_grid[:, :TILE]
            grid_ref[1, col, pl.ds(start, TILE), :] += sub_grid[:, TILE:]
        return carry

    lax.fori_loop(0, (count + 1) // 2, step, 0)

    depth = half // 2
    rows = grid_ref.shape[2]

    def outer(k, carry):
        spot = pl.ds(pl.multiple_of(k * 8, 8), 8)
        for side in range(2):
            x = []
            for b in range(depth):
                value = grid_ref[0, 2 * b + side, spot, :], grid_ref[1, 2 * b + side, spot, :]
                x.append(times(value, first_ref[b, 0], first_ref[b, 1]))
            for a, value in enumerate(sixteen(x)):
                c = turn_ref[a, side : side + 1, :]
                s = turn_ref[a, 2 + side : 3 + side, :]
                value = times(value, c, s)
                grid_ref[0, 2 * a + side, spot, :] = value[0]
                grid_ref[1, 2 * a + side, spot, :] = value[1]
        return carry

    lax.fori_loop(0, rows // 8, outer, 0)

    def inner(a, carry):
        mirrored = depth - parity - a
        mirrored = jnp.where(mirrored == depth, 0, mirrored)
        which = jnp.where((a == 0) & (parity == 0), 1, 0)
        weight = weight_ref[which]
        for part in range(rows // TILE):
            spot = pl.ds(part * TILE, TILE)
            x = jnp.concatenate([grid_ref[q, 2 * a + side, spot, :] for q in range(2) for side in range(2)], axis=1)
            high, low = two_parts(x)
            made = jnp.dot(jnp.concatenate([high, low, high], axis=1), weight, preferred_element_type=jnp.float32)
            mid = TILE // 2
            made = times((made[:, :TILE], made[:, TILE:]), undo_ref[a, 0:1, :], undo_ref[a, 1:2, :])
            for q in range(2):
                out_ref[a, spot, q * TILE : q * TILE + mid] = made[q][:, :mid]
                out_ref[mirrored, spot, q * TILE + mid : (q + 1) * TILE] = made[q][:, mid:]
        return carry

    lax.fori_loop(0, depth, inner, 0)


def split_table(x):
    high = x.astype(np.float32).astype(jnp.bfloat16)
    low = (x - high.astype(np.float64)).astype(np.float32).astype(jnp.bfloat16)
    return high, low


def undone(pixels):
    c, s = trig(pixels + G // 4, G)
    return 1.0 / (1.0 - (c - 1j * s))


def grid_row_weights(n, size):
    depth = n // 2
    span = G // 2 // depth
    half = size // n // 2
    alpha = np.arange(span)
    turns, firsts, undos = [], [], []
    for p in range(2):
        j = 2 * np.arange(depth) + p
        c, s = trig(j[:, None] * alpha[None, :], G)
        turns.append(np.concatenate([c.reshape(depth, 2, TILE), s.reshape(depth, 2, TILE)], axis=1))
        firsts.append(np.stack(trig(np.arange(depth) * p, n), axis=1))
        low = n * np.arange(half)[None, :] + j[:, None]
        high = size - n * np.arange(half)[None, :] - ((-j) % n)[:, None]
        if p == 0:
            low[0, 0], high[0, 0] = 0, size // 2
        undo = undone(np.concatenate([low, high], axis=1))
        undos.append(np.stack([undo.real, undo.imag], axis=1))
    weights = []
    i = np.arange(half)
    for special in range(2):
        low = n * i
        high = size - n * i - (0 if special else n)
        if special:
            high[0] = size // 2
        parts_re, parts_im = [], []
        for cols in (low, high):
            c, s = trig(alpha[:, None] * (cols[None, :] + G // 4), G)
            parts_re.append(np.concatenate([c, -s], axis=0))
            parts_im.append(np.concatenate([s, c], axis=0))
        w = np.concatenate(parts_re + parts_im, axis=1)
        high_part, low_part = split_table(w)
        weights.append(np.concatenate([high_part, high_part, low_part], axis=0))
    turns, firsts, undos = (np.stack(x).astype(np.float32) for x in (turns, firsts, undos))
    return turns, firsts, undos, np.stack(weights)


def grid_rows_two(info, table, first, data, turns, undos, weights):
    depth = turns.shape[0]
    rows = 2 * TILE
    smem = pl.BlockSpec(memory_space=pltpu.SMEM)
    vmem = pl.BlockSpec(memory_space=pltpu.VMEM)
    return pl.pallas_call(
        grid_rows_kernel,
        out_shape=jax.ShapeDtypeStruct((depth, rows, 2 * TILE), jnp.float32),
        in_specs=[smem, smem, smem, vmem, vmem, vmem, vmem],
        out_specs=vmem,
        scratch_shapes=[pltpu.VMEM((2, 2 * depth, rows, TILE), jnp.float32)],
        compiler_params=pltpu.CompilerParams(vmem_limit_bytes=40 << 20),
        cost_estimate=pl.CostEstimate(flops=2 * 10**10, bytes_accessed=16 * 2**20, transcendentals=0),
        name="grid_rows_two",
    )(info, table, first, data, turns, undos, weights)


def shared(residual, position, owner, tile_local, xi, amplitude):
    n = lax.axis_size(parts)
    n_base = lax.axis_size("base")
    n_slab = lax.axis_size("half") * lax.axis_size("quad")
    quads = lax.axis_size("quad")
    base, parity, quad = (lax.axis_index(axis) for axis in parts)
    place = 2 * (base * quads + quad) + parity
    order = np.array([2 * (b * quads + q) + h for b in range(n_base) for h in range(2) for q in range(quads)])
    rows, size = xi.shape
    depth = size // n
    half = depth // 2
    tiles = G // TILE

    blocks = residual.shape[0]
    region_rows = G // n_slab // TILE
    region_cols = G // n_base // TILE
    room = 2 * n_base * (2 * blocks // n)
    target = owner[:, 0]
    tile_row = (target % n_slab) * region_rows + tile_local // region_cols
    tile_col = (target // n_slab) * region_cols + tile_local % region_cols
    flip = tile_row >= tiles // 2
    tile_row = jnp.where(flip, tiles - 1 - tile_row, tile_row)
    tile_col = jnp.where(flip, tiles - 1 - tile_col, tile_col)
    line = tile_row // n_slab
    code = (tile_row % n_slab) * tiles + tile_col
    flipped = flip[:, None]
    payload = jnp.stack(
        [
            residual[:, 0],
            jnp.where(flipped, -residual[:, 1], residual[:, 1]),
            jnp.where(flipped, TILE - position[:, 0], position[:, 0]),
            jnp.where(flipped, TILE - position[:, 1], position[:, 1]),
        ],
        axis=1,
    )
    earlier = (line[:, None] == line[None, :]) & (np.arange(blocks)[:, None] > np.arange(blocks)[None, :])
    slot = line * room + jnp.sum(earlier.astype(jnp.int32), axis=1)
    chosen = slot[None, :] == lax.broadcasted_iota(jnp.int32, (n_base * room, blocks), 0)
    moved = jnp.dot(chosen.astype(jnp.float32), payload.reshape(blocks, 4 * TILE), precision=fine)
    codes = jnp.sum(jnp.where(chosen, code[None, :] + 1, 0), axis=1) - 1
    codes = jnp.pad(codes.astype(jnp.float32).reshape(n_base, 1, 1, room), ((0, 0), (0, 0), (0, 3), (0, TILE - room)))
    sent = jnp.concatenate([moved.reshape(n_base, room, 4, TILE), codes], axis=1)
    got = exchange(sent, n_slab)

    outer, inner = row_tables(n, size)
    outer, inner = outer[:, :, order], inner[order]
    spectrum = (amplitude * xi).reshape(rows, n, depth)
    mid = einsum("rba,bqc->qcra", spectrum, outer)
    sent = einsum("cra,cae->cre", mid[0], inner[:, 0]) + einsum("cra,cae->cre", mid[1], inner[:, 1])
    sent, got = lax.optimization_barrier((sent, got))
    field = lax.all_to_all(sent, parts, split_axis=0, concat_axis=0, tiled=True)
    field = field.reshape(size, depth)

    sources = n_slab * n_base
    codes = got[:, :, room, 0, :room].reshape(sources, room).astype(jnp.int32)
    mine = (codes >= 0) & (codes // tiles // 2 == quad)
    ones = mine.astype(jnp.float32)
    before = jnp.dot(ones, np.triu(np.ones((room, room), np.float32), 1), precision=fine)
    above = jnp.dot(np.tril(np.ones((sources, sources), np.float32), -1), ones, precision=fine)
    rank = (before + jnp.sum(above, axis=1, keepdims=True)).astype(jnp.int32)
    rank = jnp.where(mine, rank, -1).reshape(-1)
    index = lax.broadcasted_iota(jnp.int32, (sources, room), 0) * (room + 1) + lax.broadcasted_iota(jnp.int32, (sources, room), 1)
    packed = (index * (2 * tiles) + codes % (2 * tiles)).reshape(-1)
    spots = lax.broadcasted_iota(jnp.int32, (sources * room, sources * room), 0)
    table = jnp.sum(jnp.where(spots == rank[None, :], packed[None, :], 0), axis=1)
    table = jnp.pad(table, (0, 2))
    info = jnp.stack([jnp.sum(mine.astype(jnp.int32)), parity]).astype(jnp.int32)

    turns, firsts, undos, weights = grid_row_weights(n, size)
    halves = grid_rows_two(
        info,
        table,
        lax.dynamic_index_in_dim(jnp.asarray(firsts), parity, 0, keepdims=False),
        got.reshape(sources * (room + 1), 4, TILE),
        lax.dynamic_index_in_dim(jnp.asarray(turns), parity, 0, keepdims=False),
        lax.dynamic_index_in_dim(jnp.asarray(undos), parity, 0, keepdims=False),
        jnp.asarray(weights),
    )
    whole = lax.all_to_all(halves, ("base", "quad"), split_axis=0, concat_axis=0, tiled=True)

    lane = lax.broadcasted_iota(jnp.int32, (1, depth), 1)
    still = (place == 0) & (lane % half == 0)

    def mirror(x):
        return jnp.where(still, x, jnp.roll(x, half, axis=-1))

    c_len = 128
    d_len = size // c_len
    bc, bs = (x.astype(np.float32) for x in trig(np.arange(c_len)[:, None] * np.arange(c_len)[None, :], c_len))
    shape = (c_len, d_len, depth)
    n0 = c_len * np.arange(d_len)[None, :] + np.arange(c_len)[:, None]
    ic, isn = (x.astype(np.float32) for x in trig(n0[:, :, None] * np.arange(d_len)[None, None, :], size))
    pair = jnp.stack([field.reshape(shape), mirror(field).reshape(shape)])
    first = np.stack([np.stack([bc, bs], 1), np.stack([bs, -bc], 1)], 0)
    turned = einsum("qbal,qbsc->csal", pair, first)
    second = np.stack([ic, -isn], axis=2)
    power = einsum("csal,cdsa->cdl", turned, second)
    sky = jnp.exp(power / size)

    wide = G // c_len
    deep = size // wide
    gc, gs = (x.astype(np.float32) for x in trig(np.arange(deep)[:, None] * np.arange(c_len)[None, :], c_len))
    first_g = np.stack([np.stack([gc, gs], 1), np.stack([-gs, gc], 1)], 0)
    whole = whole.reshape(deep, wide, 2, depth)
    turned_g = einsum("baql,qbsc->csal", whole, first_g)
    ac, asn = trig((n0 + G // 4)[:, :, None] * np.arange(wide)[None, None, :], G)
    wave = (ac + 1j * asn) * undone(n0)[:, :, None] / G
    second_g = np.stack([wave.real, -wave.imag], axis=2).astype(np.float32)
    back = einsum("csal,cdsa->cdl", turned_g, second_g)

    z = sky * back
    pz = einsum("cdl,cda->cal", z, ic)
    qz = einsum("cdl,cda->cal", z, isn)
    joined = jnp.stack([pz + mirror(qz), mirror(pz) - qz])
    fold = einsum("qcal,qcb->bal", joined, np.stack([bc, bs]))
    folded = lax.all_to_all(
        fold.reshape(n, rows, depth), parts, split_axis=0, concat_axis=0, tiled=True
    )
    ends = einsum("jre,jqae->qjra", folded, inner)
    final = einsum("qjra,bqj->rba", ends, outer)
    return amplitude * final.reshape(rows, size) / size


def solution(mesh):
    n_base, n_slab = mesh.shape["base"], mesh.shape["slab"]
    body, axes = general, both
    if n_slab == 2 * n_base and 2 * n_base * n_slab == G // TILE:
        body, axes = shared, parts
        mesh = jax.sharding.Mesh(mesh.devices.reshape(n_base, 2, n_slab // 2), parts)
    placed = (
        P(axes, None, None),
        P(axes, None, None),
        P(axes, None),
        P(axes),
        P(axes, None),
        P(axes, None),
    )
    return jax.shard_map(body, mesh=mesh, in_specs=placed, out_specs=P(axes, None), check_vma=False)
```

profile of v0, /device:TPU:0, one launch (start us, length us, event | category | flops | bytes accessed | tf_op | source)
XLA Modules:
  0.0 318.5 jit_solution(12524910019032009537)
XLA Ops:
  0.0 2.5 multiply_bitcast_fusion
  2.5 0.4 copy.87
  2.9 0.4 copy-done.17
  3.2 1.8 fusion.59
  5.1 1.8 slice_bitcast_fusion.1
  7.4 0.4 fusion.58
  7.8 0.3 pad_maximum_fusion.1
  8.2 0.4 fusion.32
  8.6 0.3 copy.58
  9.1 43.9 %exchange.1 = f32[8,4,65,4,128]{4,3,2,1,0:T(4,128)S(1)} custom-call(f32[4,65,4,128]{3,2,1,0:T(4,128)S(1)} %select_maximum_fusion.send_ref), custom_call_target="tpu_custom_call" | custom-call | tf_op jit(solution)/shard_map/exchange/pallas_call | solution.py:369
  53.1 2.0 copy-done
  55.0 2.5 fusion.20
  57.5 3.7 %fusion.24 = f32[32,128,128]{2,1,0:T(8,128)} fusion(f32[32,128,128]{2,1,0:T(8,128)S(1)} %fusion.20, f32[32,128,128]{2,1,0:T(8,128)S(1)} %copy-done.10, f32[32,128,128]{2,0,1:T(8,128)S(1)} %copy-done.5), kind=kOutput, calls=%fused_computation.36 | convolution fusion | flops 403177472 | bytes 8388608 | tf_op jit(solution)/shard_map/cra,cae->cre/dot_general | solution.py:129
  61.3 4.5 %all-to-all-start = ((f32[32,128,128]{2,1,0:T(8,128)}), f32[32,128,128]{2,1,0:T(8,128)}, u32[]{:S(2)}, u32[]{:S(2)}) async-start(f32[32,128,128]{2,1,0:T(8,128)} %fusion.24), calls=%async_computation | async-start | bytes 4194304 | tf_op jit(solution)/shard_map/all_to_all | solution.py:621
  65.9 1.8 fusion.53
  67.8 0.9 slice_convert_fusion
  69.2 1.7 select_reduce_fusion
  71.0 0.7 pad_add_fusion.info_ref
  71.8 2.2 copy-done.1
  74.0 50.1 %grid_rows_two.1 = f32[16,256,256]{2,1,0:T(8,128)S(1)} custom-call(s32[2]{0:T(128)S(1)} %pad_add_fusion.info_ref, s32[2050]{0:T(1024)S(1)} %pad.9.list_ref, f32[16,2]{1,0:T(8,128)S(1)} %copy.64.first_ref, f32[2080,4,128]{2,1,0:T(4,128)S(1)} %bitcast.137, f32[16,4,128]{2,1,0:T(4,128)S(1)} %dynamic-slice_bitcast_fusion.turn_ref, ...), custom_call_target="tpu_custom_call" | custom-call | flops 20000000000 | bytes 16777216 | tf_op jit(solution)/shard_map/grid_rows_two/pallas_call | solution.py:559
  124.2 2.0 copy-done.2
  126.1 28.0 %all-to-all-start.1 = ((f32[16,256,256]{2,1,0:T(8,128)}), f32[16,256,256]{2,1,0:T(8,128)}, u32[]{:S(2)}, u32[]{:S(2)}) async-start(f32[16,256,256]{2,1,0:T(8,128)} %copy-done.2), calls=%async_computation.1 | async-start | bytes 8388608 | tf_op jit(solution)/shard_map/all_to_all | solution.py:649
  154.2 2.0 copy.62
  156.2 4.9 %fusion.57 = (f32[4096,64]{1,0:T(8,128)}, f32[4096,64]{1,0:T(8,128)}) fusion(f32[4096,128]{1,0:T(8,128)} %bitcast.13), kind=kLoop, calls=%fused_computation.129 | loop fusion | bytes 4194304 | tf_op jit(solution)/shard_map/jit(_roll_static)/slice | solution.py:655
  161.1 2.7 copy.60
  163.8 3.7 %copy.59 = f32[1,128,32,64]{1,3,0,2:T(8,128)} copy(f32[1,128,32,64]{3,2,1,0:T(8,128)} %bitcast.142) | data formatting | bytes 2097152 | tf_op jit(solution)/shard_map/jit(_roll_static)/concatenate | solution.py:655
  167.5 1.6 maximum_select_fusion
  169.1 3.4 %fusion.12 = f32[128,2,32,128]{0,3,1,2:T(8,128)} fusion(f32[2,128,2,128,1]{3,1,0,2,4:T(8,128)S(1)} %copy-done.11, f32[1,128,32,128]{1,3,0,2:T(8,128)S(1)} %maximum_select_fusion, f32[1,128,32,128]{1,3,0,2:T(8,128)S(1)} %copy.62), kind=kOutput, calls=%fused_computation.14 | convolution fusion | flops 1611661312 | bytes 8650752 | tf_op jit(solution)/shard_map/qbal,qbsc->csal/dot_general | solution.py:129
  172.6 5.5 %copy.63 = f32[128,2,32,128]{3,2,1,0:T(8,128)} copy(f32[128,2,32,128]{0,3,1,2:T(8,128)} %fusion.12) | data formatting | bytes 8388608 | tf_op jit(solution)/shard_map/qbal,qbsc->csal/transpose | solution.py:129
  178.1 5.5 %fusion.60 = f32[128,128,32,1]{1,2,3,0:T(8,128)S(1)} fusion(f32[128,2,32,128]{3,2,1,0:T(8,128)} %copy.63, f32[128,32,2,32]{3,1,2,0:T(8,128)} %constant.212.clone), kind=kOutput, calls=%fused_computation.132 | convolution fusion | flops 201326592 | bytes 7340032 | tf_op jit(solution)/shard_map/csal,cdsa->cdl/dot_general | solution.py:129
  183.6 22.9 %all-to-all-done.1 = f32[16,256,256]{2,1,0:T(8,128)} async-done(((f32[16,256,256]{2,1,0:T(8,128)}), f32[16,256,256]{2,1,0:T(8,128)}, u32[]{:S(2)}, u32[]{:S(2)}) %all-to-all-start.1) | async-done | bytes 4194336 | tf_op jit(solution)/shard_map/all_to_all | solution.py:649
  206.5 5.9 %reshape.181 = f32[64,64,2,128]{3,2,1,0:T(2,128)} reshape(f32[16,256,256]{2,1,0:T(8,128)} %all-to-all-done.1) | data formatting | bytes 8388608 | tf_op jit(solution)/shard_map/reshape | solution.py:674
  212.4 11.4 %fusion.9 = f32[128,2,64,128]{0,3,1,2:T(8,128)} fusion(f32[2,64,2,128,1]{3,1,0,2,4:T(8,128)S(1)} %copy-done.12, f32[64,64,2,128,1]{3,2,1,0,4:T(2,128)} %bitcast.138), kind=kOutput, calls=%fused_computation.13 | convolution fusion | flops 1610612736 | bytes 12713984 | tf_op jit(solution)/shard_map/baql,qbsc->csal/dot_general | solution.py:129
  223.8 8.9 %copy.66 = f32[128,2,64,128]{3,2,1,0:T(8,128)} copy(f32[128,2,64,128]{0,3,1,2:T(8,128)} %fusion.9) | data formatting | bytes 16777216 | tf_op jit(solution)/shard_map/baql,qbsc->csal/transpose | solution.py:129
  232.8 8.3 %bitcast_multiply_fusion.1 = f32[128,128,32]{1,2,0:T(8,128)S(1)} fusion(f32[128,128,32,1]{1,2,3,0:T(8,128)S(1)} %fusion.60, f32[128,2,64,128]{3,2,1,0:T(8,128)} %copy.66, f32[128,32,2,64]{3,1,2,0:T(8,128)} %constant.214.clone), kind=kOutput, calls=%fused_computation.28 | convolution fusion | flops 403701760 | bytes 14680064 | tf_op jit(solution)/shard_map/csal,cdsa->cdl/dot_general | solution.py:129
  241.1 1.2 fusion.61
  242.3 0.4 copy-done.7
  242.7 1.3 fusion.62
  244.0 1.5 fusion.55
  245.4 1.5 fusion.15
  247.0 0.4 pad_maximum_fusion
  247.4 0.4 copy-done.15
  247.9 3.7 %fusion.27 = f32[128,32,128]{2,0,1:T(8,128)S(1)} fusion(f32[2,128,128,1]{1,2,0,3:T(8,128)S(1)} %copy-done.15, f32[2,128,32,128]{3,2,1,0:T(8,128)S(1)} %pad_maximum_fusion), kind=kOutput, calls=%fused_computation.37 | convolution fusion | flops 805306368 | bytes 6422528 | tf_op jit(solution)/shard_map/qcal,qcb->bal/dot_general | solution.py:129
  251.6 1.2 copy.68
  252.9 56.3 %all_to_all.15 = f32[32,128,128]{2,1,0:T(8,128)S(1)} all-to-all(f32[32,128,128]{2,1,0:T(8,128)S(1)} %bitcast.141), channel_id=1, replica_groups=mesh['base'=4,'half'=2,'quad'=4] {'base','half','quad'}, dimensions={0} | all-to-all | bytes 4194304 | tf_op jit(solution)/shard_map/all_to_all | solution.py:686
  309.1 2.1 convolution_bitcast_fusion
  311.3 3.6 %fusion.5 = f32[128,128,32,1]{1,2,3,0:T(8,128)S(1)} fusion(f32[32,2,32,1]{0,2,1,3:T(8,128)S(1)} %copy-done.16, f32[2,32,128,128]{3,2,0,1:T(8,128)S(1)} %convolution_bitcast_fusion), kind=kOutput, calls=%fused_computation.9 | convolution fusion | flops 201326592 | bytes 6299648 | tf_op jit(solution)/shard_map/qjra,bqj->rba/dot_general | solution.py:129
  314.9 3.2 fusion.13
  (72 shorter events, 1.6 us)
Async XLA Ops:
  2.5 0.8 copy-start.17
  5.1 1.8 copy-start.22
  5.1 1.8 copy-start.23
  5.1 1.9 copy-start.20
  5.1 2.2 copy-start.13
  5.1 2.2 copy-start.14
  9.1 45.9 %copy-start.9 = (f32[32,128,128]{2,1,0:T(8,128)S(1)}, f32[32,128,128]{2,1,0:T(8,128)}, u32[]{:S(2)}) copy-start(f32[32,128,128]{2,1,0:T(8,128)} %constant.204.clone) | copy-start | bytes 6291460
  53.1 2.0 copy-start
  55.0 2.5 copy-start.5
  55.0 2.5 copy-start.10
  61.3 7.4 %copy-start.19 = (f32[32,32]{1,0:T(8,128)S(1)}, f32[32,32]{1,0:T(8,128)}, u32[]{:S(2)}) copy-start(f32[32,32]{1,0:T(8,128)} %constant.206.clone) | copy-start | bytes 12292
  61.3 7.6 %copy-start.25 = (f32[64,64]{1,0:T(8,128)S(1)}, f32[64,64]{1,0:T(8,128)}, u32[]{:S(2)}) copy-start(f32[64,64]{1,0:T(8,128)} %constant.205.clone) | copy-start | bytes 49156
  61.3 9.6 %copy-start.24 = (f32[2,16,2]{1,2,0:T(2,128)S(1)}, f32[2,16,2]{1,2,0:T(2,128)}, u32[]{:S(2)}) copy-start(f32[2,16,2]{1,2,0:T(2,128)} %constant.207.clone) | copy-start | bytes 772
  61.3 10.5 %copy-start.21 = (f32[2,16,2,128]{3,2,1,0:T(2,128)S(1)}, f32[2,16,2,128]{3,2,1,0:T(2,128)}, u32[]{:S(2)}) copy-start(f32[2,16,2,128]{3,2,1,0:T(2,128)} %constant.209.clone) | copy-start | bytes 98308
  61.3 10.5 %copy-start.18 = (f32[2,16,4,128]{3,2,1,0:T(4,128)S(1)}, f32[2,16,4,128]{3,2,1,0:T(4,128)}, u32[]{:S(2)}) copy-start(f32[2,16,4,128]{3,2,1,0:T(4,128)} %constant.208.clone) | copy-start | bytes 196612
  61.3 10.5 %copy-start.3 = (bf16[2,1536,256]{2,1,0:T(8,128)(2,1)S(1)}, bf16[2,1536,256]{2,1,0:T(8,128)(2,1)}, u32[]{:S(2)}) copy-start(bf16[2,1536,256]{2,1,0:T(8,128)(2,1)} %constant.210.clone.weight_ref) | copy-start | bytes 4718596
  61.3 64.8 %all-to-all-start = ((f32[32,128,128]{2,1,0:T(8,128)}), f32[32,128,128]{2,1,0:T(8,128)}, u32[]{:S(2)}, u32[]{:S(2)}) async-start(f32[32,128,128]{2,1,0:T(8,128)} %fusion.24), calls=%async_computation | async-start | bytes 4194304 | tf_op jit(solution)/shard_map/all_to_all | solution.py:621
  71.8 2.2 copy-start.1
  124.2 2.0 copy-start.2
  126.1 80.3 %all-to-all-start.1 = ((f32[16,256,256]{2,1,0:T(8,128)}), f32[16,256,256]{2,1,0:T(8,128)}, u32[]{:S(2)}, u32[]{:S(2)}) async-start(f32[16,256,256]{2,1,0:T(8,128)} %copy-done.2), calls=%async_computation.1 | async-start | bytes 8388608 | tf_op jit(solution)/shard_map/all_to_all | solution.py:649
  167.5 1.6 copy-start.11
  183.6 28.8 %copy-start.12 = (f32[2,64,2,128,1]{3,1,0,2,4:T(8,128)S(1)}, f32[2,64,2,128,1]{3,1,0,2,4:T(8,128)}, u32[]{:S(2)}) copy-start(f32[2,64,2,128,1]{3,1,0,2,4:T(8,128)} %constant.226) | copy-start | bytes 393220
  232.8 8.3 %copy-start.8 = (f32[128,32,32]{1,2,0:T(8,128)S(1)}, f32[128,32,32]{1,2,0:T(8,128)}, u32[]{:S(2)}) copy-start(f32[128,32,32]{1,2,0:T(8,128)} %constant.215.clone) | copy-start | bytes 1572868
  241.1 1.6 copy-start.7
  247.0 0.9 copy-start.15
  252.9 56.3 %copy-start.6 = (f32[32,2,128,128]{3,2,1,0:T(8,128)S(1)}, f32[32,2,128,128]{3,2,1,0:T(8,128)}, u32[]{:S(2)}) copy-start(f32[32,2,128,128]{3,2,1,0:T(8,128)} %constant.218.clone) | copy-start | bytes 12582916
  309.1 2.1 copy-start.16
  311.3 3.6 %copy-start.4 = (f32[128,4096]{1,0:T(8,128)S(1)}, f32[128,4096]{1,0:T(8,128)}, u32[]{:S(2)}) copy-start(f32[128,4096]{1,0:T(8,128)} %param.30) | copy-start | bytes 6291460
where the time goes:
time: 322 us; the launch traced here: 319 us
  Pallas kernels  94.1 us (29%)
  blocking collectives  56.3 us (17%)
  matrix products  49.5 us (15%)
  local copies, waits for them, and re-layouts  46.9 us (15%)
  starting transfers between devices  32.5 us (10%)
  waiting for transfers between devices  22.9 us (7%)
  other arithmetic  15.6 us (5%)
    all_to_all x1, blocking collectives, shared(): lax.all_to_all(fold.reshape(n, rows, depth), parts, split_axis=0, concat_...  56.3 us
    pallas_call x1, Pallas kernels, grid_rows_two(): pl.pallas_call(grid_rows_kernel, out_shape=jax.ShapeDtypeStruct((depth, r...  50.1 us
    dot_general x12, matrix products, einsum(): jnp.einsum(form, *args, precision=precision, preferred_element_type=jnp.f...  48.7 us
    pallas_call x1, Pallas kernels, exchange(): pl.pallas_call(functools.partial(exchange_kernel, nb, ns), out_shape=jax....  43.9 us
    all_to_all x1, starting transfers between devices, shared(): lax.all_to_all(halves, ('base', 'quad'), split_axis=0, concat_axis=0, til...  28 us
    all_to_all x1, waiting for transfers between devices, shared(): lax.all_to_all(halves, ('base', 'quad'), split_axis=0, concat_axis=0, til...  22.9 us
    transpose x2, local copies, waits for them, and re-layouts, einsum(): jnp.einsum(form, *args, precision=precision, preferred_element_type=jnp.f...  14.4 us
    unnamed x53, local copies, waits for them, and re-layouts  7.8 us
  transfers between devices with their start and end apart: 2, of which 1 were waited for; matrix products, arithmetic and copies ran while one was open for 11% of the time, Pallas kernels for 16%

commit v1 on v0

--- a/solution.py
+++ b/solution.py
@@ -234,6 +234,7 @@
 
 MESH = pl.DeviceIdType.MESH
 parts = ("base", "half", "quad")
+LANES = 4
 
 
 def exchange_kernel(nb, ns, send_ref, out_ref, bsend, brecv, usend, dsend, lrecv, hrecv, psend, precv, lsem):
@@ -421,48 +422,81 @@
     return out
 
 
-def grid_rows_kernel(info_ref, list_ref, first_ref, data_ref, turn_ref, undo_ref, weight_ref, out_ref, grid_ref):
+def grid_rows_kernel(info_ref, list_ref, first_ref, data_ref, turn_ref, undo_ref, weight_ref, out_ref, grid_ref, left_ref, right_ref):
     count = info_ref[0]
     parity = info_ref[1]
     grid_ref[...] = jnp.zeros_like(grid_ref)
-    cells = lax.broadcasted_iota(jnp.int32, (TILE, TILE), 0).astype(jnp.float32) * 0.25
     half = grid_ref.shape[1]
+    group = 16
+    cells = lax.broadcasted_iota(jnp.int32, (group + 8, TILE), 0).astype(jnp.float32) * 0.25
+    nothing = jnp.zeros((group, TILE), jnp.bfloat16)
 
     def bump(offsets):
         d = cells - offsets
         kept = jnp.maximum(1.0 - d * d, 0.0)
         return kept * kept * kept
 
-    def steps(offsets):
-        offsets = offsets * 0.25
-        return bump(offsets) - bump(offsets - 0.25)
-
-    def one(k):
+    def window(offsets):
+        start = jnp.floor((offsets - 4.0) * (1.0 / group))
+        offsets = (offsets - start * group) * 0.25
+        return bump(offsets) - bump(offsets - 0.25), jnp.broadcast_to(start, (group, TILE)).astype(jnp.bfloat16)
+
+    def spread(compact, start):
+        padded = jnp.concatenate([compact, jnp.zeros((8, TILE), jnp.float32)], axis=0)
+        out = []
+        for part in two_parts(padded):
+            first, second = part[:group], part[group:]
+            pieces = []
+            for g in range(TILE // group):
+                piece = jnp.where(start == g - 1, second, nothing) if g else nothing
+                pieces.append(jnp.where(start == g, first, piece))
+            out.append(jnp.concatenate(pieces, axis=0))
+        return out
+
+    lanes = left_ref.shape[0]
+
+    def place(k):
         packed = list_ref[k]
-        col = packed % 64
-        rest = packed // 64
+        return packed % 64, packed // 64
+
+    def prepare(k, lane):
+        col, rest = place(k)
         odd = jnp.where(col >= half, parity, 0)
         sign = jnp.where(k < count, 1 - 2 * odd, 0).astype(jnp.float32)
         block = data_ref[rest // 2]
         value = block[0:2, :] * sign
-        row_taps = steps(block[2:3, :])
-        col_taps = steps(block[3:4, :])
-        weighted = jnp.concatenate([col_taps * value[0:1, :], col_taps * value[1:2, :]], axis=0)
-        rh, rl = two_parts(row_taps)
-        wh, wl = two_parts(weighted)
+        row_taps, row_start = window(block[2:3, :])
+        col_taps, col_start = window(block[3:4, :])
+        rows_split = spread(row_taps, row_start)
+        real = spread(col_taps * value[0:1, :], col_start)
+        imag = spread(col_taps * value[1:2, :], col_start)
+        for q in range(2):
+            left_ref[lane, :, q * TILE : (q + 1) * TILE] = rows_split[q]
+            right_ref[lane, :TILE, q * TILE : (q + 1) * TILE] = real[q]
+            right_ref[lane, TILE:, q * TILE : (q + 1) * TILE] = imag[q]
+
+    def product(lane):
+        rh, rl = left_ref[lane, :, :TILE], left_ref[lane, :, TILE:]
+        wh, wl = right_ref[lane, :, :TILE], right_ref[lane, :, TILE:]
         left = jnp.concatenate([rh, rh, rl], axis=1)
         right = jnp.concatenate([wh, wl, wh], axis=1)
-        made = lax.dot_general(left, right, (((1,), (1,)), ((), ())), preferred_element_type=jnp.float32)
-        return made, jnp.where(col >= half, col - half, col), pl.multiple_of((rest % 2) * TILE, TILE)
+        return lax.dot_general(left, right, (((1,), (1,)), ((), ())), preferred_element_type=jnp.float32)
 
     def step(k, carry):
-        made = [one(2 * k + u) for u in range(2)]
-        for sub_grid, col, start in made:
-            grid_ref[0, col, pl.ds(start, TILE), :] += sub_grid[:, :TILE]
-            grid_ref[1, col, pl.ds(start, TILE), :] += sub_grid[:, TILE:]
+        made = [product(lane) for lane in range(lanes)]
+        for lane in range(lanes):
+            prepare((k + 1) * lanes + lane, lane)
+        for lane in range(lanes):
+            col, rest = place(k * lanes + lane)
+            col = jnp.where(col >= half, col - half, col)
+            spot = pl.ds(pl.multiple_of((rest % 2) * TILE, TILE), TILE)
+            grid_ref[0, col, spot, :] += made[lane][:, :TILE]
+            grid_ref[1, col, spot, :] += made[lane][:, TILE:]
         return carry
 
-    lax.fori_loop(0, (count + 1) // 2, step, 0)
+    for lane in range(lanes):
+        prepare(lane, lane)
+    lax.fori_loop(0, (count + lanes - 1) // lanes, step, 0)
 
     depth = half // 2
     rows = grid_ref.shape[2]
@@ -489,8 +523,8 @@
         mirrored = jnp.where(mirrored == depth, 0, mirrored)
         which = jnp.where((a == 0) & (parity == 0), 1, 0)
         weight = weight_ref[which]
-        for part in range(rows // TILE):
-            spot = pl.ds(part * TILE, TILE)
+        for part in range(1):
+            spot = pl.ds(0, rows)
             x = jnp.concatenate([grid_ref[q, 2 * a + side, spot, :] for q in range(2) for side in range(2)], axis=1)
             high, low = two_parts(x)
             made = jnp.dot(jnp.concatenate([high, low, high], axis=1), weight, preferred_element_type=jnp.float32)
@@ -561,11 +595,175 @@
         out_shape=jax.ShapeDtypeStruct((depth, rows, 2 * TILE), jnp.float32),
         in_specs=[smem, smem, smem, vmem, vmem, vmem, vmem],
         out_specs=vmem,
-        scratch_shapes=[pltpu.VMEM((2, 2 * depth, rows, TILE), jnp.float32)],
+        scratch_shapes=[
+            pltpu.VMEM((2, 2 * depth, rows, TILE), jnp.float32),
+            pltpu.VMEM((LANES, TILE, 2 * TILE), jnp.bfloat16),
+            pltpu.VMEM((LANES, 2 * TILE, 2 * TILE), jnp.bfloat16),
+        ],
         compiler_params=pltpu.CompilerParams(vmem_limit_bytes=40 << 20),
         cost_estimate=pl.CostEstimate(flops=2 * 10**10, bytes_accessed=16 * 2**20, transcendentals=0),
         name="grid_rows_two",
     )(info, table, first, data, turns, undos, weights)
+
+
+def minus(x):
+    return [(b, a) for a, b in sixteen([(b, a) for a, b in x])]
+
+
+def pick(table, u):
+    side = table.shape[1] // 2
+    return table[:, u : u + 1], table[:, side + u : side + u + 1]
+
+
+def mirrored(x, still):
+    return jnp.where(still, x, pltpu.roll(x, x.shape[1] // 2, 1))
+
+
+def still_lanes(place, rows):
+    lane = lax.broadcasted_iota(jnp.int32, (rows, TILE), 1)
+    return (lane % (TILE // 2) == 0) & (place == 0)
+
+
+def stacked(work_ref, u):
+    sides = [jnp.concatenate([work_ref[u + q, 0], work_ref[u + q, 1]], axis=0) for q in range(2)]
+    high, low = two_parts(jnp.concatenate(sides, axis=1))
+    return jnp.concatenate([high, high, low], axis=0)
+
+
+def field_kernel(scale, info_ref, field_ref, turn_ref, mat_ref, sky_ref, work_ref):
+    still = still_lanes(info_ref[0], 8)
+    n = field_ref.shape[0]
+
+    def outer(k, carry):
+        spot = pl.ds(pl.multiple_of(k * 8, 8), 8)
+        table = turn_ref[spot, :]
+        for e in range(2):
+            x = []
+            for d in range(n // 2):
+                first, second = field_ref[d, spot, :], field_ref[d + n // 2, spot, :]
+                value = first - second if e else first + second
+                value = value, mirrored(value, still)
+                x.append(turn(value, -2 * math.pi * d / n) if e * d else value)
+            for v, value in enumerate(minus(x)):
+                u = 2 * v + e
+                work_ref[u, 0, spot, :], work_ref[u, 1, spot, :] = times(value, *pick(table, u))
+        return carry
+
+    lax.fori_loop(0, field_ref.shape[1] // 8, outer, 0)
+
+    def inner(k, carry):
+        made = jnp.dot(mat_ref[...], stacked(work_ref, 2 * k), preferred_element_type=jnp.float32)
+        made = jnp.exp(made * scale)
+        sky_ref[2 * k] = made[:, :TILE]
+        sky_ref[2 * k + 1] = made[:, TILE:]
+        return carry
+
+    lax.fori_loop(0, n // 2, inner, 0)
+
+
+def image_kernel(info_ref, bend_ref, whole_ref, sky_ref, turn_g_ref, mat_g_ref, slope_ref, mat_f_ref, turn_ref, out_ref, work_ref, half_ref):
+    still = still_lanes(info_ref[0], 8)
+    n = sky_ref.shape[0]
+    depth = n // 2
+
+    def outer(k, carry):
+        spot = pl.ds(pl.multiple_of(k * 8, 8), 8)
+        table = turn_g_ref[spot, :]
+        for e in range(2):
+            x = []
+            for a in range(depth):
+                value = whole_ref[a, spot, :TILE], whole_ref[a, spot, TILE:]
+                x.append(turn(value, 2 * math.pi * a / n) if e * a else value)
+            for v, value in enumerate(sixteen(x)):
+                u = 2 * v + e
+                work_ref[u, 0, spot, :], work_ref[u, 1, spot, :] = times(value, *pick(table, u))
+        return carry
+
+    lax.fori_loop(0, whole_ref.shape[1] // 8, outer, 0)
+
+    def inner(k, carry):
+        made = jnp.dot(mat_g_ref[...], stacked(work_ref, 2 * k), preferred_element_type=jnp.float32)
+        z = []
+        for q in range(2):
+            u = 2 * k + q
+            sine = slope_ref[0] * bend_ref[u, 0] + slope_ref[1] * bend_ref[u, 1]
+            z.append(made[:, q * TILE : (q + 1) * TILE] * sky_ref[u] / sine)
+        high, low = two_parts(jnp.concatenate(z, axis=1))
+        spread = jnp.dot(mat_f_ref[...], jnp.concatenate([high, high, low], axis=0), preferred_element_type=jnp.float32)
+        for q in range(2):
+            for c in range(2):
+                work_ref[2 * k + q, c, :TILE, :] = spread[c * TILE : (c + 1) * TILE, q * TILE : (q + 1) * TILE]
+        return carry
+
+    lax.fori_loop(0, depth, inner, 0)
+
+    def last(k, carry):
+        spot = pl.ds(pl.multiple_of(k * 8, 8), 8)
+        table = turn_ref[spot, :]
+        for e in range(2):
+            x = []
+            for v in range(depth):
+                u = 2 * v + e
+                x.append(times((work_ref[u, 0, spot, :], work_ref[u, 1, spot, :]), *pick(table, u)))
+            for d, value in enumerate(minus(x)):
+                if e == 0:
+                    half_ref[d, 0], half_ref[d, 1] = value
+                    continue
+                value = turn(value, -2 * math.pi * d / n) if d else value
+                before = half_ref[d, 0], half_ref[d, 1]
+                for side, both_parts in enumerate((add(before, value), sub(before, value))):
+                    out_ref[d + side * depth, spot, :] = both_parts[0] - mirrored(both_parts[1], still)
+        return carry
+
+    lax.fori_loop(0, TILE // 8, last, 0)
+
+
+def column_tables(n, size):
+    w = np.arange(size // n)
+    t = np.arange(TILE)
+    u = np.arange(n)
+    r = 2 * np.arange(2 * TILE) + 1
+    side = TILE // 2
+
+    def lanes(c, s):
+        out = np.zeros((c.shape[0], TILE))
+        out[:, :n], out[:, side : side + n] = c, s
+        return out.astype(np.float32)
+
+    def matrix(x, axis_first):
+        high, low = split_table(x)
+        return np.concatenate([high, low, high], axis=1)
+
+    c, s = trig(t[:, None] * u[None, :], size)
+    turns = lanes(c, -s)
+    c, s = trig(w[:, None] * t[None, :], size // n)
+    mat_h = matrix(np.concatenate([c, s], axis=1), 0)
+    mat_f = matrix(np.concatenate([c.T, -s.T], axis=0), 0)
+    c, s = trig(r[:, None] * u[None, :], 2 * G)
+    turns_g = lanes(c, s)
+    c, s = trig((w[:, None] * n + G // 4) * r[None, :], 2 * G)
+    mat_g = matrix(np.concatenate([s, c], axis=1), 0)
+    c, s = trig(w * n + G // 4, 2 * G)
+    slope = np.stack([s, c]) * (2.0 * G)
+    slope = np.broadcast_to(slope[:, :, None], slope.shape + (TILE,)).astype(np.float32)
+    c, s = trig(u, 2 * G)
+    bend = np.stack([c, s], axis=1).astype(np.float32)
+    return turns, mat_h, mat_f, turns_g, mat_g, slope, bend
+
+
+def column_call(kernel, smems, args, out_shape, scratch, name):
+    smem = pl.BlockSpec(memory_space=pltpu.SMEM)
+    vmem = pl.BlockSpec(memory_space=pltpu.VMEM)
+    return pl.pallas_call(
+        kernel,
+        out_shape=jax.ShapeDtypeStruct(out_shape, jnp.float32),
+        in_specs=[smem] * len(smems) + [vmem] * len(args),
+        out_specs=vmem,
+        scratch_shapes=scratch,
+        compiler_params=pltpu.CompilerParams(vmem_limit_bytes=40 << 20),
+        cost_estimate=pl.CostEstimate(flops=10**10, bytes_accessed=16 * 2**20, transcendentals=0),
+        name=name,
+    )(*smems, *args)
 
 
 def shared(residual, position, owner, tile_local, xi, amplitude):
@@ -633,7 +831,7 @@
     packed = (index * (2 * tiles) + codes % (2 * tiles)).reshape(-1)
     spots = lax.broadcasted_iota(jnp.int32, (sources * room, sources * room), 0)
     table = jnp.sum(jnp.where(spots == rank[None, :], packed[None, :], 0), axis=1)
-    table = jnp.pad(table, (0, 2))
+    table = jnp.pad(table, (0, 2 * LANES))
     info = jnp.stack([jnp.sum(mine.astype(jnp.int32)), parity]).astype(jnp.int32)
 
     turns, firsts, undos, weights = grid_row_weights(n, size)
@@ -648,44 +846,26 @@
     )
     whole = lax.all_to_all(halves, ("base", "quad"), split_axis=0, concat_axis=0, tiled=True)
 
-    lane = lax.broadcasted_iota(jnp.int32, (1, depth), 1)
-    still = (place == 0) & (lane % half == 0)
-
-    def mirror(x):
-        return jnp.where(still, x, jnp.roll(x, half, axis=-1))
-
-    c_len = 128
-    d_len = size // c_len
-    bc, bs = (x.astype(np.float32) for x in trig(np.arange(c_len)[:, None] * np.arange(c_len)[None, :], c_len))
-    shape = (c_len, d_len, depth)
-    n0 = c_len * np.arange(d_len)[None, :] + np.arange(c_len)[:, None]
-    ic, isn = (x.astype(np.float32) for x in trig(n0[:, :, None] * np.arange(d_len)[None, None, :], size))
-    pair = jnp.stack([field.reshape(shape), mirror(field).reshape(shape)])
-    first = np.stack([np.stack([bc, bs], 1), np.stack([bs, -bc], 1)], 0)
-    turned = einsum("qbal,qbsc->csal", pair, first)
-    second = np.stack([ic, -isn], axis=2)
-    power = einsum("csal,cdsa->cdl", turned, second)
-    sky = jnp.exp(power / size)
-
-    wide = G // c_len
-    deep = size // wide
-    gc, gs = (x.astype(np.float32) for x in trig(np.arange(deep)[:, None] * np.arange(c_len)[None, :], c_len))
-    first_g = np.stack([np.stack([gc, gs], 1), np.stack([-gs, gc], 1)], 0)
-    whole = whole.reshape(deep, wide, 2, depth)
-    turned_g = einsum("baql,qbsc->csal", whole, first_g)
-    ac, asn = trig((n0 + G // 4)[:, :, None] * np.arange(wide)[None, None, :], G)
-    wave = (ac + 1j * asn) * undone(n0)[:, :, None] / G
-    second_g = np.stack([wave.real, -wave.imag], axis=2).astype(np.float32)
-    back = einsum("csal,cdsa->cdl", turned_g, second_g)
-
-    z = sky * back
-    pz = einsum("cdl,cda->cal", z, ic)
-    qz = einsum("cdl,cda->cal", z, isn)
-    joined = jnp.stack([pz + mirror(qz), mirror(pz) - qz])
-    fold = einsum("qcal,qcb->bal", joined, np.stack([bc, bs]))
-    folded = lax.all_to_all(
-        fold.reshape(n, rows, depth), parts, split_axis=0, concat_axis=0, tiled=True
+    turns, mat_h, mat_f, turns_g, mat_g, slope, bend = (jnp.asarray(x) for x in column_tables(n, size))
+    me = jnp.reshape(place, (1,)).astype(jnp.int32)
+    block = (n, rows, depth)
+    sky = column_call(
+        functools.partial(field_kernel, 1.0 / size),
+        [me],
+        [field.reshape(block), turns, mat_h],
+        block,
+        [pltpu.VMEM((n, 2, rows, depth), jnp.float32)],
+        "field",
     )
+    fold = column_call(
+        image_kernel,
+        [me, bend],
+        [whole, sky, turns_g, mat_g, slope, mat_f, turns],
+        block,
+        [pltpu.VMEM((n, 2, 2 * rows, depth), jnp.float32), pltpu.VMEM((n // 2, 2, 8, depth), jnp.float32)],
+        "image",
+    )
+    folded = lax.all_to_all(fold, parts, split_axis=0, concat_axis=0, tiled=True)
     ends = einsum("jre,jqae->qjra", folded, inner)
     final = einsum("qjra,bqj->rba", ends, outer)
     return amplitude * final.reshape(rows, size) / size

time: 322 us -> 269 us (0.84); the launches traced: 319 us -> 270 us
  matrix products: 49.5 us -> 14.1 us
  local copies, waits for them, and re-layouts: 46.9 us -> 12.6 us
  waiting for transfers between devices: 22.9 us -> 45.7 us
  starting transfers between devices: 32.5 us -> 16.4 us
  Pallas kernels: 94.1 us -> 109 us
    dot_general x12 -> x5, matrix products: 48.7 us -> 13.3 us  [einsum(): jnp.einsum(form, *args, precision=precision, preferred_element_type=jnp.f...]
    pallas_call x0 -> x2, Pallas kernels: none -> 29.3 us  [column_call(): pl.pallas_call(kernel, out_shape=jax.ShapeDtypeStruct(out_shape, jnp.floa...]
    all_to_all x1, waiting for transfers between devices: 22.9 us -> 43.6 us  [shared(): lax.all_to_all(halves, ('base', 'quad'), split_axis=0, concat_axis=0, til...]
    all_to_all x1, starting transfers between devices: 28 us -> 12.4 us  [shared(): lax.all_to_all(halves, ('base', 'quad'), split_axis=0, concat_axis=0, til...]
    transpose x2 -> x0, local copies, waits for them, and re-layouts: 14.4 us -> none  [einsum(): jnp.einsum(form, *args, precision=precision, preferred_element_type=jnp.f...]
    pallas_call x1, Pallas kernels: 50.1 us -> 36.2 us  [grid_rows_two(): pl.pallas_call(grid_rows_kernel, out_shape=jax.ShapeDtypeStruct((depth, r...]
    concatenate x2 -> x0, local copies, waits for them, and re-layouts: 6.41 us -> none  [mirror(): return jnp.where(still, x, jnp.roll(x, half, axis=-1))]
    slice x2 -> x0, local copies, waits for them, and re-layouts: 6.39 us -> none  [mirror(): return jnp.where(still, x, jnp.roll(x, half, axis=-1))]
  transfers between devices with their start and end apart: 2 -> 2, of which waited for: 1 -> 2; matrix products, arithmetic and copies ran while one was open for 11% -> 2% of each run, Pallas kernels for 16% -> 16%
where the time goes in v1:
time: 269 us; the launch traced here: 270 us
  Pallas kernels  109 us (41%)
  blocking collectives  56.4 us (21%)
  waiting for transfers between devices  45.7 us (17%)
  starting transfers between devices  16.4 us (6%)
  other arithmetic  14.6 us (5%)
  matrix products  14.1 us (5%)
  local copies, waits for them, and re-layouts  12.6 us (5%)
    all_to_all x1, blocking collectives, shared(): lax.all_to_all(fold, parts, split_axis=0, concat_axis=0, tiled=True)  56.4 us
    pallas_call x1, Pallas kernels, exchange(): pl.pallas_call(functools.partial(exchange_kernel, nb, ns), out_shape=jax....  44 us
    all_to_all x1, waiting for transfers between devices, shared(): lax.all_to_all(halves, ('base', 'quad'), split_axis=0, concat_axis=0, til...  43.6 us
    pallas_call x1, Pallas kernels, grid_rows_two(): pl.pallas_call(grid_rows_kernel, out_shape=jax.ShapeDtypeStruct((depth, r...  36.2 us
    pallas_call x2, Pallas kernels, column_call(): pl.pallas_call(kernel, out_shape=jax.ShapeDtypeStruct(out_shape, jnp.floa...  29.3 us
    dot_general x5, matrix products, einsum(): jnp.einsum(form, *args, precision=precision, preferred_element_type=jnp.f...  13.3 us
    all_to_all x1, starting transfers between devices, shared(): lax.all_to_all(halves, ('base', 'quad'), split_axis=0, concat_axis=0, til...  12.4 us
    unnamed x51, local copies, waits for them, and re-layouts  11.3 us
  transfers between devices with their start and end apart: 2, of which 2 were waited for; matrix products, arithmetic and copies ran while one was open for 2% of the time, Pallas kernels for 16%

profile of v1, /device:TPU:0, one launch (start us, length us, event | category | flops | bytes accessed | tf_op | source)
XLA Modules:
  0.0 269.7 jit_solution(271876710054478295)
XLA Ops:
  0.0 0.8 broadcast_compare_fusion
  0.8 0.7 and_select_fusion.5
  1.5 0.9 convert_reduce_fusion
  2.4 0.1 select_reduce_fusion.1
  2.6 0.1 convert_element_type.43
  2.7 1.5 fusion.37
  4.2 0.3 pad_maximum_fusion
  4.5 0.1 copy.44
  4.6 0.4 fusion.15
  5.0 0.3 copy.35
  5.4 1.8 multiply_bitcast_fusion
  7.2 0.0 copy-start.19
  7.2 0.4 copy.46
  7.6 0.4 copy-done.19
  8.0 1.8 fusion.38
  9.8 0.4 slice_bitcast_fusion.1
  10.3 0.1 select_maximum_fusion.send_ref
  10.4 44.0 %exchange.1 = f32[8,4,65,4,128]{4,3,2,1,0:T(4,128)S(1)} custom-call(f32[4,65,4,128]{3,2,1,0:T(4,128)S(1)} %select_maximum_fusion.send_ref), custom_call_target="tpu_custom_call" | custom-call | tf_op jit(solution)/shard_map/exchange/pallas_call | solution.py:370
  54.4 2.0 copy-done
  56.3 2.2 fusion.6
  58.6 3.5 %fusion.10 = f32[32,128,128]{2,1,0:T(8,128)} fusion(f32[32,128,128]{2,1,0:T(8,128)S(1)} %fusion.6, f32[32,128,128]{2,1,0:T(8,128)S(1)} %copy-done.17, f32[32,128,128]{2,0,1:T(8,128)S(1)} %get-tuple-element.13), kind=kOutput, calls=%fused_computation.16 | convolution fusion | flops 403177472 | bytes 8388608 | tf_op jit(solution)/shard_map/cra,cae->cre/dot_general | solution.py:129
  62.1 4.0 %all-to-all-start.1 = ((f32[32,128,128]{2,1,0:T(8,128)}), f32[32,128,128]{2,1,0:T(8,128)S(1)}, u32[]{:S(2)}, u32[]{:S(2)}) async-start(f32[32,128,128]{2,1,0:T(8,128)} %fusion.10), calls=%async_computation.1 | async-start | bytes 4194304 | tf_op jit(solution)/shard_map/all_to_all | solution.py:819
  66.2 0.1 copy.36.first_ref
  66.3 0.1 add_multiply_fusion
  66.4 0.1 mul.59
  66.4 0.9 slice_convert_fusion
  67.3 0.2 convolution_reduce_fusion
  67.6 0.1 fusion.14
  67.7 0.1 eq.68
  67.8 1.8 fusion.35
  69.6 0.1 convert_element_type.48
  69.7 1.7 select_reduce_fusion
  71.4 0.7 pad_add_fusion.info_ref
  72.2 2.2 copy-done.1
  74.4 1.4 copy-done.3
  75.8 36.2 %grid_rows_two.1 = f32[16,256,256]{2,1,0:T(8,128)S(1)} custom-call(s32[2]{0:T(128)S(1)} %pad_add_fusion.info_ref, s32[2056]{0:T(1024)S(1)} %pad.9.list_ref, f32[16,2]{1,0:T(8,128)S(1)} %copy.36.first_ref, f32[2080,4,128]{2,1,0:T(4,128)S(1)} %bitcast.85, f32[16,4,128]{2,1,0:T(4,128)S(1)} %dynamic-slice_bitcast_fusion.turn_ref, ...), custom_call_target="tpu_custom_call" | custom-call | flops 20000000000 | bytes 16777216 | tf_op jit(solution)/shard_map/grid_rows_two/pallas_call | solution.py:593
  112.0 2.0 copy-done.2
  114.0 2.0 all-to-all-done.1.field_ref
  116.0 12.4 %all-to-all-start = ((f32[16,256,256]{2,1,0:T(8,128)}), f32[16,256,256]{2,1,0:T(8,128)}, u32[]{:S(2)}, u32[]{:S(2)}) async-start(f32[16,256,256]{2,1,0:T(8,128)} %copy-done.2), calls=%async_computation | async-start | bytes 8388608 | tf_op jit(solution)/shard_map/all_to_all | solution.py:847
  128.5 7.2 %field.1.sky_ref = f32[32,128,128]{2,1,0:T(8,128)S(1)} custom-call(s32[1]{0:T(128)} %bitcast.info_ref, f32[32,128,128]{2,1,0:T(8,128)S(1)} %all-to-all-done.1.field_ref, f32[128,128]{1,0:T(8,128)S(1)} %copy-done.9, bf16[128,768]{1,0:T(8,128)(2,1)S(1)} %copy-done.6), custom_call_target="tpu_custom_call" | custom-call | flops 10000000000 | bytes 16777216 | tf_op jit(solution)/shard_map/field/pallas_call | solution.py:757
  135.7 1.3 copy-done.11
  137.1 43.6 %all-to-all-done.whole_ref = f32[16,256,256]{2,1,0:T(8,128)} async-done(((f32[16,256,256]{2,1,0:T(8,128)}), f32[16,256,256]{2,1,0:T(8,128)}, u32[]{:S(2)}, u32[]{:S(2)}) %all-to-all-start) | async-done | bytes 4194336 | tf_op jit(solution)/shard_map/all_to_all | solution.py:847
  180.7 1.6 copy-done.12
  182.3 22.0 %image.1 = f32[32,128,128]{2,1,0:T(8,128)S(1)} custom-call(s32[1]{0:T(128)} %bitcast.info_ref, f32[32,2]{1,0:T(8,128)S(1)} %copy-done.10, f32[16,256,256]{2,1,0:T(8,128)} %all-to-all-done.whole_ref, f32[32,128,128]{2,1,0:T(8,128)S(1)} %copy-done.12, f32[256,128]{1,0:T(8,128)S(1)} %copy-done.8, bf16[128,1536]{1,0:T(8,128)(2,1)S(1)} %copy-done.4, ...), custom_call_target="tpu_custom_call" | custom-call | flops 10000000000 | bytes 16777216 | tf_op jit(solution)/shard_map/image/pallas_call | solution.py:757
  204.4 56.4 %all_to_all.15 = f32[32,128,128]{2,1,0:T(8,128)S(1)} all-to-all(f32[32,128,128]{2,1,0:T(8,128)S(1)} %image.1), channel_id=1, replica_groups=mesh['base'=4,'half'=2,'quad'=4] {'base','half','quad'}, dimensions={0} | all-to-all | bytes 4194304 | tf_op jit(solution)/shard_map/all_to_all | solution.py:868
  260.7 2.1 fusion.4
  262.9 3.6 %fusion = f32[128,128,32,1]{1,2,3,0:T(8,128)S(1)} fusion(f32[32,2,32,1]{0,2,1,3:T(8,128)S(1)} %copy-done.18, f32[32,128,2,128]{3,1,2,0:T(8,128)S(1)} %fusion.4), kind=kOutput, calls=%fused_computation.2 | convolution fusion | flops 201326592 | bytes 6299648 | tf_op jit(solution)/shard_map/qjra,bqj->rba/dot_general | solution.py:129
  266.6 3.2 %fusion.3 = f32[128,4096]{1,0:T(8,128)} fusion(f32[128,4096]{1,0:T(8,128)S(1)} %copy-done.14, f32[16,8,32,128]{3,2,1,0:T(8,128)S(1)} %bitcast.86), kind=kLoop, calls=%fused_computation.6 | loop fusion | flops 1048576 | bytes 6291456 | tf_op jit(solution)/shard_map/div | solution.py:871
  (52 shorter events, 0.2 us)
Async XLA Ops:
  0.0 5.4 %copy-start.13 = (f32[128,4096]{1,0:T(8,128)S(1)}, f32[128,4096]{1,0:T(8,128)}, u32[]{:S(2)}) copy-start(f32[128,4096]{1,0:T(8,128)} %param.30) | copy-start | bytes 6291460
  7.2 0.8 copy-start.19
  10.4 45.9 %copy-start.16 = (f32[32,128,128]{2,1,0:T(8,128)S(1)}, f32[32,128,128]{2,1,0:T(8,128)}, u32[]{:S(2)}) copy-start(f32[32,128,128]{2,1,0:T(8,128)} %constant.186.clone) | copy-start | bytes 6291460
  54.4 2.0 copy-start
  56.3 2.2 copy-start.17
  62.1 4.1 %copy-start.23 = (f32[2,16,2]{1,2,0:T(2,128)S(1)}, f32[2,16,2]{1,2,0:T(2,128)}, u32[]{:S(2)}) copy-start(f32[2,16,2]{1,2,0:T(2,128)} %constant.189.clone) | copy-start | bytes 772
  62.1 5.2 %copy-start.21 = (f32[32,32]{1,0:T(8,128)S(1)}, f32[32,32]{1,0:T(8,128)}, u32[]{:S(2)}) copy-start(f32[32,32]{1,0:T(8,128)} %constant.188.clone) | copy-start | bytes 12292
  62.1 5.5 %copy-start.24 = (f32[64,64]{1,0:T(8,128)S(1)}, f32[64,64]{1,0:T(8,128)}, u32[]{:S(2)}) copy-start(f32[64,64]{1,0:T(8,128)} %constant.187.clone) | copy-start | bytes 49156
  62.1 10.0 %copy-start.22 = (f32[2,16,2,128]{3,2,1,0:T(2,128)S(1)}, f32[2,16,2,128]{3,2,1,0:T(2,128)}, u32[]{:S(2)}) copy-start(f32[2,16,2,128]{3,2,1,0:T(2,128)} %constant.191.clone) | copy-start | bytes 98308
  62.1 10.0 %copy-start.20 = (f32[2,16,4,128]{3,2,1,0:T(4,128)S(1)}, f32[2,16,4,128]{3,2,1,0:T(4,128)}, u32[]{:S(2)}) copy-start(f32[2,16,4,128]{3,2,1,0:T(4,128)} %constant.190.clone) | copy-start | bytes 196612
  62.1 53.9 %all-to-all-start.1 = ((f32[32,128,128]{2,1,0:T(8,128)}), f32[32,128,128]{2,1,0:T(8,128)S(1)}, u32[]{:S(2)}, u32[]{:S(2)}) async-start(f32[32,128,128]{2,1,0:T(8,128)} %fusion.10), calls=%async_computation.1 | async-start | bytes 4194304 | tf_op jit(solution)/shard_map/all_to_all | solution.py:819
  72.2 2.2 copy-start.1
  74.4 1.4 copy-start.3
  112.0 2.0 copy-start.2
  114.0 14.5 %copy-start.6 = (bf16[128,768]{1,0:T(8,128)(2,1)S(1)}, bf16[128,768]{1,0:T(8,128)(2,1)}, u32[]{:S(2)}) copy-start(bf16[128,768]{1,0:T(8,128)(2,1)} %constant.194.clone.mat_ref) | copy-start | bytes 589828
  114.0 14.5 %copy-start.9 = (f32[128,128]{1,0:T(8,128)S(1)}, f32[128,128]{1,0:T(8,128)}, u32[]{:S(2)}) copy-start(f32[128,128]{1,0:T(8,128)} %constant.193.clone.turn_ref) | copy-start | bytes 196612
  116.0 64.7 %all-to-all-start = ((f32[16,256,256]{2,1,0:T(8,128)}), f32[16,256,256]{2,1,0:T(8,128)}, u32[]{:S(2)}, u32[]{:S(2)}) async-start(f32[16,256,256]{2,1,0:T(8,128)} %copy-done.2), calls=%async_computation | async-start | bytes 8388608 | tf_op jit(solution)/shard_map/all_to_all | solution.py:847
  128.4 52.3 %copy-start.4 = (bf16[128,1536]{1,0:T(8,128)(2,1)S(1)}, bf16[128,1536]{1,0:T(8,128)(2,1)}, u32[]{:S(2)}) copy-start(bf16[128,1536]{1,0:T(8,128)(2,1)} %constant.197.clone.mat_g_ref) | copy-start | bytes 1179652
  128.4 52.2 %copy-start.5 = (bf16[256,384]{1,0:T(8,128)(2,1)S(1)}, bf16[256,384]{1,0:T(8,128)(2,1)}, u32[]{:S(2)}) copy-start(bf16[256,384]{1,0:T(8,128)(2,1)} %constant.195.clone.mat_f_ref) | copy-start | bytes 589828
  128.5 52.2 %copy-start.7 = (f32[2,128,128]{2,1,0:T(8,128)S(1)}, f32[2,128,128]{2,1,0:T(8,128)}, u32[]{:S(2)}) copy-start(f32[2,128,128]{2,1,0:T(8,128)} %constant.198.clone.slope_ref) | copy-start | bytes 393220
  128.5 52.2 %copy-start.8 = (f32[256,128]{1,0:T(8,128)S(1)}, f32[256,128]{1,0:T(8,128)}, u32[]{:S(2)}) copy-start(f32[256,128]{1,0:T(8,128)} %constant.196.clone.turn_g_ref) | copy-start | bytes 393220
  128.5 52.2 %copy-start.10 = (f32[32,2]{1,0:T(8,128)S(1)}, f32[32,2]{1,0:T(8,128)}, u32[]{:S(2)}) copy-start(f32[32,2]{1,0:T(8,128)} %constant.199.clone.bend_ref) | copy-start | bytes 772
  135.7 1.3 copy-start.11
  180.7 1.6 copy-start.12
  204.4 56.4 %copy-start.15 = (f32[32,2,128,128]{3,2,1,0:T(8,128)S(1)}, f32[32,2,128,128]{3,2,1,0:T(8,128)}, u32[]{:S(2)}) copy-start(f32[32,2,128,128]{3,2,1,0:T(8,128)} %constant.200.clone) | copy-start | bytes 12582916
  260.7 2.1 copy-start.18
  262.9 3.6 %copy-start.14 = (f32[128,4096]{1,0:T(8,128)S(1)}, f32[128,4096]{1,0:T(8,128)}, u32[]{:S(2)}) copy-start(f32[128,4096]{1,0:T(8,128)} %param.30) | copy-start | bytes 6291460

commit v2 on v1

--- a/solution.py
+++ b/solution.py
@@ -371,7 +371,7 @@
         functools.partial(exchange_kernel, nb, ns),
         out_shape=jax.ShapeDtypeStruct((ns,) + sent.shape, jnp.float32),
         in_specs=[vmem],
-        out_specs=vmem,
+        out_specs=pl.BlockSpec(memory_space=pl.ANY),
         scratch_shapes=[
             dma((nb,)), dma((nb,)), dma((nz, nb)), dma((nz, nb)), dma((nz, nb)), dma((nz, nb)),
             dma((nz, nb)), dma((nz, nb)), dma,
@@ -384,6 +384,13 @@
 def two_parts(x):
     high = x.astype(jnp.bfloat16)
     return high, (x - high.astype(jnp.float32)).astype(jnp.bfloat16)
+
+
+def through(x, weight_ref, which):
+    rows, depth = x.shape
+    high, low = two_parts(x)
+    made = jnp.dot(jnp.concatenate([high, low], axis=0), weight_ref[which, :depth], preferred_element_type=jnp.float32)
+    return made[:rows] + made[rows:] + jnp.dot(high, weight_ref[which, depth:], preferred_element_type=jnp.float32)
 
 
 def times(x, c, s):
@@ -422,7 +429,7 @@
     return out
 
 
-def grid_rows_kernel(info_ref, list_ref, first_ref, data_ref, turn_ref, undo_ref, weight_ref, out_ref, grid_ref, left_ref, right_ref):
+def grid_kernel_two(info_ref, list_ref, first_ref, data_ref, turn_ref, undo_ref, weight_ref, out_ref, grid_ref, left_ref, right_ref):
     count = info_ref[0]
     parity = info_ref[1]
     grid_ref[...] = jnp.zeros_like(grid_ref)
@@ -522,12 +529,10 @@
         mirrored = depth - parity - a
         mirrored = jnp.where(mirrored == depth, 0, mirrored)
         which = jnp.where((a == 0) & (parity == 0), 1, 0)
-        weight = weight_ref[which]
         for part in range(1):
             spot = pl.ds(0, rows)
             x = jnp.concatenate([grid_ref[q, 2 * a + side, spot, :] for q in range(2) for side in range(2)], axis=1)
-            high, low = two_parts(x)
-            made = jnp.dot(jnp.concatenate([high, low, high], axis=1), weight, preferred_element_type=jnp.float32)
+            made = through(x, weight_ref, which)
             mid = TILE // 2
             made = times((made[:, :TILE], made[:, TILE:]), undo_ref[a, 0:1, :], undo_ref[a, 1:2, :])
             for q in range(2):
@@ -579,8 +584,7 @@
             parts_re.append(np.concatenate([c, -s], axis=0))
             parts_im.append(np.concatenate([s, c], axis=0))
         w = np.concatenate(parts_re + parts_im, axis=1)
-        high_part, low_part = split_table(w)
-        weights.append(np.concatenate([high_part, high_part, low_part], axis=0))
+        weights.append(np.concatenate(split_table(w), axis=0))
     turns, firsts, undos = (np.stack(x).astype(np.float32) for x in (turns, firsts, undos))
     return turns, firsts, undos, np.stack(weights)
 
@@ -591,7 +595,7 @@
     smem = pl.BlockSpec(memory_space=pltpu.SMEM)
     vmem = pl.BlockSpec(memory_space=pltpu.VMEM)
     return pl.pallas_call(
-        grid_rows_kernel,
+        grid_kernel_two,
         out_shape=jax.ShapeDtypeStruct((depth, rows, 2 * TILE), jnp.float32),
         in_specs=[smem, smem, smem, vmem, vmem, vmem, vmem],
         out_specs=vmem,
@@ -600,7 +604,7 @@
             pltpu.VMEM((LANES, TILE, 2 * TILE), jnp.bfloat16),
             pltpu.VMEM((LANES, 2 * TILE, 2 * TILE), jnp.bfloat16),
         ],
-        compiler_params=pltpu.CompilerParams(vmem_limit_bytes=40 << 20),
+        compiler_params=pltpu.CompilerParams(vmem_limit_bytes=20 << 20),
         cost_estimate=pl.CostEstimate(flops=2 * 10**10, bytes_accessed=16 * 2**20, transcendentals=0),
         name="grid_rows_two",
     )(info, table, first, data, turns, undos, weights)
@@ -624,13 +628,19 @@
     return (lane % (TILE // 2) == 0) & (place == 0)
 
 
-def stacked(work_ref, u):
+def product(mat_ref, x):
+    rows = mat_ref.shape[0] // 2
+    high, low = two_parts(x)
+    made = jnp.dot(mat_ref[...], high, preferred_element_type=jnp.float32)
+    return made[:rows] + made[rows:] + jnp.dot(mat_ref[:rows], low, preferred_element_type=jnp.float32)
+
+
+def beside(work_ref, u):
     sides = [jnp.concatenate([work_ref[u + q, 0], work_ref[u + q, 1]], axis=0) for q in range(2)]
-    high, low = two_parts(jnp.concatenate(sides, axis=1))
-    return jnp.concatenate([high, high, low], axis=0)
-
-
-def field_kernel(scale, info_ref, field_ref, turn_ref, mat_ref, sky_ref, work_ref):
+    return jnp.concatenate(sides, axis=1)
+
+
+def field_kernel(scale, info_ref, bend_ref, field_ref, turn_ref, mat_ref, slope_ref, sky_ref, work_ref):
     still = still_lanes(info_ref[0], 8)
     n = field_ref.shape[0]
 
@@ -652,16 +662,17 @@
     lax.fori_loop(0, field_ref.shape[1] // 8, outer, 0)
 
     def inner(k, carry):
-        made = jnp.dot(mat_ref[...], stacked(work_ref, 2 * k), preferred_element_type=jnp.float32)
-        made = jnp.exp(made * scale)
-        sky_ref[2 * k] = made[:, :TILE]
-        sky_ref[2 * k + 1] = made[:, TILE:]
-        return carry
-
-    lax.fori_loop(0, n // 2, inner, 0)
-
-
-def image_kernel(info_ref, bend_ref, whole_ref, sky_ref, turn_g_ref, mat_g_ref, slope_ref, mat_f_ref, turn_ref, out_ref, work_ref, half_ref):
+        for u in (4 * k, 4 * k + 2):
+            made = jnp.exp(product(mat_ref, beside(work_ref, u)) * scale)
+            for q in range(2):
+                sine = slope_ref[0] * bend_ref[u + q, 0] + slope_ref[1] * bend_ref[u + q, 1]
+                sky_ref[u + q] = made[:, q * TILE : (q + 1) * TILE] / sine
+        return carry
+
+    lax.fori_loop(0, n // 4, inner, 0)
+
+
+def image_kernel(info_ref, whole_ref, sky_ref, turn_g_ref, mat_g_ref, mat_f_ref, turn_ref, out_ref, work_ref, half_ref):
     still = still_lanes(info_ref[0], 8)
     n = sky_ref.shape[0]
     depth = n // 2
@@ -682,20 +693,16 @@
     lax.fori_loop(0, whole_ref.shape[1] // 8, outer, 0)
 
     def inner(k, carry):
-        made = jnp.dot(mat_g_ref[...], stacked(work_ref, 2 * k), preferred_element_type=jnp.float32)
-        z = []
-        for q in range(2):
-            u = 2 * k + q
-            sine = slope_ref[0] * bend_ref[u, 0] + slope_ref[1] * bend_ref[u, 1]
-            z.append(made[:, q * TILE : (q + 1) * TILE] * sky_ref[u] / sine)
-        high, low = two_parts(jnp.concatenate(z, axis=1))
-        spread = jnp.dot(mat_f_ref[...], jnp.concatenate([high, high, low], axis=0), preferred_element_type=jnp.float32)
-        for q in range(2):
-            for c in range(2):
-                work_ref[2 * k + q, c, :TILE, :] = spread[c * TILE : (c + 1) * TILE, q * TILE : (q + 1) * TILE]
-        return carry
-
-    lax.fori_loop(0, depth, inner, 0)
+        for u in (4 * k, 4 * k + 2):
+            made = product(mat_g_ref, beside(work_ref, u))
+            z = jnp.concatenate([made[:, q * TILE : (q + 1) * TILE] * sky_ref[u + q] for q in range(2)], axis=1)
+            spread = product(mat_f_ref, z)
+            for q in range(2):
+                for c in range(2):
+                    work_ref[u + q, c, :TILE, :] = spread[c * TILE : (c + 1) * TILE, q * TILE : (q + 1) * TILE]
+        return carry
+
+    lax.fori_loop(0, n // 4, inner, 0)
 
     def last(k, carry):
         spot = pl.ds(pl.multiple_of(k * 8, 8), 8)
@@ -718,6 +725,108 @@
     lax.fori_loop(0, TILE // 8, last, 0)
 
 
+def seat(j, quads):
+    a = j // 2
+    return a // quads * (2 * quads) + j % 2 * quads + a % quads
+
+
+def spectrum_kernel(quads, xi_ref, amplitude_ref, turn_ref, mat_ref, out_ref, work_ref):
+    n = out_ref.shape[0]
+
+    def outer(k, carry):
+        spot = pl.ds(pl.multiple_of(k * 8, 8), 8)
+        for e in range(2):
+            x = []
+            for b in range(n // 2):
+                first, second = (
+                    xi_ref[spot, c * TILE : (c + 1) * TILE] * amplitude_ref[spot, c * TILE : (c + 1) * TILE]
+                    for c in (b, b + n // 2)
+                )
+                value = first - second if e else first + second
+                if e * b:
+                    angle = 2 * math.pi * b / n
+                    x.append((value * math.cos(angle), value * math.sin(angle)))
+                else:
+                    x.append((value, jnp.zeros_like(value)))
+            for v, value in enumerate(sixteen(x)):
+                j = 2 * v + e
+                work_ref[j, 0, spot, :], work_ref[j, 1, spot, :] = times(value, turn_ref[j, 0:1, :], turn_ref[j, 1:2, :])
+        return carry
+
+    lax.fori_loop(0, xi_ref.shape[0] // 8, outer, 0)
+    rows = xi_ref.shape[0]
+
+    def left(entries):
+        return jnp.concatenate([jnp.concatenate([work_ref[j, 0], work_ref[j, 1]], axis=1) for j in entries], axis=0)
+
+    def inner(k, carry):
+        entries = [4 * k + q for q in range(4)]
+        made = through(left(entries), mat_ref, 0)
+        for q, j in enumerate(entries):
+            out_ref[seat(j, quads)] = made[q * rows : (q + 1) * rows]
+        return carry
+
+    lax.fori_loop(0, n // 4, inner, 0)
+    out_ref[0] = through(left([0]), mat_ref, 1)
+
+
+def gradient_kernel(quads, scale, folded_ref, amplitude_ref, turn_ref, mat_ref, out_ref, work_ref, half_ref):
+    n = folded_ref.shape[0]
+    rows = folded_ref.shape[1]
+
+    def before(entries, which):
+        made = through(jnp.concatenate([folded_ref[seat(j, quads)] for j in entries], axis=0), mat_ref, which)
+        for q, j in enumerate(entries):
+            part = made[q * rows : (q + 1) * rows]
+            work_ref[j, 0], work_ref[j, 1] = part[:, :TILE], part[:, TILE:]
+
+    def inner(k, carry):
+        before([4 * k + q for q in range(4)], 0)
+        return carry
+
+    lax.fori_loop(0, n // 4, inner, 0)
+    before([0], 1)
+
+    def outer(k, carry):
+        spot = pl.ds(pl.multiple_of(k * 8, 8), 8)
+        for e in range(2):
+            x = []
+            for v in range(n // 2):
+                j = 2 * v + e
+                x.append(times((work_ref[j, 0, spot, :], work_ref[j, 1, spot, :]), turn_ref[j, 0:1, :], turn_ref[j, 1:2, :]))
+            for b, value in enumerate(sixteen(x)):
+                if e == 0:
+                    half_ref[b] = value[0]
+                    continue
+                real = turn(value, 2 * math.pi * b / n)[0] if b else value[0]
+                for c, total in ((b, half_ref[b] + real), (b + n // 2, half_ref[b] - real)):
+                    lanes = slice(c * TILE, (c + 1) * TILE)
+                    out_ref[spot, lanes] = total * amplitude_ref[spot, lanes] * scale
+        return carry
+
+    lax.fori_loop(0, rows // 8, outer, 0)
+
+
+def row_weights(n, size):
+    alpha = np.arange(TILE)
+    i = np.arange(size // n // 2)
+    turns = np.stack(trig(np.arange(n)[:, None] * alpha[None, :], size), axis=1).astype(np.float32)
+    c, s = trig(alpha[:, None] * i[None, :], size // n)
+    there, back = [], []
+    for special in range(2):
+        real = np.concatenate([c + s, c - s], axis=1)
+        imag = np.concatenate([c - s, -c - s], axis=1)
+        from_real = np.concatenate([c + s, c - s], axis=1)
+        from_imag = np.concatenate([s - c, s + c], axis=1)
+        if special:
+            lane = len(i)
+            real[:, lane] = from_real[:, lane] = 1.0 - 2.0 * (alpha % 2)
+            imag[:, lane] = from_imag[:, lane] = 0.0
+        for target, matrix in ((there, np.concatenate([real, imag], axis=0)), (back, np.concatenate([from_real.T, from_imag.T], axis=1))):
+            target.append(np.concatenate(split_table(matrix), axis=0))
+    return turns, np.stack(there), np.stack(back)
+
+
 def column_tables(n, size):
     w = np.arange(size // n)
     t = np.arange(TILE)
@@ -730,19 +839,18 @@
         out[:, :n], out[:, side : side + n] = c, s
         return out.astype(np.float32)
 
-    def matrix(x, axis_first):
-        high, low = split_table(x)
-        return np.concatenate([high, low, high], axis=1)
+    def matrix(x):
+        return np.concatenate(split_table(x), axis=0)
 
     c, s = trig(t[:, None] * u[None, :], size)
     turns = lanes(c, -s)
     c, s = trig(w[:, None] * t[None, :], size // n)
-    mat_h = matrix(np.concatenate([c, s], axis=1), 0)
-    mat_f = matrix(np.concatenate([c.T, -s.T], axis=0), 0)
+    mat_h = matrix(np.concatenate([c, s], axis=1))
+    mat_f = matrix(np.concatenate([c.T, -s.T], axis=0))
     c, s = trig(r[:, None] * u[None, :], 2 * G)
     turns_g = lanes(c, s)
     c, s = trig((w[:, None] * n + G // 4) * r[None, :], 2 * G)
-    mat_g = matrix(np.concatenate([s, c], axis=1), 0)
+    mat_g = matrix(np.concatenate([s, c], axis=1))
     c, s = trig(w * n + G // 4, 2 * G)
     slope = np.stack([s, c]) * (2.0 * G)
     slope = np.broadcast_to(slope[:, :, None], slope.shape + (TILE,)).astype(np.float32)
@@ -760,7 +868,7 @@
         in_specs=[smem] * len(smems) + [vmem] * len(args),
         out_specs=vmem,
         scratch_shapes=scratch,
-        compiler_params=pltpu.CompilerParams(vmem_limit_bytes=40 << 20),
+        compiler_params=pltpu.CompilerParams(vmem_limit_bytes=24 << 20),
         cost_estimate=pl.CostEstimate(flops=10**10, bytes_accessed=16 * 2**20, transcendentals=0),
         name=name,
     )(*smems, *args)
@@ -773,11 +881,17 @@
     quads = lax.axis_size("quad")
     base, parity, quad = (lax.axis_index(axis) for axis in parts)
     place = 2 * (base * quads + quad) + parity
-    order = np.array([2 * (b * quads + q) + h for b in range(n_base) for h in range(2) for q in range(quads)])
     rows, size = xi.shape
     depth = size // n
     half = depth // 2
     tiles = G // TILE
+
+    row_turns, there, back_again = (jnp.asarray(x) for x in row_weights(n, size))
+    block = (n, rows, depth)
+    work = pltpu.VMEM((n, 2, rows, depth), jnp.float32)
+    spectrum = column_call(
+        functools.partial(spectrum_kernel, quads), [], [xi, amplitude, row_turns, there], block, [work], "spectrum"
+    )
 
     blocks = residual.shape[0]
     region_rows = G // n_slab // TILE
@@ -809,15 +923,8 @@
     codes = jnp.pad(codes.astype(jnp.float32).reshape(n_base, 1, 1, room), ((0, 0), (0, 0), (0, 3), (0, TILE - room)))
     sent = jnp.concatenate([moved.reshape(n_base, room, 4, TILE), codes], axis=1)
     got = exchange(sent, n_slab)
-
-    outer, inner = row_tables(n, size)
-    outer, inner = outer[:, :, order], inner[order]
-    spectrum = (amplitude * xi).reshape(rows, n, depth)
-    mid = einsum("rba,bqc->qcra", spectrum, outer)
-    sent = einsum("cra,cae->cre", mid[0], inner[:, 0]) + einsum("cra,cae->cre", mid[1], inner[:, 1])
-    sent, got = lax.optimization_barrier((sent, got))
-    field = lax.all_to_all(sent, parts, split_axis=0, concat_axis=0, tiled=True)
-    field = field.reshape(size, depth)
+    spectrum, got = lax.optimization_barrier((spectrum, got))
+    field = lax.all_to_all(spectrum, parts, split_axis=0, concat_axis=0, tiled=True)
 
     sources = n_slab * n_base
     codes = got[:, :, room, 0, :room].reshape(sources, room).astype(jnp.int32)
@@ -848,27 +955,31 @@
 
     turns, mat_h, mat_f, turns_g, mat_g, slope, bend = (jnp.asarray(x) for x in column_tables(n, size))
     me = jnp.reshape(place, (1,)).astype(jnp.int32)
-    block = (n, rows, depth)
     sky = column_call(
         functools.partial(field_kernel, 1.0 / size),
-        [me],
-        [field.reshape(block), turns, mat_h],
+        [me, bend],
+        [field, turns, mat_h, slope],
         block,
-        [pltpu.VMEM((n, 2, rows, depth), jnp.float32)],
+        [work],
         "field",
     )
     fold = column_call(
         image_kernel,
-        [me, bend],
-        [whole, sky, turns_g, mat_g, slope, mat_f, turns],
+        [me],
+        [whole, sky, turns_g, mat_g, mat_f, turns],
         block,
         [pltpu.VMEM((n, 2, 2 * rows, depth), jnp.float32), pltpu.VMEM((n // 2, 2, 8, depth), jnp.float32)],
         "image",
     )
     folded = lax.all_to_all(fold, parts, split_axis=0, concat_axis=0, tiled=True)
-    ends = einsum("jre,jqae->qjra", folded, inner)
-    final = einsum("qjra,bqj->rba", ends, outer)
-    return amplitude * final.reshape(rows, size) / size
+    return column_call(
+        functools.partial(gradient_kernel, quads, 1.0 / size),
+        [],
+        [folded, amplitude, row_turns, back_again],
+        (rows, size),
+        [work, pltpu.VMEM((n // 2, 8, depth), jnp.float32)],
+        "gradient",
+    )
 
 
 def solution(mesh):

time: 269 us -> 258 us (0.959)
  matrix products: 14.1 us -> 0.79 us
  Pallas kernels: 109 us -> 121 us
  other arithmetic: 14.6 us -> 9.47 us
  starting transfers between devices: 16.4 us -> 11.6 us
    dot_general x5 -> x0, matrix products: 13.3 us -> none  [einsum(): jnp.einsum(form, *args, precision=precision, preferred_element_type=jnp.f...]
    pallas_call x2 -> x4, Pallas kernels: 29.3 us -> 39.4 us  [column_call(): pl.pallas_call(kernel, out_shape=jax.ShapeDtypeStruct(out_shape, jnp.floa...]
    all_to_all x1, starting transfers between devices: 12.4 us -> 7.77 us  [shared(): lax.all_to_all(halves, ('base', 'quad'), split_axis=0, concat_axis=0, til...]
    div x1 -> x0, other arithmetic: 3.17 us -> none  [shared(): return amplitude * final.reshape(rows, size) / size]
    unnamed x51 -> x50, local copies, waits for them, and re-layouts: 11.3 us -> 10.4 us
  transfers between devices with their start and end apart: 2 -> 2, of which waited for: 2 -> 2; matrix products, arithmetic and copies ran while one was open for 2% -> 2% of each run, Pallas kernels for 16% -> 17%
where the time goes in v2:
time: 258 us
  Pallas kernels  121 us (47%)
  blocking collectives  56.5 us (22%)
  waiting for transfers between devices  46.2 us (18%)
  starting transfers between devices  11.6 us (4%)
  local copies, waits for them, and re-layouts  11.3 us (4%)
  other arithmetic  9.47 us (4%)
    all_to_all x1, blocking collectives, shared(): lax.all_to_all(fold, parts, split_axis=0, concat_axis=0, tiled=True)  56.5 us
    all_to_all x1, waiting for transfers between devices, shared(): lax.all_to_all(halves, ('base', 'quad'), split_axis=0, concat_axis=0, til...  44.2 us
    pallas_call x1, Pallas kernels, exchange(): pl.pallas_call(functools.partial(exchange_kernel, nb, ns), out_shape=jax....  44 us
    pallas_call x4, Pallas kernels, column_call(): pl.pallas_call(kernel, out_shape=jax.ShapeDtypeStruct(out_shape, jnp.floa...  39.4 us
    pallas_call x1, Pallas kernels, grid_rows_two(): pl.pallas_call(grid_kernel_two, out_shape=jax.ShapeDtypeStruct((depth, ro...  37.9 us
    unnamed x50, local copies, waits for them, and re-layouts  10.4 us
    all_to_all x1, starting transfers between devices, shared(): lax.all_to_all(halves, ('base', 'quad'), split_axis=0, concat_axis=0, til...  7.77 us
  transfers between devices with their start and end apart: 2, of which 2 were waited for; matrix products, arithmetic and copies ran while one was open for 2% of the time, Pallas kernels for 17%

profile of v2, /device:TPU:0, one launch (start us, length us, event | category | flops | bytes accessed | tf_op | source)
XLA Modules:
  0.0 257.6 jit_solution(13020515068062070058)
XLA Ops:
  0.0 0.7 broadcast_compare_fusion
  0.7 0.7 and_select_fusion.5
  1.4 0.9 convert_reduce_fusion
  2.3 0.1 select_reduce_fusion.1
  2.4 0.1 convert_element_type.43
  2.5 1.5 fusion.24
  4.0 0.3 pad_maximum_fusion
  4.3 0.0 copy-start.4
  4.3 0.0 copy-start.10
  4.3 0.0 copy-start.16
  4.3 0.1 copy.31
  4.5 0.4 fusion.2
  4.9 0.3 copy.28
  5.3 0.1 select_maximum_fusion.send_ref
  5.4 44.0 %exchange.1 = f32[8,4,65,4,128]{4,3,2,1,0:T(4,128)S(1)} custom-call(f32[4,65,4,128]{3,2,1,0:T(4,128)S(1)} %select_maximum_fusion.send_ref), custom_call_target="tpu_custom_call" | custom-call | tf_op jit(solution)/shard_map/exchange/pallas_call | solution.py:370
  49.4 2.0 copy-done
  51.4 4.7 %spectrum.1 = f32[32,128,128]{2,1,0:T(8,128)S(1)} custom-call(f32[128,4096]{1,0:T(8,128)S(1)} %copy-done.4, f32[128,4096]{1,0:T(8,128)S(1)} %copy-done.5, f32[32,2,128]{2,1,0:T(2,128)S(1)} %copy-done.16, bf16[2,512,128]{2,1,0:T(8,128)(2,1)S(1)} %copy-done.10), custom_call_target="tpu_custom_call" | custom-call | flops 10000000000 | bytes 16777216 | tf_op jit(solution)/shard_map/spectrum/pallas_call | solution.py:865
  56.1 1.3 copy-done.3
  57.4 0.0 copy-start.20
  57.4 0.0 copy-start.7
  57.4 3.9 %all-to-all-start.1 = ((f32[32,128,128]{2,1,0:T(8,128)}), f32[32,128,128]{2,1,0:T(8,128)S(1)}, u32[]{:S(2)}, u32[]{:S(2)}) async-start(f32[32,128,128]{2,1,0:T(8,128)} %copy-done.3), calls=%async_computation.1 | async-start | bytes 4194304 | tf_op jit(solution)/shard_map/all_to_all | solution.py:927
  61.3 0.1 copy.29.first_ref
  61.4 0.1 add_multiply_fusion
  61.5 0.1 mul.52
  61.5 0.9 slice_convert_fusion
  62.5 0.2 convolution_reduce_fusion
  62.7 0.1 fusion.1
  62.8 0.1 eq.68
  62.9 1.7 fusion.22
  64.6 0.1 convert_element_type.48
  64.7 1.7 select_reduce_fusion
  66.5 0.7 pad_add_fusion.info_ref
  67.2 2.2 copy-done.1
  69.4 37.9 %grid_rows_two.1 = f32[16,256,256]{2,1,0:T(8,128)S(1)} custom-call(s32[2]{0:T(128)S(1)} %pad_add_fusion.info_ref, s32[2056]{0:T(1024)S(1)} %pad.9.list_ref, f32[16,2]{1,0:T(8,128)S(1)} %copy.29.first_ref, f32[2080,4,128]{2,1,0:T(4,128)S(1)} %bitcast.49, f32[16,4,128]{2,1,0:T(4,128)S(1)} %dynamic-slice_bitcast_fusion.turn_ref, ...), custom_call_target="tpu_custom_call" | custom-call | flops 20000000000 | bytes 16777216 | tf_op jit(solution)/shard_map/grid_rows_two/pallas_call | solution.py:597
  107.4 2.0 copy-done.2
  109.3 2.0 all-to-all-done.1.field_ref
  111.3 7.8 %all-to-all-start = ((f32[16,256,256]{2,1,0:T(8,128)}), f32[16,256,256]{2,1,0:T(8,128)}, u32[]{:S(2)}, u32[]{:S(2)}) async-start(f32[16,256,256]{2,1,0:T(8,128)} %copy-done.2), calls=%async_computation | async-start | bytes 8388608 | tf_op jit(solution)/shard_map/all_to_all | solution.py:954
  119.1 0.0 copy-start.9
  119.1 0.0 copy-start.11
  119.2 0.0 copy-start.12
  119.2 6.6 %field.1.sky_ref = f32[32,128,128]{2,1,0:T(8,128)S(1)} custom-call(s32[1]{0:T(128)} %bitcast.info_ref, f32[32,2]{1,0:T(8,128)S(1)} %copy-done.17, f32[32,128,128]{2,1,0:T(8,128)S(1)} %all-to-all-done.1.field_ref, f32[128,128]{1,0:T(8,128)S(1)} %copy-done.15, bf16[256,256]{1,0:T(8,128)(2,1)S(1)} %copy-done.14, f32[2,128,128]{2,1,0:T(8,128)S(1)} %copy-done.13), custom_call_target="tpu_custom_call" | custom-call | flops 10000000000 | bytes 16777216 | tf_op jit(solution)/shard_map/field/pallas_call | solution.py:865
  125.8 1.3 copy-done.18
  127.1 44.2 %all-to-all-done.whole_ref = f32[16,256,256]{2,1,0:T(8,128)} async-done(((f32[16,256,256]{2,1,0:T(8,128)}), f32[16,256,256]{2,1,0:T(8,128)}, u32[]{:S(2)}, u32[]{:S(2)}) %all-to-all-start) | async-done | bytes 4194336 | tf_op jit(solution)/shard_map/all_to_all | solution.py:954
  171.4 1.6 copy-done.19
  173.0 22.1 %image.1 = f32[32,128,128]{2,1,0:T(8,128)S(1)} custom-call(s32[1]{0:T(128)} %bitcast.info_ref, f32[16,256,256]{2,1,0:T(8,128)} %all-to-all-done.whole_ref, f32[32,128,128]{2,1,0:T(8,128)S(1)} %copy-done.19, f32[256,128]{1,0:T(8,128)S(1)} %copy-done.11, bf16[256,512]{1,0:T(8,128)(2,1)S(1)} %copy-done.9, bf16[512,128]{1,0:T(8,128)(2,1)S(1)} %copy-done.12, ...), custom_call_target="tpu_custom_call" | custom-call | flops 10000000000 | bytes 16777216 | tf_op jit(solution)/shard_map/image/pallas_call | solution.py:865
  195.1 0.0 copy-start.8
  195.1 56.5 %all_to_all.15.folded_ref = f32[32,128,128]{2,1,0:T(8,128)S(1)} all-to-all(f32[32,128,128]{2,1,0:T(8,128)S(1)} %image.1), channel_id=1, replica_groups=mesh['base'=4,'half'=2,'quad'=4] {'base','half','quad'}, dimensions={0} | all-to-all | bytes 4194304 | tf_op jit(solution)/shard_map/all_to_all | solution.py:974
  251.6 6.0 %gradient.1 = f32[128,4096]{1,0:T(8,128)} custom-call(f32[32,128,128]{2,1,0:T(8,128)S(1)} %all_to_all.15.folded_ref, f32[128,4096]{1,0:T(8,128)S(1)} %copy-done.6, f32[32,2,128]{2,1,0:T(2,128)S(1)} %copy-done.16, bf16[2,256,256]{2,1,0:T(8,128)(2,1)S(1)} %copy-done.8), custom_call_target="tpu_custom_call" | custom-call | flops 10000000000 | bytes 16777216 | tf_op jit(solution)/shard_map/gradient/pallas_call | solution.py:865
  (45 shorter events, 0.2 us)
Async XLA Ops:
  4.3 47.0 %copy-start.4 = (f32[128,4096]{1,0:T(8,128)S(1)}, f32[128,4096]{1,0:T(8,128)}, u32[]{:S(2)}) copy-start(f32[128,4096]{1,0:T(8,128)} %xi_ref.1) | copy-start | bytes 6291460
  4.3 47.0 %copy-start.10 = (bf16[2,512,128]{2,1,0:T(8,128)(2,1)S(1)}, bf16[2,512,128]{2,1,0:T(8,128)(2,1)}, u32[]{:S(2)}) copy-start(bf16[2,512,128]{2,1,0:T(8,128)(2,1)} %constant.179.clone.mat_ref) | copy-start | bytes 786436
  4.3 47.0 %copy-start.16 = (f32[32,2,128]{2,1,0:T(2,128)S(1)}, f32[32,2,128]{2,1,0:T(2,128)}, u32[]{:S(2)}) copy-start(f32[32,2,128]{2,1,0:T(2,128)} %constant.178.clone.turn_ref) | copy-start | bytes 98308
  4.5 46.9 %copy-start.5 = (f32[128,4096]{1,0:T(8,128)S(1)}, f32[128,4096]{1,0:T(8,128)}, u32[]{:S(2)}) copy-start(f32[128,4096]{1,0:T(8,128)} %amplitude_ref.3) | copy-start | bytes 6291460
  49.4 2.0 copy-start
  56.0 1.3 copy-start.3
  57.4 3.9 %copy-start.23 = (f32[2,16,2]{1,2,0:T(2,128)S(1)}, f32[2,16,2]{1,2,0:T(2,128)}, u32[]{:S(2)}) copy-start(f32[2,16,2]{1,2,0:T(2,128)} %constant.184.clone) | copy-start | bytes 772
  57.4 5.1 %copy-start.21 = (f32[32,32]{1,0:T(8,128)S(1)}, f32[32,32]{1,0:T(8,128)}, u32[]{:S(2)}) copy-start(f32[32,32]{1,0:T(8,128)} %constant.183.clone) | copy-start | bytes 12292
  57.4 5.3 %copy-start.24 = (f32[64,64]{1,0:T(8,128)S(1)}, f32[64,64]{1,0:T(8,128)}, u32[]{:S(2)}) copy-start(f32[64,64]{1,0:T(8,128)} %constant.182.clone) | copy-start | bytes 49156
  57.4 9.8 %copy-start.22 = (f32[2,16,2,128]{3,2,1,0:T(2,128)S(1)}, f32[2,16,2,128]{3,2,1,0:T(2,128)}, u32[]{:S(2)}) copy-start(f32[2,16,2,128]{3,2,1,0:T(2,128)} %constant.186.clone) | copy-start | bytes 98308
  57.4 9.8 %copy-start.20 = (f32[2,16,4,128]{3,2,1,0:T(4,128)S(1)}, f32[2,16,4,128]{3,2,1,0:T(4,128)}, u32[]{:S(2)}) copy-start(f32[2,16,4,128]{3,2,1,0:T(4,128)} %constant.185.clone) | copy-start | bytes 196612
  57.4 9.8 %copy-start.7 = (bf16[2,1024,256]{2,1,0:T(8,128)(2,1)S(1)}, bf16[2,1024,256]{2,1,0:T(8,128)(2,1)}, u32[]{:S(2)}) copy-start(bf16[2,1024,256]{2,1,0:T(8,128)(2,1)} %constant.187.clone.weight_ref) | copy-start | bytes 3145732
  57.4 53.9 %all-to-all-start.1 = ((f32[32,128,128]{2,1,0:T(8,128)}), f32[32,128,128]{2,1,0:T(8,128)S(1)}, u32[]{:S(2)}, u32[]{:S(2)}) async-start(f32[32,128,128]{2,1,0:T(8,128)} %copy-done.3), calls=%async_computation.1 | async-start | bytes 4194304 | tf_op jit(solution)/shard_map/all_to_all | solution.py:927
  67.2 2.2 copy-start.1
  107.4 2.0 copy-start.2
  109.3 9.8 %copy-start.13 = (f32[2,128,128]{2,1,0:T(8,128)S(1)}, f32[2,128,128]{2,1,0:T(8,128)}, u32[]{:S(2)}) copy-start(f32[2,128,128]{2,1,0:T(8,128)} %constant.193.clone.slope_ref) | copy-start | bytes 393220
  109.3 9.8 %copy-start.14 = (bf16[256,256]{1,0:T(8,128)(2,1)S(1)}, bf16[256,256]{1,0:T(8,128)(2,1)}, u32[]{:S(2)}) copy-start(bf16[256,256]{1,0:T(8,128)(2,1)} %constant.189.clone.mat_ref) | copy-start | bytes 393220
  109.3 9.8 %copy-start.15 = (f32[128,128]{1,0:T(8,128)S(1)}, f32[128,128]{1,0:T(8,128)}, u32[]{:S(2)}) copy-start(f32[128,128]{1,0:T(8,128)} %constant.188.clone.turn_ref) | copy-start | bytes 196612
  109.3 9.8 %copy-start.17 = (f32[32,2]{1,0:T(8,128)S(1)}, f32[32,2]{1,0:T(8,128)}, u32[]{:S(2)}) copy-start(f32[32,2]{1,0:T(8,128)} %constant.194.clone.bend_ref) | copy-start | bytes 772
  111.3 60.1 %all-to-all-start = ((f32[16,256,256]{2,1,0:T(8,128)}), f32[16,256,256]{2,1,0:T(8,128)}, u32[]{:S(2)}, u32[]{:S(2)}) async-start(f32[16,256,256]{2,1,0:T(8,128)} %copy-done.2), calls=%async_computation | async-start | bytes 8388608 | tf_op jit(solution)/shard_map/all_to_all | solution.py:954
  119.1 52.2 %copy-start.9 = (bf16[256,512]{1,0:T(8,128)(2,1)S(1)}, bf16[256,512]{1,0:T(8,128)(2,1)}, u32[]{:S(2)}) copy-start(bf16[256,512]{1,0:T(8,128)(2,1)} %constant.192.clone.mat_g_ref) | copy-start | bytes 786436
  119.1 52.2 %copy-start.11 = (f32[256,128]{1,0:T(8,128)S(1)}, f32[256,128]{1,0:T(8,128)}, u32[]{:S(2)}) copy-start(f32[256,128]{1,0:T(8,128)} %constant.191.clone.turn_g_ref) | copy-start | bytes 393220
  119.2 52.2 %copy-start.12 = (bf16[512,128]{1,0:T(8,128)(2,1)S(1)}, bf16[512,128]{1,0:T(8,128)(2,1)}, u32[]{:S(2)}) copy-start(bf16[512,128]{1,0:T(8,128)(2,1)} %constant.190.clone.mat_f_ref) | copy-start | bytes 393220
  125.8 1.3 copy-start.18
  171.4 1.6 copy-start.19
  195.1 56.6 %copy-start.6 = (f32[128,4096]{1,0:T(8,128)S(1)}, f32[128,4096]{1,0:T(8,128)}, u32[]{:S(2)}) copy-start(f32[128,4096]{1,0:T(8,128)} %amplitude_ref.3) | copy-start | bytes 6291460
  195.1 56.6 %copy-start.8 = (bf16[2,256,256]{2,1,0:T(8,128)(2,1)S(1)}, bf16[2,256,256]{2,1,0:T(8,128)(2,1)}, u32[]{:S(2)}) copy-start(bf16[2,256,256]{2,1,0:T(8,128)(2,1)} %constant.180.clone.mat_ref) | copy-start | bytes 786436

commit v3 on v2

--- a/solution.py
+++ b/solution.py
@@ -237,150 +237,6 @@
 LANES = 4
 
 
-def exchange_kernel(nb, ns, send_ref, out_ref, bsend, brecv, usend, dsend, lrecv, hrecv, psend, precv, lsem):
-    quads = ns // 2
-    nz = ns // 2
-    base = lax.axis_index("base")
-    slab = lax.axis_index("half") * quads + lax.axis_index("quad")
-    z = slab // 2
-    core = slab % 2
-
-    def at(b, s):
-        return (b, s // quads, s % quads)
-
-    def copy(source, target, here, there, device):
-        return pltpu.make_async_remote_copy(
-            src_ref=source, dst_ref=target, send_sem=here, recv_sem=there, device_id=device, device_id_type=MESH
-        )
-
-    def crossing(k):
-        other = (base + k) % nb
-        return copy(send_ref.at[other], out_ref.at[slab, base], bsend.at[k], brecv.at[k], at(other, slab))
-
-    def arriving(k):
-        from_base = (base - k + nb) % nb
-        return copy(send_ref.at[base], out_ref.at[slab, from_base], bsend.at[k], brecv.at[k], at(from_base, slab))
-
-    def block(origin, k):
-        return out_ref.at[2 * origin + core, (base - k + nb) % nb]
-
-    def upward(s, k):
-        part = block(z - s, k)
-        return copy(part, part, usend.at[s, k], lrecv.at[s + 1, k], at(base, slab + 2))
-
-    def downward(s, k):
-        part = block(z + s, k)
-        return copy(part, part, dsend.at[s, k], hrecv.at[s + 1, k], at(base, slab - 2))
-
-    def from_below(s, k):
-        part = block(z - s, k)
-        return copy(part, part, usend.at[s, k], lrecv.at[s, k], at(base, slab - 2))
-
-    def from_above(s, k):
-        part = block(z + s, k)
-        return copy(part, part, dsend.at[s, k], hrecv.at[s, k], at(base, slab + 2))
-
-    def across(origin, k):
-        part = block(origin, k)
-        return copy(part, part, psend.at[origin, k], precv.at[origin, k], at(base, slab + 1 - 2 * core))
-
-    def from_partner(origin, k):
-        part = out_ref.at[2 * origin + 1 - core, (base - k + nb) % nb]
-        return copy(part, part, psend.at[origin, k], precv.at[origin, k], at(base, slab + 1 - 2 * core))
-
-    barrier = pltpu.get_barrier_semaphore()
-    for k in range(1, nb):
-        pl.semaphore_signal(barrier, inc=1, device_id=at((base + k) % nb, slab), device_id_type=MESH)
-    pl.semaphore_signal(barrier, inc=1, device_id=at(base, slab + 1 - 2 * core), device_id_type=MESH)
-
-    @pl.when(z < nz - 1)
-    def _():
-        pl.semaphore_signal(barrier, inc=1, device_id=at(base, slab + 2), device_id_type=MESH)
-
-    @pl.when(z > 0)
-    def _():
-        pl.semaphore_signal(barrier, inc=1, device_id=at(base, slab - 2), device_id_type=MESH)
-
-    pl.semaphore_wait(barrier, nb + jnp.where(z < nz - 1, 1, 0) + jnp.where(z > 0, 1, 0))
-
-    for k in range(1, nb):
-        crossing(k).start()
-    own = pltpu.make_async_copy(send_ref.at[base], out_ref.at[slab, base], lsem)
-    own.start()
-
-    def pass_on(s, k, ascending, descending):
-        if ascending:
-            @pl.when((z - s >= 0) & (z < nz - 1))
-            def _():
-                upward(s, k).start()
-
-        if descending:
-            @pl.when((z + s < nz) & (z > 0))
-            def _():
-                downward(s, k).start()
-
-    for k in range(nb):
-        if k == 0:
-            own.wait()
-        else:
-            arriving(k).wait_recv()
-        pass_on(0, k, True, True)
-        across(z, k).start()
-    for s in range(1, nz):
-        for k in range(nb):
-            @pl.when(z - s >= 0)
-            def _():
-                from_below(s, k).wait_recv()
-                if s < nz - 1:
-                    pass_on(s, k, True, False)
-                across(z - s, k).start()
-
-            @pl.when(z + s < nz)
-            def _():
-                from_above(s, k).wait_recv()
-                if s < nz - 1:
-                    pass_on(s, k, False, True)
-                across(z + s, k).start()
-
-    for origin in range(nz):
-        for k in range(nb):
-            from_partner(origin, k).wait_recv()
-    for k in range(1, nb):
-        crossing(k).wait_send()
-    for s in range(nz - 1):
-        for k in range(nb):
-            @pl.when((z - s >= 0) & (z < nz - 1))
-            def _():
-                upward(s, k).wait_send()
-
-            @pl.when((z + s < nz) & (z > 0))
-            def _():
-                downward(s, k).wait_send()
-
-    for origin in range(nz):
-        for k in range(nb):
-            across(origin, k).wait_send()
-
-
-def exchange(sent, ns):
-    nb = sent.shape[0]
-    nz = ns // 2
-    dma = pltpu.SemaphoreType.DMA
-    vmem = pl.BlockSpec(memory_space=pltpu.VMEM)
-    return pl.pallas_call(
-        functools.partial(exchange_kernel, nb, ns),
-        out_shape=jax.ShapeDtypeStruct((ns,) + sent.shape, jnp.float32),
-        in_specs=[vmem],
-        out_specs=pl.BlockSpec(memory_space=pl.ANY),
-        scratch_shapes=[
-            dma((nb,)), dma((nb,)), dma((nz, nb)), dma((nz, nb)), dma((nz, nb)), dma((nz, nb)),
-            dma((nz, nb)), dma((nz, nb)), dma,
-        ],
-        compiler_params=pltpu.CompilerParams(collective_id=0, has_side_effects=True, vmem_limit_bytes=16 << 20),
-        name="exchange",
-    )(sent)
-
-
 def two_parts(x):
     high = x.astype(jnp.bfloat16)
     return high, (x - high.astype(jnp.float32)).astype(jnp.bfloat16)
@@ -429,9 +285,274 @@
     return out
 
 
-def grid_kernel_two(info_ref, list_ref, first_ref, data_ref, turn_ref, undo_ref, weight_ref, out_ref, grid_ref, left_ref, right_ref):
-    count = info_ref[0]
+def seat(j, quads):
+    a = j // 2
+    return a // quads * (2 * quads) + j % 2 * quads + a % quads
+
+
+def transform_rows(quads, xi_ref, amplitude_ref, turn_ref, mat_ref, out_ref, work_ref):
+    n = out_ref.shape[0]
+
+    def outer(k, carry):
+        spot = pl.ds(pl.multiple_of(k * 8, 8), 8)
+        for e in range(2):
+            x = []
+            for b in range(n // 2):
+                first, second = (
+                    xi_ref[spot, c * TILE : (c + 1) * TILE] * amplitude_ref[spot, c * TILE : (c + 1) * TILE]
+                    for c in (b, b + n // 2)
+                )
+                value = first - second if e else first + second
+                if e * b:
+                    angle = 2 * math.pi * b / n
+                    x.append((value * math.cos(angle), value * math.sin(angle)))
+                else:
+                    x.append((value, jnp.zeros_like(value)))
+            for v, value in enumerate(sixteen(x)):
+                j = 2 * v + e
+                work_ref[j, 0, spot, :], work_ref[j, 1, spot, :] = times(value, turn_ref[j, 0:1, :], turn_ref[j, 1:2, :])
+        return carry
+
+    lax.fori_loop(0, xi_ref.shape[0] // 8, outer, 0)
+    rows = xi_ref.shape[0]
+
+    def left(entries):
+        return jnp.concatenate([jnp.concatenate([work_ref[j, 0], work_ref[j, 1]], axis=1) for j in entries], axis=0)
+
+    def inner(k, carry):
+        entries = [4 * k + q for q in range(4)]
+        made = through(left(entries), mat_ref, 0)
+        for q, j in enumerate(entries):
+            out_ref[seat(j, quads)] = made[q * rows : (q + 1) * rows]
+        return carry
+
+    lax.fori_loop(0, n // 4, inner, 0)
+    out_ref[0] = through(left([0]), mat_ref, 1)
+
+
+def exchange_kernel(nb, ns, send_ref, xi_ref, amplitude_ref, turn_ref, mat_ref, out_ref, spectrum_ref, work_ref, rows_ref, rows_sem, bsend, brecv, usend, dsend, lrecv, hrecv, psend, precv, lsem):
+    quads = ns // 2
+    nz = ns // 2
+    base = lax.axis_index("base")
+    slab = lax.axis_index("half") * quads + lax.axis_index("quad")
+    z = slab // 2
+    core = slab % 2
+
+    def at(b, s):
+        return (b, s // quads, s % quads)
+
+    def copy(source, target, here, there, device):
+        return pltpu.make_async_remote_copy(
+            src_ref=source, dst_ref=target, send_sem=here, recv_sem=there, device_id=device, device_id_type=MESH
+        )
+
+    def crossing(k):
+        other = (base + k) % nb
+        return copy(send_ref.at[other], out_ref.at[slab, base], bsend.at[k], brecv.at[k], at(other, slab))
+
+    def arriving(k):
+        from_base = (base - k + nb) % nb
+        return copy(send_ref.at[base], out_ref.at[slab, from_base], bsend.at[k], brecv.at[k], at(from_base, slab))
+
+    def block(origin, k):
+        return out_ref.at[2 * origin + core, (base - k + nb) % nb]
+
+    def upward(s, k):
+        part = block(z - s, k)
+        return copy(part, part, usend.at[s, k], lrecv.at[s + 1, k], at(base, slab + 2))
+
+    def downward(s, k):
+        part = block(z + s, k)
+        return copy(part, part, dsend.at[s, k], hrecv.at[s + 1, k], at(base, slab - 2))
+
+    def from_below(s, k):
+        part = block(z - s, k)
+        return copy(part, part, usend.at[s, k], lrecv.at[s, k], at(base, slab - 2))
+
+    def from_above(s, k):
+        part = block(z + s, k)
+        return copy(part, part, dsend.at[s, k], hrecv.at[s, k], at(base, slab + 2))
+
+    def across(origin, k):
+        part = block(origin, k)
+        return copy(part, part, psend.at[origin, k], precv.at[origin, k], at(base, slab + 1 - 2 * core))
+
+    def from_partner(origin, k):
+        part = out_ref.at[2 * origin + 1 - core, (base - k + nb) % nb]
+        return copy(part, part, psend.at[origin, k], precv.at[origin, k], at(base, slab + 1 - 2 * core))
+
+    fetches = [
+        pltpu.make_async_copy(source, rows_ref.at[k], rows_sem.at[k]) for k, source in enumerate((xi_ref, amplitude_ref))
+    ]
+    for fetch in fetches:
+        fetch.start()
+    barrier = pltpu.get_barrier_semaphore()
+    for k in range(1, nb):
+        pl.semaphore_signal(barrier, inc=1, device_id=at((base + k) % nb, slab), device_id_type=MESH)
+    pl.semaphore_signal(barrier, inc=1, device_id=at(base, slab + 1 - 2 * core), device_id_type=MESH)
+
+    @pl.when(z < nz - 1)
+    def _():
+        pl.semaphore_signal(barrier, inc=1, device_id=at(base, slab + 2), device_id_type=MESH)
+
+    @pl.when(z > 0)
+    def _():
+        pl.semaphore_signal(barrier, inc=1, device_id=at(base, slab - 2), device_id_type=MESH)
+
+    pl.semaphore_wait(barrier, nb + jnp.where(z < nz - 1, 1, 0) + jnp.where(z > 0, 1, 0))
+
+    for k in range(1, nb):
+        crossing(k).start()
+    own = pltpu.make_async_copy(send_ref.at[base], out_ref.at[slab, base], lsem)
+    own.start()
+
+    def pass_on(s, k, ascending, descending):
+        if ascending:
+            @pl.when((z - s >= 0) & (z < nz - 1))
+            def _():
+                upward(s, k).start()
+
+        if descending:
+            @pl.when((z + s < nz) & (z > 0))
+            def _():
+                downward(s, k).start()
+
+    for k in range(nb):
+        if k == 0:
+            own.wait()
+        else:
+            arriving(k).wait_recv()
+        pass_on(0, k, True, True)
+        across(z, k).start()
+        if k == 0:
+            for fetch in fetches:
+                fetch.wait()
+            transform_rows(quads, rows_ref.at[0], rows_ref.at[1], turn_ref, mat_ref, spectrum_ref, work_ref)
+    for s in range(1, nz):
+        for k in range(nb):
+            @pl.when(z - s >= 0)
+            def _():
+                from_below(s, k).wait_recv()
+                if s < nz - 1:
+                    pass_on(s, k, True, False)
+                across(z - s, k).start()
+
+            @pl.when(z + s < nz)
+            def _():
+                from_above(s, k).wait_recv()
+                if s < nz - 1:
+                    pass_on(s, k, False, True)
+                across(z + s, k).start()
+
+    for origin in range(nz):
+        for k in range(nb):
+            from_partner(origin, k).wait_recv()
+    for k in range(1, nb):
+        crossing(k).wait_send()
+    for s in range(nz - 1):
+        for k in range(nb):
+            @pl.when((z - s >= 0) & (z < nz - 1))
+            def _():
+                upward(s, k).wait_send()
+
+            @pl.when((z + s < nz) & (z > 0))
+            def _():
+                downward(s, k).wait_send()
+
+    for origin in range(nz):
+        for k in range(nb):
+            across(origin, k).wait_send()
+
+
+def pack_kernel(keys, room, what_ref, residual_ref, position_ref, out_ref):
+    blocks = residual_ref.shape[0]
+    nb = out_ref.shape[0]
+    across = lax.broadcasted_iota(jnp.int32, (blocks, blocks), 1)
+    down = lax.broadcasted_iota(jnp.int32, (blocks, blocks), 0)
+
+    def column(row):
+        return jnp.sum(jnp.where(across == down, row, 0.0), axis=1, keepdims=True)
+
+    what = what_ref[...].astype(jnp.float32)
+    line, key, code, flip = (what[k : k + 1, :] for k in range(4))
+    line_down, key_down, flip_down = column(line), column(key), column(flip)
+    before = (line_down == line) & ((key_down < key) | ((key_down == key) & (down < across)))
+    slot = line * room + jnp.sum(jnp.where(before, 1.0, 0.0), axis=0, keepdims=True)
+    slots = lax.broadcasted_iota(jnp.int32, (nb * room, blocks), 0).astype(jnp.float32)
+    chosen = jnp.where(slots == slot, 1.0, 0.0).astype(jnp.bfloat16)
+    sides = [residual_ref[:, 0, :], residual_ref[:, 1, :] * (1.0 - 2.0 * flip_down)]
+    for k in range(2):
+        place = position_ref[:, k, :]
+        sides.append(jnp.where(flip_down > 0.5, TILE - place, place))
+    pieces = split_three(jnp.concatenate(sides, axis=1))
+    moved = jnp.dot(
+        jnp.concatenate([chosen] * 3, axis=1), jnp.concatenate(pieces, axis=0), preferred_element_type=jnp.float32
+    )
+    codes = 0.0
+    for part in two_parts(jnp.broadcast_to(code + 1.0, (8, blocks))):
+        codes = codes + lax.dot_general(part, chosen, (((1,), (1,)), ((), ())), preferred_element_type=jnp.float32)
+    codes = codes - 1.0
+    lanes = lax.broadcasted_iota(jnp.int32, (1, blocks), 1)
+    shift = (across - room).astype(jnp.float32)
+    per = blocks // room
+    for k in range(nb):
+        for c in range(4):
+            out_ref[k, :room, c, :] = moved[k * room : (k + 1) * room, c * TILE : (c + 1) * TILE]
+        start = k // per * blocks
+        own = codes[:, start : start + blocks]
+        if k % per:
+            own = pltpu.roll(own, blocks - k % per * room, 1)
+        earlier = (line_down == k) & (key_down - keys * k < shift)
+        starts = jnp.sum(jnp.where(earlier, 1.0, 0.0), axis=0, keepdims=True)
+        out_ref[k, room] = jnp.broadcast_to(jnp.where(lanes < room, own[0:1, :], starts), (4, TILE))
+
+
+def pack(what, residual, position, nb, keys, room):
+    vmem = pl.BlockSpec(memory_space=pltpu.VMEM)
+    return pl.pallas_call(
+        functools.partial(pack_kernel, keys, room),
+        out_shape=jax.ShapeDtypeStruct((nb, room + 1, 4, TILE), jnp.float32),
+        in_specs=[vmem] * 3,
+        out_specs=vmem,
+        compiler_params=pltpu.CompilerParams(vmem_limit_bytes=16 << 20),
+        name="pack",
+    )(what, residual, position)
+
+
+def exchange(sent, ns, xi, amplitude, turns, mats):
+    nb = sent.shape[0]
+    nz = ns // 2
+    rows, n = xi.shape[0], turns.shape[0]
+    dma = pltpu.SemaphoreType.DMA
+    vmem = pl.BlockSpec(memory_space=pltpu.VMEM)
+    hbm = pl.BlockSpec(memory_space=pltpu.HBM)
+    return pl.pallas_call(
+        functools.partial(exchange_kernel, nb, ns),
+        out_shape=(
+            jax.ShapeDtypeStruct((ns,) + sent.shape, jnp.float32),
+            jax.ShapeDtypeStruct((n, rows, TILE), jnp.float32),
+        ),
+        in_specs=[vmem, hbm, hbm, vmem, vmem],
+        out_specs=(hbm, vmem),
+        scratch_shapes=[
+            pltpu.VMEM((n, 2, rows, TILE), jnp.float32),
+            pltpu.VMEM((2,) + xi.shape, jnp.float32), dma((2,)),
+            dma((nb,)), dma((nb,)), dma((nz, nb)), dma((nz, nb)), dma((nz, nb)), dma((nz, nb)),
+            dma((nz, nb)), dma((nz, nb)), dma,
+        ],
+        compiler_params=pltpu.CompilerParams(collective_id=0, has_side_effects=True, vmem_limit_bytes=60 << 20),
+        cost_estimate=pl.CostEstimate(flops=3 * 10**10, bytes_accessed=16 * 2**20, transcendentals=0),
+        name="exchange",
+    )(sent, xi, amplitude, turns, mats)
+
+
+def grid_kernel_two(room, info_ref, codes_ref, first_ref, data_hbm_ref, turn_ref, undo_ref, weight_hbm_ref, away_ref, grid_ref, left_ref, right_ref, out_ref, data_ref, weight_ref, list_ref, sems):
+    quad = info_ref[0]
     parity = info_ref[1]
+    data = pltpu.make_async_copy(data_hbm_ref, data_ref, sems.at[out_ref.shape[0]])
+    weight = pltpu.make_async_copy(weight_hbm_ref, weight_ref, sems.at[out_ref.shape[0] + 1])
+    data.start()
+    weight.start()
     grid_ref[...] = jnp.zeros_like(grid_ref)
     half = grid_ref.shape[1]
     group = 16
@@ -466,7 +587,7 @@
         packed = list_ref[k]
         return packed % 64, packed // 64
 
-    def prepare(k, lane):
+    def prepare(k, lane, count):
         col, rest = place(k)
         odd = jnp.where(col >= half, parity, 0)
         sign = jnp.where(k < count, 1 - 2 * odd, 0).astype(jnp.float32)
@@ -492,7 +613,7 @@
     def step(k, carry):
         made = [product(lane) for lane in range(lanes)]
         for lane in range(lanes):
-            prepare((k + 1) * lanes + lane, lane)
+            prepare((k + 1) * lanes + lane, lane, count)
         for lane in range(lanes):
             col, rest = place(k * lanes + lane)
             col = jnp.where(col >= half, col - half, col)
@@ -501,8 +622,23 @@
             grid_ref[1, col, spot, :] += made[lane][:, TILE:]
         return carry
 
+    def gather(source, filled):
+        start = codes_ref[source, room + quad]
+        stop = codes_ref[source, room + quad + 1]
+
+        def entry(i, carry):
+            list_ref[filled + i - start] = (source * (room + 1) + i) * TILE + codes_ref[source, i] % TILE
+            return carry
+
+        lax.fori_loop(start, stop, entry, 0)
+        return filled + stop - start
+
+    count = lax.fori_loop(0, codes_ref.shape[0], gather, 0)
+    for lane in range(2 * lanes):
+        list_ref[count + lane] = 0
+    data.wait()
     for lane in range(lanes):
-        prepare(lane, lane)
+        prepare(lane, lane, count)
     lax.fori_loop(0, (count + lanes - 1) // lanes, step, 0)
 
     depth = half // 2
@@ -514,10 +650,10 @@
             x = []
             for b in range(depth):
                 value = grid_ref[0, 2 * b + side, spot, :], grid_ref[1, 2 * b + side, spot, :]
-                x.append(times(value, first_ref[b, 0], first_ref[b, 1]))
+                x.append(times(value, first_ref[parity, b, 0], first_ref[parity, b, 1]))
             for a, value in enumerate(sixteen(x)):
-                c = turn_ref[a, side : side + 1, :]
-                s = turn_ref[a, 2 + side : 3 + side, :]
+                c = turn_ref[parity, a, side : side + 1, :]
+                s = turn_ref[parity, a, 2 + side : 3 + side, :]
                 value = times(value, c, s)
                 grid_ref[0, 2 * a + side, spot, :] = value[0]
                 grid_ref[1, 2 * a + side, spot, :] = value[1]
@@ -534,13 +670,25 @@
             x = jnp.concatenate([grid_ref[q, 2 * a + side, spot, :] for q in range(2) for side in range(2)], axis=1)
             made = through(x, weight_ref, which)
             mid = TILE // 2
-            made = times((made[:, :TILE], made[:, TILE:]), undo_ref[a, 0:1, :], undo_ref[a, 1:2, :])
+            made = times((made[:, :TILE], made[:, TILE:]), undo_ref[parity, a, 0:1, :], undo_ref[parity, a, 1:2, :])
             for q in range(2):
                 out_ref[a, spot, q * TILE : q * TILE + mid] = made[q][:, :mid]
                 out_ref[mirrored, spot, q * TILE + mid : (q + 1) * TILE] = made[q][:, mid:]
-        return carry
-
+
+        @pl.when(a >= depth // 2)
+        def _():
+            leave(a).start()
+            leave(jnp.where((parity == 0) & (a == depth // 2), 0, mirrored)).start()
+
+        return carry
+
+    def leave(a):
+        return pltpu.make_async_copy(out_ref.at[a], away_ref.at[a], sems.at[a])
+
+    weight.wait()
     lax.fori_loop(0, depth, inner, 0)
+    for a in range(depth):
+        leave(a).wait()
 
 
 def split_table(x):
@@ -589,25 +737,31 @@
     return turns, firsts, undos, np.stack(weights)
 
 
-def grid_rows_two(info, table, first, data, turns, undos, weights):
-    depth = turns.shape[0]
+def grid_rows_two(room, info, codes, first, data, turns, undos, weights):
+    depth = turns.shape[1]
     rows = 2 * TILE
     smem = pl.BlockSpec(memory_space=pltpu.SMEM)
     vmem = pl.BlockSpec(memory_space=pltpu.VMEM)
+    hbm = pl.BlockSpec(memory_space=pltpu.HBM)
     return pl.pallas_call(
-        grid_kernel_two,
+        functools.partial(grid_kernel_two, room),
         out_shape=jax.ShapeDtypeStruct((depth, rows, 2 * TILE), jnp.float32),
-        in_specs=[smem, smem, smem, vmem, vmem, vmem, vmem],
-        out_specs=vmem,
+        in_specs=[smem, smem, smem, hbm, vmem, vmem, hbm],
+        out_specs=hbm,
         scratch_shapes=[
             pltpu.VMEM((2, 2 * depth, rows, TILE), jnp.float32),
             pltpu.VMEM((LANES, TILE, 2 * TILE), jnp.bfloat16),
             pltpu.VMEM((LANES, 2 * TILE, 2 * TILE), jnp.bfloat16),
+            pltpu.VMEM((depth, rows, 2 * TILE), jnp.float32),
+            pltpu.VMEM(data.shape, jnp.float32),
+            pltpu.VMEM(weights.shape, jnp.bfloat16),
+            pltpu.SMEM((codes.shape[0] * room + 2 * LANES,), jnp.int32),
+            pltpu.SemaphoreType.DMA((depth + 2,)),
         ],
-        compiler_params=pltpu.CompilerParams(vmem_limit_bytes=20 << 20),
+        compiler_params=pltpu.CompilerParams(vmem_limit_bytes=60 << 20),
         cost_estimate=pl.CostEstimate(flops=2 * 10**10, bytes_accessed=16 * 2**20, transcendentals=0),
         name="grid_rows_two",
-    )(info, table, first, data, turns, undos, weights)
+    )(info, codes, first, data, turns, undos, weights)
 
 
 def minus(x):
@@ -672,9 +826,11 @@
     lax.fori_loop(0, n // 4, inner, 0)
 
 
-def image_kernel(info_ref, whole_ref, sky_ref, turn_g_ref, mat_g_ref, mat_f_ref, turn_ref, out_ref, work_ref, half_ref):
+def image_kernel(info_ref, whole_ref, sky_ref, turn_g_ref, mat_g_ref, mat_f_ref, turn_ref, out_ref, work_ref, half_ref, held_ref, held_sem):
     still = still_lanes(info_ref[0], 8)
     n = sky_ref.shape[0]
+    fetch = pltpu.make_async_copy(sky_ref, held_ref, held_sem)
+    fetch.start()
     depth = n // 2
 
     def outer(k, carry):
@@ -692,10 +848,12 @@
 
     lax.fori_loop(0, whole_ref.shape[1] // 8, outer, 0)
 
+    fetch.wait()
+
     def inner(k, carry):
         for u in (4 * k, 4 * k + 2):
             made = product(mat_g_ref, beside(work_ref, u))
-            z = jnp.concatenate([made[:, q * TILE : (q + 1) * TILE] * sky_ref[u + q] for q in range(2)], axis=1)
+            z = jnp.concatenate([made[:, q * TILE : (q + 1) * TILE] * held_ref[u + q] for q in range(2)], axis=1)
             spread = product(mat_f_ref, z)
             for q in range(2):
                 for c in range(2):
@@ -723,51 +881,6 @@
         return carry
 
     lax.fori_loop(0, TILE // 8, last, 0)
-
-
-def seat(j, quads):
-    a = j // 2
-    return a // quads * (2 * quads) + j % 2 * quads + a % quads
-
-
-def spectrum_kernel(quads, xi_ref, amplitude_ref, turn_ref, mat_ref, out_ref, work_ref):
-    n = out_ref.shape[0]
-
-    def outer(k, carry):
-        spot = pl.ds(pl.multiple_of(k * 8, 8), 8)
-        for e in range(2):
-            x = []
-            for b in range(n // 2):
-                first, second = (
-                    xi_ref[spot, c * TILE : (c + 1) * TILE] * amplitude_ref[spot, c * TILE : (c + 1) * TILE]
-                    for c in (b, b + n // 2)
-                )
-                value = first - second if e else first + second
-                if e * b:
-                    angle = 2 * math.pi * b / n
-                    x.append((value * math.cos(angle), value * math.sin(angle)))
-                else:
-                    x.append((value, jnp.zeros_like(value)))
-            for v, value in enumerate(sixteen(x)):
-                j = 2 * v + e
-                work_ref[j, 0, spot, :], work_ref[j, 1, spot, :] = times(value, turn_ref[j, 0:1, :], turn_ref[j, 1:2, :])
-        return carry
-
-    lax.fori_loop(0, xi_ref.shape[0] // 8, outer, 0)
-    rows = xi_ref.shape[0]
-
-    def left(entries):
-        return jnp.concatenate([jnp.concatenate([work_ref[j, 0], work_ref[j, 1]], axis=1) for j in entries], axis=0)
-
-    def inner(k, carry):
-        entries = [4 * k + q for q in range(4)]
-        made = through(left(entries), mat_ref, 0)
-        for q, j in enumerate(entries):
-            out_ref[seat(j, quads)] = made[q * rows : (q + 1) * rows]
-        return carry
-
-    lax.fori_loop(0, n // 4, inner, 0)
-    out_ref[0] = through(left([0]), mat_ref, 1)
 
 
 def gradient_kernel(quads, scale, folded_ref, amplitude_ref, turn_ref, mat_ref, out_ref, work_ref, half_ref):
@@ -859,13 +972,14 @@
     return turns, mat_h, mat_f, turns_g, mat_g, slope, bend
 
 
-def column_call(kernel, smems, args, out_shape, scratch, name):
+def column_call(kernel, smems, args, out_shape, scratch, name, away=()):
     smem = pl.BlockSpec(memory_space=pltpu.SMEM)
     vmem = pl.BlockSpec(memory_space=pltpu.VMEM)
+    anywhere = pl.BlockSpec(memory_space=pltpu.HBM)
     return pl.pallas_call(
         kernel,
         out_shape=jax.ShapeDtypeStruct(out_shape, jnp.float32),
-        in_specs=[smem] * len(smems) + [vmem] * len(args),
+        in_specs=[smem] * len(smems) + [anywhere if k in away else vmem for k in range(len(args))],
         out_specs=vmem,
         scratch_shapes=scratch,
         compiler_params=pltpu.CompilerParams(vmem_limit_bytes=24 << 20),
@@ -889,10 +1003,6 @@
     row_turns, there, back_again = (jnp.asarray(x) for x in row_weights(n, size))
     block = (n, rows, depth)
     work = pltpu.VMEM((n, 2, rows, depth), jnp.float32)
-    spectrum = column_call(
-        functools.partial(spectrum_kernel, quads), [], [xi, amplitude, row_turns, there], block, [work], "spectrum"
-    )
-
     blocks = residual.shape[0]
     region_rows = G // n_slab // TILE
     region_cols = G // n_base // TILE
@@ -905,50 +1015,25 @@
     tile_col = jnp.where(flip, tiles - 1 - tile_col, tile_col)
     line = tile_row // n_slab
     code = (tile_row % n_slab) * tiles + tile_col
-    flipped = flip[:, None]
-    payload = jnp.stack(
-        [
-            residual[:, 0],
-            jnp.where(flipped, -residual[:, 1], residual[:, 1]),
-            jnp.where(flipped, TILE - position[:, 0], position[:, 0]),
-            jnp.where(flipped, TILE - position[:, 1], position[:, 1]),
-        ],
-        axis=1,
-    )
-    earlier = (line[:, None] == line[None, :]) & (np.arange(blocks)[:, None] > np.arange(blocks)[None, :])
-    slot = line * room + jnp.sum(earlier.astype(jnp.int32), axis=1)
-    chosen = slot[None, :] == lax.broadcasted_iota(jnp.int32, (n_base * room, blocks), 0)
-    moved = jnp.dot(chosen.astype(jnp.float32), payload.reshape(blocks, 4 * TILE), precision=fine)
-    codes = jnp.sum(jnp.where(chosen, code[None, :] + 1, 0), axis=1) - 1
-    codes = jnp.pad(codes.astype(jnp.float32).reshape(n_base, 1, 1, room), ((0, 0), (0, 0), (0, 3), (0, TILE - room)))
-    sent = jnp.concatenate([moved.reshape(n_base, room, 4, TILE), codes], axis=1)
-    got = exchange(sent, n_slab)
-    spectrum, got = lax.optimization_barrier((spectrum, got))
+    pair = tile_row // 2
+    what = jnp.stack([line, pair, code, flip.astype(jnp.int32)])
+    sent = pack(what, residual, position, n_base, n_slab // 2, room)
+    got, spectrum = exchange(sent, n_slab, xi, amplitude, row_turns, there)
     field = lax.all_to_all(spectrum, parts, split_axis=0, concat_axis=0, tiled=True)
 
     sources = n_slab * n_base
-    codes = got[:, :, room, 0, :room].reshape(sources, room).astype(jnp.int32)
-    mine = (codes >= 0) & (codes // tiles // 2 == quad)
-    ones = mine.astype(jnp.float32)
-    before = jnp.dot(ones, np.triu(np.ones((room, room), np.float32), 1), precision=fine)
-    above = jnp.dot(np.tril(np.ones((sources, sources), np.float32), -1), ones, precision=fine)
-    rank = (before + jnp.sum(above, axis=1, keepdims=True)).astype(jnp.int32)
-    rank = jnp.where(mine, rank, -1).reshape(-1)
-    index = lax.broadcasted_iota(jnp.int32, (sources, room), 0) * (room + 1) + lax.broadcasted_iota(jnp.int32, (sources, room), 1)
-    packed = (index * (2 * tiles) + codes % (2 * tiles)).reshape(-1)
-    spots = lax.broadcasted_iota(jnp.int32, (sources * room, sources * room), 0)
-    table = jnp.sum(jnp.where(spots == rank[None, :], packed[None, :], 0), axis=1)
-    table = jnp.pad(table, (0, 2 * LANES))
-    info = jnp.stack([jnp.sum(mine.astype(jnp.int32)), parity]).astype(jnp.int32)
+    codes = got[:, :, room, 0, :].reshape(sources, TILE).astype(jnp.int32)
+    info = jnp.stack([quad, parity]).astype(jnp.int32)
 
     turns, firsts, undos, weights = grid_row_weights(n, size)
     halves = grid_rows_two(
+        room,
         info,
-        table,
-        lax.dynamic_index_in_dim(jnp.asarray(firsts), parity, 0, keepdims=False),
+        codes,
+        jnp.asarray(firsts),
         got.reshape(sources * (room + 1), 4, TILE),
-        lax.dynamic_index_in_dim(jnp.asarray(turns), parity, 0, keepdims=False),
-        lax.dynamic_index_in_dim(jnp.asarray(undos), parity, 0, keepdims=False),
+        jnp.asarray(turns),
+        jnp.asarray(undos),
         jnp.asarray(weights),
     )
     whole = lax.all_to_all(halves, ("base", "quad"), split_axis=0, concat_axis=0, tiled=True)
@@ -968,8 +1053,10 @@
         [me],
         [whole, sky, turns_g, mat_g, mat_f, turns],
         block,
-        [pltpu.VMEM((n, 2, 2 * rows, depth), jnp.float32), pltpu.VMEM((n // 2, 2, 8, depth), jnp.float32)],
+        [pltpu.VMEM((n, 2, 2 * rows, depth), jnp.float32), pltpu.VMEM((n // 2, 2, 8, depth), jnp.float32),
+         pltpu.VMEM(block, jnp.float32), pltpu.SemaphoreType.DMA],
         "image",
+        away=(1,),
     )
     folded = lax.all_to_all(fold, parts, split_axis=0, concat_axis=0, tiled=True)
     return column_call(

time: 258 us -> 255 us (0.988)
  Pallas kernels: 121 us -> 135 us
  other arithmetic: 9.47 us -> 3.44 us
  local copies, waits for them, and re-layouts: 11.3 us -> 5.57 us
  starting transfers between devices: 11.6 us -> 8.8 us
    pallas_call x2 -> x3, Pallas kernels: 81.9 us -> 100 us  [the longest x1 51.6 us: grid_rows_two(): pl.pallas_call(functools.partial(grid_kernel_two, room), out_shape=jax.Sh...]
    unnamed x50 -> x30, local copies, waits for them, and re-layouts: 10.4 us -> 5.57 us
    pallas_call x4 -> x3, Pallas kernels: 39.4 us -> 34.9 us  [column_call(): pl.pallas_call(kernel, out_shape=jax.ShapeDtypeStruct(out_shape, jnp.floa...]
    all_to_all x1, starting transfers between devices: 7.77 us -> 4.68 us  [shared(): lax.all_to_all(halves, ('base', 'quad'), split_axis=0, concat_axis=0, til...]
    reduce_sum x3 -> x0, other arithmetic: 2.75 us -> none  [the longest x1 1.74 us: shared(): jnp.sum(jnp.where(spots == rank[None, :], packed[None, :], 0), axis=1)]
  transfers between devices with their start and end apart: 2 -> 2, of which waited for: 2 -> 1; matrix products, arithmetic and copies ran while one was open for 2% -> 1% of each run, Pallas kernels for 17% -> 23%
where the time goes in v3:
time: 255 us; the launch traced here: 254 us
  Pallas kernels  135 us (53%)
  blocking collectives  56.6 us (22%)
  waiting for transfers between devices  44.1 us (17%)
  starting transfers between devices  8.8 us (3%)
  local copies, waits for them, and re-layouts  5.57 us (2%)
  other arithmetic  3.44 us (1%)
    all_to_all x1, blocking collectives, shared(): lax.all_to_all(fold, parts, split_axis=0, concat_axis=0, tiled=True)  56.6 us
    pallas_call x1, Pallas kernels, grid_rows_two(): pl.pallas_call(functools.partial(grid_kernel_two, room), out_shape=jax.Sh...  51.6 us
    pallas_call x1, Pallas kernels, exchange(): pl.pallas_call(functools.partial(exchange_kernel, nb, ns), out_shape=(jax...  47.9 us
    all_to_all x1, waiting for transfers between devices, shared(): lax.all_to_all(halves, ('base', 'quad'), split_axis=0, concat_axis=0, til...  44.1 us
    pallas_call x3, Pallas kernels, column_call(): pl.pallas_call(kernel, out_shape=jax.ShapeDtypeStruct(out_shape, jnp.floa...  34.9 us
    unnamed x30, local copies, waits for them, and re-layouts  5.57 us
  transfers between devices with their start and end apart: 2, of which 1 were waited for; matrix products, arithmetic and copies ran while one was open for 1% of the time, Pallas kernels for 23%

profile of v3, /device:TPU:0, one launch (start us, length us, event | category | flops | bytes accessed | tf_op | source)
XLA Modules:
  0.0 253.9 jit_solution(12274834870861887875)
XLA Ops:
  0.0 0.7 fusion.8
  0.7 0.7 fusion.7
  1.4 0.0 copy-start.1
  1.4 0.9 copy-done.1
  2.3 0.0 copy-start.2
  2.3 0.9 copy-done.2
  3.2 0.9 pack.1.send_ref
  4.1 0.0 copy-start
  4.1 0.8 copy-done
  4.9 47.9 %exchange.1 = (f32[8,4,65,4,128]{4,3,2,1,0:T(4,128)}, f32[32,128,128]{2,1,0:T(8,128)}) custom-call(f32[4,65,4,128]{3,2,1,0:T(4,128)} %copy-done, f32[128,4096]{1,0:T(8,128)} %xi_ref.1, f32[128,4096]{1,0:T(8,128)} %amplitude_ref.3, f32[32,2,128]{2,1,0:T(2,128)} %constant.119.clone.turn_ref, bf16[2,512,128]{2,1,0:T(8,128)(2,1)} %constant.120.clone.mat_ref), custom_call_target="tpu_custom_call" | custom-call | flops 30000001024 | bytes 16777216 | tf_op jit(solution)/shard_map/exchange/pallas_call | solution.py:529
  52.8 4.1 %all-to-all-start.1 = ((f32[32,128,128]{2,1,0:T(8,128)}), f32[32,128,128]{2,1,0:T(8,128)S(1)}, u32[]{:S(2)}, u32[]{:S(2)}) async-start(f32[32,128,128]{2,1,0:T(8,128)} %get-tuple-element.8), calls=%async_computation.1 | async-start | bytes 4194304 | tf_op jit(solution)/shard_map/all_to_all | solution.py:1022
  56.9 0.6 pad_add_fusion.1.info_ref
  57.5 1.5 slice_convert_fusion
  58.9 51.6 %grid_rows_two.1 = f32[16,256,256]{2,1,0:T(8,128)} custom-call(s32[2]{0:T(128)} %pad_add_fusion.1.info_ref, s32[32,128]{1,0:T(8,128)} %bitcast.33, f32[2,16,2]{2,1,0:T(8,128)} %constant.122.clone.first_ref, f32[2080,4,128]{2,1,0:T(4,128)} %bitcast.34, f32[2,16,4,128]{3,2,1,0:T(4,128)} %constant.123.clone.turn_ref, ...), custom_call_target="tpu_custom_call" | custom-call | flops 20000000000 | bytes 16777216 | tf_op jit(solution)/shard_map/grid_rows_two/pallas_call | solution.py:746
  110.5 0.0 copy-start.8
  110.5 0.0 copy-start.9
  110.5 0.0 copy-start.10
  110.6 0.0 copy-start.12
  110.6 0.0 all-to-all-done.1.field_ref
  110.6 4.7 %all-to-all-start = ((f32[16,256,256]{2,1,0:T(8,128)}), f32[16,256,256]{2,1,0:T(8,128)}, u32[]{:S(2)}, u32[]{:S(2)}) async-start(f32[16,256,256]{2,1,0:T(8,128)} %grid_rows_two.1), calls=%async_computation | async-start | bytes 8388608 | tf_op jit(solution)/shard_map/all_to_all | solution.py:1039
  115.3 0.0 copy-done.8
  115.3 0.0 copy-done.9
  115.3 0.0 copy-done.10
  115.3 0.0 copy-done.12
  115.3 0.0 copy-start.5
  115.3 0.0 copy-start.6
  115.3 0.0 copy-start.7
  115.4 6.6 %field.1.sky_ref = f32[32,128,128]{2,1,0:T(8,128)S(1)} custom-call(s32[1]{0:T(128)} %bitcast.info_ref, f32[32,2]{1,0:T(8,128)S(1)} %copy-done.12, f32[32,128,128]{2,1,0:T(8,128)S(1)} %all-to-all-done.1.field_ref, f32[128,128]{1,0:T(8,128)S(1)} %copy-done.10, bf16[256,256]{1,0:T(8,128)(2,1)S(1)} %copy-done.9, f32[2,128,128]{2,1,0:T(8,128)S(1)} %copy-done.8), custom_call_target="tpu_custom_call" | custom-call | flops 10000000000 | bytes 16777216 | tf_op jit(solution)/shard_map/field/pallas_call | solution.py:979
  122.0 0.0 copy-start.13
  122.0 1.3 copy-done.13
  123.3 44.1 %all-to-all-done.whole_ref = f32[16,256,256]{2,1,0:T(8,128)} async-done(((f32[16,256,256]{2,1,0:T(8,128)}), f32[16,256,256]{2,1,0:T(8,128)}, u32[]{:S(2)}, u32[]{:S(2)}) %all-to-all-start) | async-done | bytes 4194336 | tf_op jit(solution)/shard_map/all_to_all | solution.py:1039
  167.4 0.0 copy-done.5
  167.4 0.0 copy-done.6
  167.4 0.0 copy-done.7
  167.4 0.0 copy-start.14
  167.4 1.6 copy-done.14
  169.0 22.3 %image.1 = f32[32,128,128]{2,1,0:T(8,128)S(1)} custom-call(s32[1]{0:T(128)} %bitcast.info_ref, f32[16,256,256]{2,1,0:T(8,128)} %all-to-all-done.whole_ref, f32[32,128,128]{2,1,0:T(8,128)S(1)} %copy-done.14, f32[256,128]{1,0:T(8,128)S(1)} %copy-done.6, bf16[256,512]{1,0:T(8,128)(2,1)S(1)} %copy-done.5, bf16[512,128]{1,0:T(8,128)(2,1)S(1)} %copy-done.7, ...), custom_call_target="tpu_custom_call" | custom-call | flops 10000000000 | bytes 16777216 | tf_op jit(solution)/shard_map/image/pallas_call | solution.py:979
  191.3 0.0 copy-start.3
  191.3 0.0 copy-start.4
  191.3 0.0 copy-start.11
  191.3 56.6 %all_to_all.15.folded_ref = f32[32,128,128]{2,1,0:T(8,128)S(1)} all-to-all(f32[32,128,128]{2,1,0:T(8,128)S(1)} %image.1), channel_id=1, replica_groups=mesh['base'=4,'half'=2,'quad'=4] {'base','half','quad'}, dimensions={0} | all-to-all | bytes 4194304 | tf_op jit(solution)/shard_map/all_to_all | solution.py:1061
  247.9 0.0 copy-done.3
  247.9 0.0 copy-done.4
  247.9 0.0 copy-done.11
  247.9 6.0 %gradient.1 = f32[128,4096]{1,0:T(8,128)} custom-call(f32[32,128,128]{2,1,0:T(8,128)S(1)} %all_to_all.15.folded_ref, f32[128,4096]{1,0:T(8,128)S(1)} %copy-done.3, f32[32,2,128]{2,1,0:T(2,128)S(1)} %copy-done.11, bf16[2,256,256]{2,1,0:T(8,128)(2,1)S(1)} %copy-done.4), custom_call_target="tpu_custom_call" | custom-call | flops 10000000000 | bytes 16777216 | tf_op jit(solution)/shard_map/gradient/pallas_call | solution.py:979
  (2 shorter events, 0.0 us)
Async XLA Ops:
  1.4 0.9 copy-start.1
  2.3 0.9 copy-start.2
  4.1 0.8 copy-start
  52.8 57.8 %all-to-all-start.1 = ((f32[32,128,128]{2,1,0:T(8,128)}), f32[32,128,128]{2,1,0:T(8,128)S(1)}, u32[]{:S(2)}, u32[]{:S(2)}) async-start(f32[32,128,128]{2,1,0:T(8,128)} %get-tuple-element.8), calls=%async_computation.1 | async-start | bytes 4194304 | tf_op jit(solution)/shard_map/all_to_all | solution.py:1022
  110.5 4.8 %copy-start.8 = (f32[2,128,128]{2,1,0:T(8,128)S(1)}, f32[2,128,128]{2,1,0:T(8,128)}, u32[]{:S(2)}) copy-start(f32[2,128,128]{2,1,0:T(8,128)} %constant.131.clone.slope_ref) | copy-start | bytes 393220
  110.5 4.8 %copy-start.9 = (bf16[256,256]{1,0:T(8,128)(2,1)S(1)}, bf16[256,256]{1,0:T(8,128)(2,1)}, u32[]{:S(2)}) copy-start(bf16[256,256]{1,0:T(8,128)(2,1)} %constant.127.clone.mat_ref) | copy-start | bytes 393220
  110.5 4.8 %copy-start.10 = (f32[128,128]{1,0:T(8,128)S(1)}, f32[128,128]{1,0:T(8,128)}, u32[]{:S(2)}) copy-start(f32[128,128]{1,0:T(8,128)} %constant.126.clone.turn_ref) | copy-start | bytes 196612
  110.6 4.8 %copy-start.12 = (f32[32,2]{1,0:T(8,128)S(1)}, f32[32,2]{1,0:T(8,128)}, u32[]{:S(2)}) copy-start(f32[32,2]{1,0:T(8,128)} %constant.132.clone.bend_ref) | copy-start | bytes 772
  110.6 56.8 %all-to-all-start = ((f32[16,256,256]{2,1,0:T(8,128)}), f32[16,256,256]{2,1,0:T(8,128)}, u32[]{:S(2)}, u32[]{:S(2)}) async-start(f32[16,256,256]{2,1,0:T(8,128)} %grid_rows_two.1), calls=%async_computation | async-start | bytes 8388608 | tf_op jit(solution)/shard_map/all_to_all | solution.py:1039
  115.3 52.1 %copy-start.5 = (bf16[256,512]{1,0:T(8,128)(2,1)S(1)}, bf16[256,512]{1,0:T(8,128)(2,1)}, u32[]{:S(2)}) copy-start(bf16[256,512]{1,0:T(8,128)(2,1)} %constant.130.clone.mat_g_ref) | copy-start | bytes 786436
  115.3 52.1 %copy-start.6 = (f32[256,128]{1,0:T(8,128)S(1)}, f32[256,128]{1,0:T(8,128)}, u32[]{:S(2)}) copy-start(f32[256,128]{1,0:T(8,128)} %constant.129.clone.turn_g_ref) | copy-start | bytes 393220
  115.3 52.1 %copy-start.7 = (bf16[512,128]{1,0:T(8,128)(2,1)S(1)}, bf16[512,128]{1,0:T(8,128)(2,1)}, u32[]{:S(2)}) copy-start(bf16[512,128]{1,0:T(8,128)(2,1)} %constant.128.clone.mat_f_ref) | copy-start | bytes 393220
  122.0 1.3 copy-start.13
  167.4 1.6 copy-start.14
  191.3 56.7 %copy-start.3 = (f32[128,4096]{1,0:T(8,128)S(1)}, f32[128,4096]{1,0:T(8,128)}, u32[]{:S(2)}) copy-start(f32[128,4096]{1,0:T(8,128)} %amplitude_ref.3) | copy-start | bytes 6291460
  191.3 56.7 %copy-start.4 = (bf16[2,256,256]{2,1,0:T(8,128)(2,1)S(1)}, bf16[2,256,256]{2,1,0:T(8,128)(2,1)}, u32[]{:S(2)}) copy-start(bf16[2,256,256]{2,1,0:T(8,128)(2,1)} %constant.121.clone.mat_ref) | copy-start | bytes 786436
  191.3 56.6 %copy-start.11 = (f32[32,2,128]{2,1,0:T(2,128)S(1)}, f32[32,2,128]{2,1,0:T(2,128)}, u32[]{:S(2)}) copy-start(f32[32,2,128]{2,1,0:T(2,128)} %constant.119.clone.turn_ref) | copy-start | bytes 98308

commit v4 on v3

--- a/solution.py
+++ b/solution.py
@@ -330,7 +330,7 @@
     out_ref[0] = through(left([0]), mat_ref, 1)
 
 
-def exchange_kernel(nb, ns, send_ref, xi_ref, amplitude_ref, turn_ref, mat_ref, out_ref, spectrum_ref, work_ref, rows_ref, rows_sem, bsend, brecv, usend, dsend, lrecv, hrecv, psend, precv, lsem):
+def exchange_kernel(nb, ns, send_ref, xi_ref, amplitude_ref, turn_ref, mat_ref, out_ref, spectrum_ref, work_ref, made_ref, rows_ref, rows_sem, bsend, brecv, usend, dsend, lrecv, hrecv, psend, precv, lsem):
     quads = ns // 2
     nz = ns // 2
     base = lax.axis_index("base")
@@ -384,6 +384,7 @@
     fetches = [
         pltpu.make_async_copy(source, rows_ref.at[k], rows_sem.at[k]) for k, source in enumerate((xi_ref, amplitude_ref))
     ]
+    ready = pltpu.make_async_copy(made_ref, spectrum_ref, rows_sem.at[2])
     for fetch in fetches:
         fetch.start()
     barrier = pltpu.get_barrier_semaphore()
@@ -427,7 +428,8 @@
         if k == 0:
             for fetch in fetches:
                 fetch.wait()
-            transform_rows(quads, rows_ref.at[0], rows_ref.at[1], turn_ref, mat_ref, spectrum_ref, work_ref)
+            transform_rows(quads, rows_ref.at[0], rows_ref.at[1], turn_ref, mat_ref, made_ref, work_ref)
+            ready.start()
     for s in range(1, nz):
         for k in range(nb):
             @pl.when(z - s >= 0)
@@ -444,6 +446,7 @@
                     pass_on(s, k, False, True)
                 across(z + s, k).start()
 
+    ready.wait()
     for origin in range(nz):
         for k in range(nb):
             from_partner(origin, k).wait_recv()
@@ -464,7 +467,7 @@
             across(origin, k).wait_send()
 
 
-def pack_kernel(keys, room, what_ref, residual_ref, position_ref, out_ref):
+def pack_kernel(ns, tiles, room, owner_ref, local_ref, residual_ref, position_ref, out_ref):
     blocks = residual_ref.shape[0]
     nb = out_ref.shape[0]
     across = lax.broadcasted_iota(jnp.int32, (blocks, blocks), 1)
@@ -473,8 +476,23 @@
     def column(row):
         return jnp.sum(jnp.where(across == down, row, 0.0), axis=1, keepdims=True)
 
-    what = what_ref[...].astype(jnp.float32)
-    line, key, code, flip = (what[k : k + 1, :] for k in range(4))
+    def divided(x, d):
+        whole = jnp.floor((x + 0.5) * (1.0 / d))
+        return whole, x - whole * d
+
+    local = local_ref[...].astype(jnp.float32)
+    target = owner_ref[...].astype(jnp.float32)
+    region_col, region_row = divided(target, ns)
+    tile_row, tile_col = divided(local, tiles // nb)
+    tile_row = tile_row + region_row * (tiles // ns)
+    tile_col = tile_col + region_col * (tiles // nb)
+    flip = jnp.where(tile_row >= tiles // 2, 1.0, 0.0)
+    tile_row = jnp.where(flip > 0.5, tiles - 1 - tile_row, tile_row)
+    tile_col = jnp.where(flip > 0.5, tiles - 1 - tile_col, tile_col)
+    line, within = divided(tile_row, ns)
+    key = divided(tile_row, 2)[0]
+    code = within * tiles + tile_col
+    keys = ns // 2
     line_down, key_down, flip_down = column(line), column(key), column(flip)
     before = (line_down == line) & ((key_down < key) | ((key_down == key) & (down < across)))
     slot = line * room + jnp.sum(jnp.where(before, 1.0, 0.0), axis=0, keepdims=True)
@@ -507,16 +525,16 @@
         out_ref[k, room] = jnp.broadcast_to(jnp.where(lanes < room, own[0:1, :], starts), (4, TILE))
 
 
-def pack(what, residual, position, nb, keys, room):
+def pack(owner, local, residual, position, nb, ns, room):
     vmem = pl.BlockSpec(memory_space=pltpu.VMEM)
     return pl.pallas_call(
-        functools.partial(pack_kernel, keys, room),
+        functools.partial(pack_kernel, ns, G // TILE, room),
         out_shape=jax.ShapeDtypeStruct((nb, room + 1, 4, TILE), jnp.float32),
-        in_specs=[vmem] * 3,
+        in_specs=[vmem] * 4,
         out_specs=vmem,
-        compiler_params=pltpu.CompilerParams(vmem_limit_bytes=16 << 20),
+        compiler_params=pltpu.CompilerParams(vmem_limit_bytes=60 << 20),
         name="pack",
-    )(what, residual, position)
+    )(owner.reshape(1, -1), local.reshape(1, -1), residual, position)
 
 
 def exchange(sent, ns, xi, amplitude, turns, mats):
@@ -533,10 +551,11 @@
             jax.ShapeDtypeStruct((n, rows, TILE), jnp.float32),
         ),
         in_specs=[vmem, hbm, hbm, vmem, vmem],
-        out_specs=(hbm, vmem),
+        out_specs=(hbm, hbm),
         scratch_shapes=[
             pltpu.VMEM((n, 2, rows, TILE), jnp.float32),
-            pltpu.VMEM((2,) + xi.shape, jnp.float32), dma((2,)),
+            pltpu.VMEM((n, rows, TILE), jnp.float32),
+            pltpu.VMEM((2,) + xi.shape, jnp.float32), dma((3,)),
             dma((nb,)), dma((nb,)), dma((nz, nb)), dma((nz, nb)), dma((nz, nb)), dma((nz, nb)),
             dma((nz, nb)), dma((nz, nb)), dma,
         ],
@@ -826,9 +845,42 @@
     lax.fori_loop(0, n // 4, inner, 0)
 
 
-def image_kernel(info_ref, whole_ref, sky_ref, turn_g_ref, mat_g_ref, mat_f_ref, turn_ref, out_ref, work_ref, half_ref, held_ref, held_sem):
-    still = still_lanes(info_ref[0], 8)
+def image_kernel(scale, whole_ref, sky_ref, turn_g_ref, mat_g_ref, mat_f_ref, turn_ref, turn_r_ref, mat_r_ref, out_ref, work_ref, half_ref, held_ref, fold_ref, folded_ref, real_ref, held_sem, send_sems, recv_sems):
     n = sky_ref.shape[0]
+    quads = lax.axis_size("quad")
+    halves = lax.axis_size("half")
+    me = (lax.axis_index("base") * halves + lax.axis_index("half")) * quads + lax.axis_index("quad")
+    place = 2 * (lax.axis_index("base") * quads + lax.axis_index("quad")) + lax.axis_index("half")
+    still = still_lanes(place, 8)
+    pieces = send_sems.shape[0]
+    span = TILE // pieces
+
+    def at(device):
+        return (device // (halves * quads), device // quads % halves, device % quads)
+
+    def sending(c, k):
+        target = (me + k) % n
+        part = pl.ds(c * span, span)
+        return pltpu.make_async_remote_copy(
+            src_ref=fold_ref.at[target, part], dst_ref=folded_ref.at[me, part],
+            send_sem=send_sems.at[c, k], recv_sem=recv_sems.at[c, k], device_id=at(target), device_id_type=MESH,
+        )
+
+    def arriving(c, k):
+        source = (me - k + n) % n
+        part = pl.ds(c * span, span)
+        return pltpu.make_async_remote_copy(
+            src_ref=fold_ref.at[source, part], dst_ref=folded_ref.at[source, part],
+            send_sem=send_sems.at[c, k], recv_sem=recv_sems.at[c, k], device_id=at(source), device_id_type=MESH,
+        )
+
+    barrier = pltpu.get_barrier_semaphore()
+
+    def greet(k, carry):
+        pl.semaphore_signal(barrier, inc=1, device_id=at((me + k) % n), device_id_type=MESH)
+        return carry
+
+    lax.fori_loop(1, n, greet, 0)
     fetch = pltpu.make_async_copy(sky_ref, held_ref, held_sem)
     fetch.start()
     depth = n // 2
@@ -877,47 +929,61 @@
                 value = turn(value, -2 * math.pi * d / n) if d else value
                 before = half_ref[d, 0], half_ref[d, 1]
                 for side, both_parts in enumerate((add(before, value), sub(before, value))):
-                    out_ref[d + side * depth, spot, :] = both_parts[0] - mirrored(both_parts[1], still)
-        return carry
-
-    lax.fori_loop(0, TILE // 8, last, 0)
-
-
-def gradient_kernel(quads, scale, folded_ref, amplitude_ref, turn_ref, mat_ref, out_ref, work_ref, half_ref):
-    n = folded_ref.shape[0]
-    rows = folded_ref.shape[1]
-
-    def before(entries, which):
-        made = through(jnp.concatenate([folded_ref[seat(j, quads)] for j in entries], axis=0), mat_ref, which)
-        for q, j in enumerate(entries):
-            part = made[q * rows : (q + 1) * rows]
-            work_ref[j, 0], work_ref[j, 1] = part[:, :TILE], part[:, TILE:]
-
-    def inner(k, carry):
-        before([4 * k + q for q in range(4)], 0)
-        return carry
-
-    lax.fori_loop(0, n // 4, inner, 0)
-    before([0], 1)
-
-    def outer(k, carry):
+                    fold_ref[d + side * depth, spot, :] = both_parts[0] - mirrored(both_parts[1], still)
+        return carry
+
+    def send(c, k, carry):
+        sending(c, k).start()
+        return carry
+
+    for c in range(pieces):
+        lax.fori_loop(c * span // 8, (c + 1) * span // 8, last, 0)
+        if c == 0:
+            pl.semaphore_wait(barrier, n - 1)
+        lax.fori_loop(1, n, functools.partial(send, c), 0)
+    folded_ref[me] = fold_ref[me]
+
+    def receive(source):
+        a = source // (halves * quads) * quads + source % quads
+        j = 2 * a + source // quads % halves
+        made = through(folded_ref[source], mat_r_ref, jnp.where(j == 0, 1, 0))
+        work_ref[j, 0, :TILE, :], work_ref[j, 1, :TILE, :] = made[:, :TILE], made[:, TILE:]
+
+    receive(me)
+
+    def arrive(k, carry):
+        for c in range(pieces):
+            arriving(c, k).wait_recv()
+        receive((me - k + n) % n)
+        return carry
+
+    lax.fori_loop(1, n, arrive, 0)
+
+    def gradient(k, carry):
         spot = pl.ds(pl.multiple_of(k * 8, 8), 8)
         for e in range(2):
             x = []
-            for v in range(n // 2):
+            for v in range(depth):
                 j = 2 * v + e
-                x.append(times((work_ref[j, 0, spot, :], work_ref[j, 1, spot, :]), turn_ref[j, 0:1, :], turn_ref[j, 1:2, :]))
+                x.append(times((work_ref[j, 0, spot, :], work_ref[j, 1, spot, :]), turn_r_ref[j, 0:1, :], turn_r_ref[j, 1:2, :]))
             for b, value in enumerate(sixteen(x)):
                 if e == 0:
-                    half_ref[b] = value[0]
+                    real_ref[b] = value[0]
                     continue
                 real = turn(value, 2 * math.pi * b / n)[0] if b else value[0]
-                for c, total in ((b, half_ref[b] + real), (b + n // 2, half_ref[b] - real)):
+                for c, total in ((b, real_ref[b] + real), (b + depth, real_ref[b] - real)):
                     lanes = slice(c * TILE, (c + 1) * TILE)
-                    out_ref[spot, lanes] = total * amplitude_ref[spot, lanes] * scale
-        return carry
-
-    lax.fori_loop(0, rows // 8, outer, 0)
+                    out_ref[spot, lanes] = total * scale
+        return carry
+
+    lax.fori_loop(0, TILE // 8, gradient, 0)
+
+    def sent(k, carry):
+        for c in range(pieces):
+            sending(c, k).wait_send()
+        return carry
+
+    lax.fori_loop(1, n, sent, 0)
 
 
 def row_weights(n, size):
@@ -972,7 +1038,7 @@
     return turns, mat_h, mat_f, turns_g, mat_g, slope, bend
 
 
-def column_call(kernel, smems, args, out_shape, scratch, name, away=()):
+def column_call(kernel, smems, args, out_shape, scratch, name, away=(), **params):
     smem = pl.BlockSpec(memory_space=pltpu.SMEM)
     vmem = pl.BlockSpec(memory_space=pltpu.VMEM)
     anywhere = pl.BlockSpec(memory_space=pltpu.HBM)
@@ -982,7 +1048,7 @@
         in_specs=[smem] * len(smems) + [anywhere if k in away else vmem for k in range(len(args))],
         out_specs=vmem,
         scratch_shapes=scratch,
-        compiler_params=pltpu.CompilerParams(vmem_limit_bytes=24 << 20),
+        compiler_params=pltpu.CompilerParams(**{"vmem_limit_bytes": 24 << 20, **params}),
         cost_estimate=pl.CostEstimate(flops=10**10, bytes_accessed=16 * 2**20, transcendentals=0),
         name=name,
     )(*smems, *args)
@@ -1004,20 +1070,8 @@
     block = (n, rows, depth)
     work = pltpu.VMEM((n, 2, rows, depth), jnp.float32)
     blocks = residual.shape[0]
-    region_rows = G // n_slab // TILE
-    region_cols = G // n_base // TILE
     room = 2 * n_base * (2 * blocks // n)
-    target = owner[:, 0]
-    tile_row = (target % n_slab) * region_rows + tile_local // region_cols
-    tile_col = (target // n_slab) * region_cols + tile_local % region_cols
-    flip = tile_row >= tiles // 2
-    tile_row = jnp.where(flip, tiles - 1 - tile_row, tile_row)
-    tile_col = jnp.where(flip, tiles - 1 - tile_col, tile_col)
-    line = tile_row // n_slab
-    code = (tile_row % n_slab) * tiles + tile_col
-    pair = tile_row // 2
-    what = jnp.stack([line, pair, code, flip.astype(jnp.int32)])
-    sent = pack(what, residual, position, n_base, n_slab // 2, room)
+    sent = pack(owner, tile_local, residual, position, n_base, n_slab, room)
     got, spectrum = exchange(sent, n_slab, xi, amplitude, row_turns, there)
     field = lax.all_to_all(spectrum, parts, split_axis=0, concat_axis=0, tiled=True)
 
@@ -1048,24 +1102,23 @@
         [work],
         "field",
     )
-    fold = column_call(
-        image_kernel,
-        [me],
-        [whole, sky, turns_g, mat_g, mat_f, turns],
-        block,
-        [pltpu.VMEM((n, 2, 2 * rows, depth), jnp.float32), pltpu.VMEM((n // 2, 2, 8, depth), jnp.float32),
-         pltpu.VMEM(block, jnp.float32), pltpu.SemaphoreType.DMA],
+    pieces = 4
+    dma = pltpu.SemaphoreType.DMA
+    return amplitude * column_call(
+        functools.partial(image_kernel, 1.0 / size),
+        [],
+        [whole, sky, turns_g, mat_g, mat_f, turns, row_turns, back_again],
+        (rows, size),
+        [
+            pltpu.VMEM((n, 2, 2 * rows, depth), jnp.float32), pltpu.VMEM((n // 2, 2, 8, depth), jnp.float32),
+            pltpu.VMEM(block, jnp.float32), pltpu.VMEM(block, jnp.float32), pltpu.VMEM(block, jnp.float32),
+            pltpu.VMEM((n // 2, 8, depth), jnp.float32), dma, dma((pieces, n)), dma((pieces, n)),
+        ],
         "image",
         away=(1,),
-    )
-    folded = lax.all_to_all(fold, parts, split_axis=0, concat_axis=0, tiled=True)
-    return column_call(
-        functools.partial(gradient_kernel, quads, 1.0 / size),
-        [],
-        [folded, amplitude, row_turns, back_again],
-        (rows, size),
-        [work, pltpu.VMEM((n // 2, 8, depth), jnp.float32)],
-        "gradient",
+        vmem_limit_bytes=36 << 20,
+        collective_id=1,
+        has_side_effects=True,
     )
 
 

time: 255 us -> 240 us (0.941)
  blocking collectives: 56.6 us -> 0 us
  Pallas kernels: 135 us -> 168 us
  waiting for transfers between devices: 44.1 us -> 53.6 us
  local copies, waits for them, and re-layouts: 5.57 us -> 2.97 us
    all_to_all x1 -> x0, blocking collectives: 56.6 us -> none  [shared(): lax.all_to_all(fold, parts, split_axis=0, concat_axis=0, tiled=True)]
    pallas_call x3 -> x2, Pallas kernels: 34.9 us -> 80.7 us  [column_call(): pl.pallas_call(kernel, out_shape=jax.ShapeDtypeStruct(out_shape, jnp.floa...]
    pallas_call x1, Pallas kernels: 51.6 us -> 38.5 us  [grid_rows_two(): pl.pallas_call(functools.partial(grid_kernel_two, room), out_shape=jax.Sh...]
    all_to_all x1, waiting for transfers between devices: 0.01 us -> 9.38 us  [shared(): lax.all_to_all(spectrum, parts, split_axis=0, concat_axis=0, tiled=True)]
    unnamed x30 -> x24, local copies, waits for them, and re-layouts: 5.57 us -> 2.97 us
  transfers between devices with their start and end apart: 2 -> 2, of which waited for: 1 -> 2; matrix products, arithmetic and copies ran while one was open for 1% -> 1% of each run, Pallas kernels for 23% -> 19%
where the time goes in v4:
time: 240 us; the launch traced here: 239 us
  Pallas kernels  168 us (70%)
  waiting for transfers between devices  53.6 us (22%)
  starting transfers between devices  10.3 us (4%)
  other arithmetic  3.68 us (2%)
  local copies, waits for them, and re-layouts  2.97 us (1%)
    pallas_call x2, Pallas kernels, column_call(): pl.pallas_call(kernel, out_shape=jax.ShapeDtypeStruct(out_shape, jnp.floa...  80.7 us
    pallas_call x1, Pallas kernels, exchange(): pl.pallas_call(functools.partial(exchange_kernel, nb, ns), out_shape=(jax...  46.4 us
    all_to_all x1, waiting for transfers between devices, shared(): lax.all_to_all(halves, ('base', 'quad'), split_axis=0, concat_axis=0, til...  44.2 us
    pallas_call x1, Pallas kernels, grid_rows_two(): pl.pallas_call(functools.partial(grid_kernel_two, room), out_shape=jax.Sh...  38.5 us
    all_to_all x1, waiting for transfers between devices, shared(): lax.all_to_all(spectrum, parts, split_axis=0, concat_axis=0, tiled=True)  9.38 us
    all_to_all x1, starting transfers between devices, shared(): lax.all_to_all(halves, ('base', 'quad'), split_axis=0, concat_axis=0, til...  6.21 us
  transfers between devices with their start and end apart: 2, of which 2 were waited for; matrix products, arithmetic and copies ran while one was open for 1% of the time, Pallas kernels for 19%

profile of v4, /device:TPU:0, one launch (start us, length us, event | category | flops | bytes accessed | tf_op | source)
XLA Modules:
  0.0 239.1 jit_solution(11704474012814763467)
XLA Ops:
  0.0 2.7 %pack.1.send_ref = f32[4,65,4,128]{3,2,1,0:T(4,128)} custom-call(s32[1,128]{1,0:T(1,128)} %bitcast.8, s32[1,128]{1,0:T(1,128)} %bitcast.9, f32[128,2,128]{2,1,0:T(2,128)} %residual_ref.1, f32[128,2,128]{2,1,0:T(2,128)} %position_ref.1), custom_call_target="tpu_custom_call" | custom-call | tf_op jit(solution)/shard_map/pack/pallas_call | solution.py:530
  2.7 46.4 %exchange.1 = (f32[8,4,65,4,128]{4,3,2,1,0:T(4,128)}, f32[32,128,128]{2,1,0:T(8,128)}) custom-call(f32[4,65,4,128]{3,2,1,0:T(4,128)} %pack.1.send_ref, f32[128,4096]{1,0:T(8,128)} %xi_ref.1, f32[128,4096]{1,0:T(8,128)} %amplitude_ref.1, f32[32,2,128]{2,1,0:T(2,128)} %constant.44.clone.turn_ref.turn_r_ref, bf16[2,512,128]{2,1,0:T(8,128)(2,1)} %constant.45.clone.mat_ref), custom_call_target="tpu_custom_call" | custom-call | flops 30000001024 | bytes 16777216 | tf_op jit(solution)/shard_map/exchange/pallas_call | solution.py:547
  49.2 4.1 %all-to-all-start.1 = ((f32[32,128,128]{2,1,0:T(8,128)}), f32[32,128,128]{2,1,0:T(8,128)S(1)}, u32[]{:S(2)}, u32[]{:S(2)}) async-start(f32[32,128,128]{2,1,0:T(8,128)} %get-tuple-element.8), calls=%async_computation.1 | async-start | bytes 4194304 | tf_op jit(solution)/shard_map/all_to_all | solution.py:1076
  53.2 0.6 pad_add_fusion.info_ref
  53.9 1.5 slice_convert_fusion
  55.3 38.5 %grid_rows_two.1 = f32[16,256,256]{2,1,0:T(8,128)} custom-call(s32[2]{0:T(128)} %pad_add_fusion.info_ref, s32[32,128]{1,0:T(8,128)} %bitcast.7, f32[2,16,2]{2,1,0:T(8,128)} %constant.47.clone.first_ref, f32[2080,4,128]{2,1,0:T(4,128)} %bitcast.10, f32[2,16,4,128]{3,2,1,0:T(4,128)} %constant.48.clone.turn_ref, f32[2,16,2,128]{3,2,1,0:T(2,128)} %constant.49.clone.undo_ref, ...), custom_call_target="tpu_custom_call" | custom-call | flops 20000000000 | bytes 16777216 | tf_op jit(solution)/shard_map/grid_rows_two/pallas_call | solution.py:765
  93.8 0.0 copy-start.4
  93.9 0.0 copy-start.5
  93.9 0.0 copy-start.6
  93.9 0.0 copy-start.8
  93.9 9.4 %all-to-all-done.1.field_ref = f32[32,128,128]{2,1,0:T(8,128)S(1)} async-done(((f32[32,128,128]{2,1,0:T(8,128)}), f32[32,128,128]{2,1,0:T(8,128)S(1)}, u32[]{:S(2)}, u32[]{:S(2)}) %all-to-all-start.1) | async-done | bytes 2097184 | tf_op jit(solution)/shard_map/all_to_all | solution.py:1076
  103.3 6.2 %all-to-all-start = ((f32[16,256,256]{2,1,0:T(8,128)}), f32[16,256,256]{2,1,0:T(8,128)}, u32[]{:S(2)}, u32[]{:S(2)}) async-start(f32[16,256,256]{2,1,0:T(8,128)} %grid_rows_two.1), calls=%async_computation | async-start | bytes 8388608 | tf_op jit(solution)/shard_map/all_to_all | solution.py:1093
  109.5 0.0 copy-done.4
  109.5 0.0 copy-done.5
  109.5 0.0 copy-done.6
  109.5 0.0 copy-done.8
  109.5 0.0 copy-start
  109.5 0.0 copy-start.1
  109.6 0.0 copy-start.2
  109.6 0.0 copy-start.3
  109.6 0.0 copy-start.7
  109.6 6.6 %field.1.sky_ref = f32[32,128,128]{2,1,0:T(8,128)S(1)} custom-call(s32[1]{0:T(128)} %bitcast.6.info_ref, f32[32,2]{1,0:T(8,128)S(1)} %copy-done.8, f32[32,128,128]{2,1,0:T(8,128)S(1)} %all-to-all-done.1.field_ref, f32[128,128]{1,0:T(8,128)S(1)} %copy-done.6, bf16[256,256]{1,0:T(8,128)(2,1)S(1)} %copy-done.5, f32[2,128,128]{2,1,0:T(8,128)S(1)} %copy-done.4), custom_call_target="tpu_custom_call" | custom-call | flops 10000000000 | bytes 16777216 | tf_op jit(solution)/shard_map/field/pallas_call | solution.py:1045
  116.2 0.0 copy-start.9
  116.3 1.3 copy-done.9
  117.6 44.2 %all-to-all-done.whole_ref = f32[16,256,256]{2,1,0:T(8,128)} async-done(((f32[16,256,256]{2,1,0:T(8,128)}), f32[16,256,256]{2,1,0:T(8,128)}, u32[]{:S(2)}, u32[]{:S(2)}) %all-to-all-start) | async-done | bytes 4194336 | tf_op jit(solution)/shard_map/all_to_all | solution.py:1093
  161.8 0.0 copy-done
  161.8 0.0 copy-done.1
  161.8 0.0 copy-done.2
  161.8 0.0 copy-done.3
  161.8 0.0 copy-done.7
  161.8 0.0 copy-start.10
  161.8 1.6 copy-done.10
  163.4 0.0 copy-start.11
  163.4 74.1 %image.1 = f32[128,4096]{1,0:T(8,128)S(1)} custom-call(f32[16,256,256]{2,1,0:T(8,128)} %all-to-all-done.whole_ref, f32[32,128,128]{2,1,0:T(8,128)S(1)} %copy-done.10, f32[256,128]{1,0:T(8,128)S(1)} %copy-done.2, bf16[256,512]{1,0:T(8,128)(2,1)S(1)} %copy-done, bf16[512,128]{1,0:T(8,128)(2,1)S(1)} %copy-done.3, f32[128,128]{1,0:T(8,128)S(1)} %copy-done.6, ...), custom_call_target="tpu_custom_call" | custom-call | flops 10000000000 | bytes 16777216 | tf_op jit(solution)/shard_map/image/pallas_call | solution.py:1045
  237.5 0.0 copy-done.11
  237.5 1.6 mul.7
Async XLA Ops:
  49.2 54.1 %all-to-all-start.1 = ((f32[32,128,128]{2,1,0:T(8,128)}), f32[32,128,128]{2,1,0:T(8,128)S(1)}, u32[]{:S(2)}, u32[]{:S(2)}) async-start(f32[32,128,128]{2,1,0:T(8,128)} %get-tuple-element.8), calls=%async_computation.1 | async-start | bytes 4194304 | tf_op jit(solution)/shard_map/all_to_all | solution.py:1076
  93.8 15.7 %copy-start.4 = (f32[2,128,128]{2,1,0:T(8,128)S(1)}, f32[2,128,128]{2,1,0:T(8,128)}, u32[]{:S(2)}) copy-start(f32[2,128,128]{2,1,0:T(8,128)} %constant.56.clone.slope_ref) | copy-start | bytes 393220
  93.9 15.7 %copy-start.5 = (bf16[256,256]{1,0:T(8,128)(2,1)S(1)}, bf16[256,256]{1,0:T(8,128)(2,1)}, u32[]{:S(2)}) copy-start(bf16[256,256]{1,0:T(8,128)(2,1)} %constant.52.clone.mat_ref) | copy-start | bytes 393220
  93.9 15.6 %copy-start.6 = (f32[128,128]{1,0:T(8,128)S(1)}, f32[128,128]{1,0:T(8,128)}, u32[]{:S(2)}) copy-start(f32[128,128]{1,0:T(8,128)} %constant.51.clone.turn_ref) | copy-start | bytes 196612
  93.9 15.6 %copy-start.8 = (f32[32,2]{1,0:T(8,128)S(1)}, f32[32,2]{1,0:T(8,128)}, u32[]{:S(2)}) copy-start(f32[32,2]{1,0:T(8,128)} %constant.57.clone.bend_ref) | copy-start | bytes 772
  103.3 58.5 %all-to-all-start = ((f32[16,256,256]{2,1,0:T(8,128)}), f32[16,256,256]{2,1,0:T(8,128)}, u32[]{:S(2)}, u32[]{:S(2)}) async-start(f32[16,256,256]{2,1,0:T(8,128)} %grid_rows_two.1), calls=%async_computation | async-start | bytes 8388608 | tf_op jit(solution)/shard_map/all_to_all | solution.py:1093
  109.5 52.2 %copy-start = (bf16[256,512]{1,0:T(8,128)(2,1)S(1)}, bf16[256,512]{1,0:T(8,128)(2,1)}, u32[]{:S(2)}) copy-start(bf16[256,512]{1,0:T(8,128)(2,1)} %constant.55.clone.mat_g_ref) | copy-start | bytes 786436
  109.5 52.2 %copy-start.1 = (bf16[2,256,256]{2,1,0:T(8,128)(2,1)S(1)}, bf16[2,256,256]{2,1,0:T(8,128)(2,1)}, u32[]{:S(2)}) copy-start(bf16[2,256,256]{2,1,0:T(8,128)(2,1)} %constant.46.clone.mat_r_ref) | copy-start | bytes 786436
  109.6 52.2 %copy-start.2 = (f32[256,128]{1,0:T(8,128)S(1)}, f32[256,128]{1,0:T(8,128)}, u32[]{:S(2)}) copy-start(f32[256,128]{1,0:T(8,128)} %constant.54.clone.turn_g_ref) | copy-start | bytes 393220
  109.6 52.2 %copy-start.3 = (bf16[512,128]{1,0:T(8,128)(2,1)S(1)}, bf16[512,128]{1,0:T(8,128)(2,1)}, u32[]{:S(2)}) copy-start(bf16[512,128]{1,0:T(8,128)(2,1)} %constant.53.clone.mat_f_ref) | copy-start | bytes 393220
  109.6 52.2 %copy-start.7 = (f32[32,2,128]{2,1,0:T(2,128)S(1)}, f32[32,2,128]{2,1,0:T(2,128)}, u32[]{:S(2)}) copy-start(f32[32,2,128]{2,1,0:T(2,128)} %constant.44.clone.turn_ref.turn_r_ref) | copy-start | bytes 98308
  116.2 1.3 copy-start.9
  161.8 1.6 copy-start.10
  163.4 74.1 %copy-start.11 = (f32[128,4096]{1,0:T(8,128)S(1)}, f32[128,4096]{1,0:T(8,128)}, u32[]{:S(2)}) copy-start(f32[128,4096]{1,0:T(8,128)} %amplitude_ref.1) | copy-start | bytes 6291460

commit v5 on v4

--- a/solution.py
+++ b/solution.py
@@ -330,56 +330,56 @@
     out_ref[0] = through(left([0]), mat_ref, 1)
 
 
-def exchange_kernel(nb, ns, send_ref, xi_ref, amplitude_ref, turn_ref, mat_ref, out_ref, spectrum_ref, work_ref, made_ref, rows_ref, rows_sem, bsend, brecv, usend, dsend, lrecv, hrecv, psend, precv, lsem):
-    quads = ns // 2
-    nz = ns // 2
-    base = lax.axis_index("base")
-    slab = lax.axis_index("half") * quads + lax.axis_index("quad")
-    z = slab // 2
-    core = slab % 2
-
-    def at(b, s):
-        return (b, s // quads, s % quads)
-
-    def copy(source, target, here, there, device):
+def seats(base, quad):
+    return base // 2, base % 2, quad // 2, quad % 2
+
+
+def group_of(base, quad):
+    y, x, low, core = seats(base, quad)
+    return 2 * x + low, 2 * y + core
+
+
+def exchange_kernel(send_ref, xi_ref, amplitude_ref, turn_ref, mat_ref, out_ref, spectrum_ref, work_ref, made_ref, rows_ref, rows_sem, bsend, brecv, zsend, zrecv, ysend, yrecv, csend, crecv, lsem):
+    nb = send_ref.shape[0]
+    quads = lax.axis_size("quad")
+    half = lax.axis_index("half")
+    y, x, low, core = seats(lax.axis_index("base"), lax.axis_index("quad"))
+    group = 2 * x + low
+
+    def at(y, group, half, core):
+        return (2 * y + group // 2, half, group % 2 * 2 + core)
+
+    def block(y, half, core, k):
+        return out_ref.at[(2 * y + half) * 2 + core, (group - k + nb) % nb]
+
+    def copy(part, here, there, device):
         return pltpu.make_async_remote_copy(
-            src_ref=source, dst_ref=target, send_sem=here, recv_sem=there, device_id=device, device_id_type=MESH
+            src_ref=part, dst_ref=part, send_sem=here, recv_sem=there, device_id=device, device_id_type=MESH
         )
 
-    def crossing(k):
-        other = (base + k) % nb
-        return copy(send_ref.at[other], out_ref.at[slab, base], bsend.at[k], brecv.at[k], at(other, slab))
-
-    def arriving(k):
-        from_base = (base - k + nb) % nb
-        return copy(send_ref.at[base], out_ref.at[slab, from_base], bsend.at[k], brecv.at[k], at(from_base, slab))
-
-    def block(origin, k):
-        return out_ref.at[2 * origin + core, (base - k + nb) % nb]
-
-    def upward(s, k):
-        part = block(z - s, k)
-        return copy(part, part, usend.at[s, k], lrecv.at[s + 1, k], at(base, slab + 2))
-
-    def downward(s, k):
-        part = block(z + s, k)
-        return copy(part, part, dsend.at[s, k], hrecv.at[s + 1, k], at(base, slab - 2))
-
-    def from_below(s, k):
-        part = block(z - s, k)
-        return copy(part, part, usend.at[s, k], lrecv.at[s, k], at(base, slab - 2))
-
-    def from_above(s, k):
-        part = block(z + s, k)
-        return copy(part, part, dsend.at[s, k], hrecv.at[s, k], at(base, slab + 2))
-
-    def across(origin, k):
-        part = block(origin, k)
-        return copy(part, part, psend.at[origin, k], precv.at[origin, k], at(base, slab + 1 - 2 * core))
-
-    def from_partner(origin, k):
-        part = out_ref.at[2 * origin + 1 - core, (base - k + nb) % nb]
-        return copy(part, part, psend.at[origin, k], precv.at[origin, k], at(base, slab + 1 - 2 * core))
+    def moved(target, source, k):
+        return pltpu.make_async_remote_copy(
+            src_ref=send_ref.at[target],
+            dst_ref=out_ref.at[(2 * y + half) * 2 + core, source],
+            send_sem=bsend.at[k],
+            recv_sem=brecv.at[k],
+            device_id=at(y, target, half, core),
+            device_id_type=MESH,
+        )
+
+    far, beside, partner = at(y, group, 1 - half, core), at(1 - y, group, half, core), at(y, group, half, 1 - core)
+
+    def along_z(own, k):
+        return copy(block(y, half if own else 1 - half, core, k), zsend.at[k], zrecv.at[k], far)
+
+    def along_y(own, kind, k):
+        place = half if kind == 0 else 1 - half
+        return copy(block(y if own else 1 - y, place, core, k), ysend.at[kind, k], yrecv.at[kind, k], beside)
+
+    def over(own, kind, k):
+        row = y if kind < 2 else 1 - y
+        place = half if kind % 2 == 0 else 1 - half
+        return copy(block(row, place, core if own else 1 - core, k), csend.at[kind, k], crecv.at[kind, k], partner)
 
     fetches = [
         pltpu.make_async_copy(source, rows_ref.at[k], rows_sem.at[k]) for k, source in enumerate((xi_ref, amplitude_ref))
@@ -388,83 +388,48 @@
     for fetch in fetches:
         fetch.start()
     barrier = pltpu.get_barrier_semaphore()
+    peers = [at(y, (group + k) % nb, half, core) for k in range(1, nb)] + [far, beside, partner]
+    for peer in peers:
+        pl.semaphore_signal(barrier, inc=1, device_id=peer, device_id_type=MESH)
+    pl.semaphore_wait(barrier, len(peers))
+
+    own = pltpu.make_async_copy(send_ref.at[group], block(y, half, core, 0), lsem)
+    own.start()
     for k in range(1, nb):
-        pl.semaphore_signal(barrier, inc=1, device_id=at((base + k) % nb, slab), device_id_type=MESH)
-    pl.semaphore_signal(barrier, inc=1, device_id=at(base, slab + 1 - 2 * core), device_id_type=MESH)
-
-    @pl.when(z < nz - 1)
-    def _():
-        pl.semaphore_signal(barrier, inc=1, device_id=at(base, slab + 2), device_id_type=MESH)
-
-    @pl.when(z > 0)
-    def _():
-        pl.semaphore_signal(barrier, inc=1, device_id=at(base, slab - 2), device_id_type=MESH)
-
-    pl.semaphore_wait(barrier, nb + jnp.where(z < nz - 1, 1, 0) + jnp.where(z > 0, 1, 0))
-
-    for k in range(1, nb):
-        crossing(k).start()
-    own = pltpu.make_async_copy(send_ref.at[base], out_ref.at[slab, base], lsem)
-    own.start()
-
-    def pass_on(s, k, ascending, descending):
-        if ascending:
-            @pl.when((z - s >= 0) & (z < nz - 1))
-            def _():
-                upward(s, k).start()
-
-        if descending:
-            @pl.when((z + s < nz) & (z > 0))
-            def _():
-                downward(s, k).start()
-
+        moved((group + k) % nb, group, k).start()
     for k in range(nb):
         if k == 0:
             own.wait()
         else:
-            arriving(k).wait_recv()
-        pass_on(0, k, True, True)
-        across(z, k).start()
+            moved((group - k + nb) % nb, (group - k + nb) % nb, k).wait_recv()
+        along_z(True, k).start()
+        along_y(True, 0, k).start()
+        over(True, 0, k).start()
         if k == 0:
             for fetch in fetches:
                 fetch.wait()
             transform_rows(quads, rows_ref.at[0], rows_ref.at[1], turn_ref, mat_ref, made_ref, work_ref)
             ready.start()
-    for s in range(1, nz):
+    for k in range(nb):
+        along_z(False, k).wait_recv()
+        along_y(True, 1, k).start()
+        over(True, 1, k).start()
+    for kind in range(2):
         for k in range(nb):
-            @pl.when(z - s >= 0)
-            def _():
-                from_below(s, k).wait_recv()
-                if s < nz - 1:
-                    pass_on(s, k, True, False)
-                across(z - s, k).start()
-
-            @pl.when(z + s < nz)
-            def _():
-                from_above(s, k).wait_recv()
-                if s < nz - 1:
-                    pass_on(s, k, False, True)
-                across(z + s, k).start()
-
+            along_y(False, kind, k).wait_recv()
+            over(True, 2 + kind, k).start()
     ready.wait()
-    for origin in range(nz):
+    for kind in range(4):
         for k in range(nb):
-            from_partner(origin, k).wait_recv()
-    for k in range(1, nb):
-        crossing(k).wait_send()
-    for s in range(nz - 1):
-        for k in range(nb):
-            @pl.when((z - s >= 0) & (z < nz - 1))
-            def _():
-                upward(s, k).wait_send()
-
-            @pl.when((z + s < nz) & (z > 0))
-            def _():
-                downward(s, k).wait_send()
-
-    for origin in range(nz):
-        for k in range(nb):
-            across(origin, k).wait_send()
+            over(False, kind, k).wait_recv()
+    for k in range(nb):
+        if k:
+            moved((group + k) % nb, group, k).wait_send()
+        along_z(True, k).wait_send()
+        for kind in range(2):
+            along_y(True, kind, k).wait_send()
+        for kind in range(4):
+            over(True, kind, k).wait_send()
 
 
 def pack_kernel(ns, tiles, room, owner_ref, local_ref, residual_ref, position_ref, out_ref):
@@ -539,13 +504,12 @@
 
 def exchange(sent, ns, xi, amplitude, turns, mats):
     nb = sent.shape[0]
-    nz = ns // 2
     rows, n = xi.shape[0], turns.shape[0]
     dma = pltpu.SemaphoreType.DMA
     vmem = pl.BlockSpec(memory_space=pltpu.VMEM)
     hbm = pl.BlockSpec(memory_space=pltpu.HBM)
     return pl.pallas_call(
-        functools.partial(exchange_kernel, nb, ns),
+        exchange_kernel,
         out_shape=(
             jax.ShapeDtypeStruct((ns,) + sent.shape, jnp.float32),
             jax.ShapeDtypeStruct((n, rows, TILE), jnp.float32),
@@ -556,8 +520,7 @@
             pltpu.VMEM((n, 2, rows, TILE), jnp.float32),
             pltpu.VMEM((n, rows, TILE), jnp.float32),
             pltpu.VMEM((2,) + xi.shape, jnp.float32), dma((3,)),
-            dma((nb,)), dma((nb,)), dma((nz, nb)), dma((nz, nb)), dma((nz, nb)), dma((nz, nb)),
-            dma((nz, nb)), dma((nz, nb)), dma,
+            dma((nb,)), dma((nb,)), dma((nb,)), dma((nb,)), dma((2, nb)), dma((2, nb)), dma((4, nb)), dma((4, nb)), dma,
         ],
         compiler_params=pltpu.CompilerParams(collective_id=0, has_side_effects=True, vmem_limit_bytes=60 << 20),
         cost_estimate=pl.CostEstimate(flops=3 * 10**10, bytes_accessed=16 * 2**20, transcendentals=0),
@@ -881,6 +844,10 @@
         return carry
 
     lax.fori_loop(1, n, greet, 0)
+    origins = [0] * (n // 2)
+    for k in range(n // 2):
+        group, member = group_of(k // quads, k % quads)
+        origins[group * quads + member] = k
     fetch = pltpu.make_async_copy(sky_ref, held_ref, held_sem)
     fetch.start()
     depth = n // 2
@@ -891,7 +858,7 @@
         for e in range(2):
             x = []
             for a in range(depth):
-                value = whole_ref[a, spot, :TILE], whole_ref[a, spot, TILE:]
+                value = whole_ref[origins[a], spot, :TILE], whole_ref[origins[a], spot, TILE:]
                 x.append(turn(value, 2 * math.pi * a / n) if e * a else value)
             for v, value in enumerate(sixteen(x)):
                 u = 2 * v + e
@@ -1077,7 +1044,7 @@
 
     sources = n_slab * n_base
     codes = got[:, :, room, 0, :].reshape(sources, TILE).astype(jnp.int32)
-    info = jnp.stack([quad, parity]).astype(jnp.int32)
+    info = jnp.stack([group_of(base, quad)[1], parity]).astype(jnp.int32)
 
     turns, firsts, undos, weights = grid_row_weights(n, size)
     halves = grid_rows_two(
@@ -1125,7 +1092,7 @@
 def solution(mesh):
     n_base, n_slab = mesh.shape["base"], mesh.shape["slab"]
     body, axes = general, both
-    if n_slab == 2 * n_base and 2 * n_base * n_slab == G // TILE:
+    if n_base == 4 and n_slab == 2 * n_base and 2 * n_base * n_slab == G // TILE:
         body, axes = shared, parts
         mesh = jax.sharding.Mesh(mesh.devices.reshape(n_base, 2, n_slab // 2), parts)
     placed = (

time: 240 us -> 235 us (0.979)
  waiting for transfers between devices: 53.6 us -> 49.4 us
    pallas_call x1, Pallas kernels: 46.4 us -> 40.6 us  [exchange(): pl.pallas_call(exchange_kernel, out_shape=(jax.ShapeDtypeStruct((ns,) + s...]
    all_to_all x1, waiting for transfers between devices: 9.38 us -> 5.16 us  [shared(): lax.all_to_all(spectrum, parts, split_axis=0, concat_axis=0, tiled=True)]
    pallas_call x1, Pallas kernels: 38.5 us -> 42.7 us  [grid_rows_two(): pl.pallas_call(functools.partial(grid_kernel_two, room), out_shape=jax.Sh...]
  transfers between devices with their start and end apart: 2 -> 2, of which waited for: 2 -> 2; matrix products, arithmetic and copies ran while one was open for 1% -> 1% of each run, Pallas kernels for 19% -> 21%
where the time goes in v5:
time: 235 us; the launch traced here: 233 us
  Pallas kernels  167 us (71%)
  waiting for transfers between devices  49.4 us (21%)
  starting transfers between devices  10.4 us (4%)
  other arithmetic  3.7 us (2%)
  local copies, waits for them, and re-layouts  2.97 us (1%)
    pallas_call x2, Pallas kernels, column_call(): pl.pallas_call(kernel, out_shape=jax.ShapeDtypeStruct(out_shape, jnp.floa...  80.7 us
    all_to_all x1, waiting for transfers between devices, shared(): lax.all_to_all(halves, ('base', 'quad'), split_axis=0, concat_axis=0, til...  44.2 us
    pallas_call x1, Pallas kernels, grid_rows_two(): pl.pallas_call(functools.partial(grid_kernel_two, room), out_shape=jax.Sh...  42.7 us
    pallas_call x1, Pallas kernels, exchange(): pl.pallas_call(exchange_kernel, out_shape=(jax.ShapeDtypeStruct((ns,) + s...  40.6 us
    all_to_all x1, starting transfers between devices, shared(): lax.all_to_all(halves, ('base', 'quad'), split_axis=0, concat_axis=0, til...  7.64 us
    all_to_all x1, waiting for transfers between devices, shared(): lax.all_to_all(spectrum, parts, split_axis=0, concat_axis=0, tiled=True)  5.16 us
  transfers between devices with their start and end apart: 2, of which 2 were waited for; matrix products, arithmetic and copies ran while one was open for 1% of the time, Pallas kernels for 21%

profile of v5, /device:TPU:0, one launch (start us, length us, event | category | flops | bytes accessed | tf_op | source)
XLA Modules:
  0.0 233.4 jit_solution(17337688627886538795)
XLA Ops:
  0.0 2.7 %pack.1.send_ref = f32[4,65,4,128]{3,2,1,0:T(4,128)} custom-call(s32[1,128]{1,0:T(1,128)} %bitcast.8, s32[1,128]{1,0:T(1,128)} %bitcast.9, f32[128,2,128]{2,1,0:T(2,128)} %residual_ref.1, f32[128,2,128]{2,1,0:T(2,128)} %position_ref.1), custom_call_target="tpu_custom_call" | custom-call | tf_op jit(solution)/shard_map/pack/pallas_call | solution.py:495
  2.7 40.6 %exchange.1 = (f32[8,4,65,4,128]{4,3,2,1,0:T(4,128)}, f32[32,128,128]{2,1,0:T(8,128)}) custom-call(f32[4,65,4,128]{3,2,1,0:T(4,128)} %pack.1.send_ref, f32[128,4096]{1,0:T(8,128)} %xi_ref.1, f32[128,4096]{1,0:T(8,128)} %amplitude_ref.1, f32[32,2,128]{2,1,0:T(2,128)} %constant.66.clone.turn_ref.turn_r_ref, bf16[2,512,128]{2,1,0:T(8,128)(2,1)} %constant.67.clone.mat_ref), custom_call_target="tpu_custom_call" | custom-call | flops 30000001024 | bytes 16777216 | tf_op jit(solution)/shard_map/exchange/pallas_call | solution.py:511
  43.3 2.7 %all-to-all-start.1 = ((f32[32,128,128]{2,1,0:T(8,128)}), f32[32,128,128]{2,1,0:T(8,128)S(1)}, u32[]{:S(2)}, u32[]{:S(2)}) async-start(f32[32,128,128]{2,1,0:T(8,128)} %get-tuple-element.8), calls=%async_computation.1 | async-start | bytes 4194304 | tf_op jit(solution)/shard_map/all_to_all | solution.py:1043
  46.1 0.7 pad_add_fusion.info_ref
  46.7 1.5 slice_convert_fusion
  48.2 42.7 %grid_rows_two.1 = f32[16,256,256]{2,1,0:T(8,128)} custom-call(s32[2]{0:T(128)} %pad_add_fusion.info_ref, s32[32,128]{1,0:T(8,128)} %bitcast.7, f32[2,16,2]{2,1,0:T(8,128)} %constant.69.clone.first_ref, f32[2080,4,128]{2,1,0:T(4,128)} %bitcast.10, f32[2,16,4,128]{3,2,1,0:T(4,128)} %constant.70.clone.turn_ref, f32[2,16,2,128]{3,2,1,0:T(2,128)} %constant.71.clone.undo_ref, ...), custom_call_target="tpu_custom_call" | custom-call | flops 20000000000 | bytes 16777216 | tf_op jit(solution)/shard_map/grid_rows_two/pallas_call | solution.py:728
  90.9 0.0 copy-start.4
  90.9 0.0 copy-start.5
  90.9 0.0 copy-start.6
  90.9 0.0 copy-start.8
  90.9 5.2 %all-to-all-done.1.field_ref = f32[32,128,128]{2,1,0:T(8,128)S(1)} async-done(((f32[32,128,128]{2,1,0:T(8,128)}), f32[32,128,128]{2,1,0:T(8,128)S(1)}, u32[]{:S(2)}, u32[]{:S(2)}) %all-to-all-start.1) | async-done | bytes 2097184 | tf_op jit(solution)/shard_map/all_to_all | solution.py:1043
  96.1 7.6 %all-to-all-start = ((f32[16,256,256]{2,1,0:T(8,128)}), f32[16,256,256]{2,1,0:T(8,128)}, u32[]{:S(2)}, u32[]{:S(2)}) async-start(f32[16,256,256]{2,1,0:T(8,128)} %grid_rows_two.1), calls=%async_computation | async-start | bytes 8388608 | tf_op jit(solution)/shard_map/all_to_all | solution.py:1060
  103.7 0.0 copy-done.4
  103.8 0.0 copy-done.5
  103.8 0.0 copy-done.6
  103.8 0.0 copy-done.8
  103.8 0.0 copy-start
  103.8 0.0 copy-start.1
  103.8 0.0 copy-start.2
  103.8 0.0 copy-start.3
  103.8 0.0 copy-start.7
  103.8 6.6 %field.1.sky_ref = f32[32,128,128]{2,1,0:T(8,128)S(1)} custom-call(s32[1]{0:T(128)} %bitcast.6.info_ref, f32[32,2]{1,0:T(8,128)S(1)} %copy-done.8, f32[32,128,128]{2,1,0:T(8,128)S(1)} %all-to-all-done.1.field_ref, f32[128,128]{1,0:T(8,128)S(1)} %copy-done.6, bf16[256,256]{1,0:T(8,128)(2,1)S(1)} %copy-done.5, f32[2,128,128]{2,1,0:T(8,128)S(1)} %copy-done.4), custom_call_target="tpu_custom_call" | custom-call | flops 10000000000 | bytes 16777216 | tf_op jit(solution)/shard_map/field/pallas_call | solution.py:1012
  110.5 0.0 copy-start.9
  110.5 1.3 copy-done.9
  111.8 44.2 %all-to-all-done.whole_ref = f32[16,256,256]{2,1,0:T(8,128)} async-done(((f32[16,256,256]{2,1,0:T(8,128)}), f32[16,256,256]{2,1,0:T(8,128)}, u32[]{:S(2)}, u32[]{:S(2)}) %all-to-all-start) | async-done | bytes 4194336 | tf_op jit(solution)/shard_map/all_to_all | solution.py:1060
  156.0 0.0 copy-done
  156.0 0.0 copy-done.1
  156.0 0.0 copy-done.2
  156.0 0.0 copy-done.3
  156.0 0.0 copy-done.7
  156.1 0.0 copy-start.10
  156.1 1.6 copy-done.10
  157.7 0.0 copy-start.11
  157.7 74.1 %image.1 = f32[128,4096]{1,0:T(8,128)S(1)} custom-call(f32[16,256,256]{2,1,0:T(8,128)} %all-to-all-done.whole_ref, f32[32,128,128]{2,1,0:T(8,128)S(1)} %copy-done.10, f32[256,128]{1,0:T(8,128)S(1)} %copy-done.2, bf16[256,512]{1,0:T(8,128)(2,1)S(1)} %copy-done, bf16[512,128]{1,0:T(8,128)(2,1)S(1)} %copy-done.3, f32[128,128]{1,0:T(8,128)S(1)} %copy-done.6, ...), custom_call_target="tpu_custom_call" | custom-call | flops 10000000000 | bytes 16777216 | tf_op jit(solution)/shard_map/image/pallas_call | solution.py:1012
  231.8 0.0 copy-done.11
  231.8 1.6 mul.15
Async XLA Ops:
  43.3 52.8 %all-to-all-start.1 = ((f32[32,128,128]{2,1,0:T(8,128)}), f32[32,128,128]{2,1,0:T(8,128)S(1)}, u32[]{:S(2)}, u32[]{:S(2)}) async-start(f32[32,128,128]{2,1,0:T(8,128)} %get-tuple-element.8), calls=%async_computation.1 | async-start | bytes 4194304 | tf_op jit(solution)/shard_map/all_to_all | solution.py:1043
  90.9 12.9 %copy-start.4 = (f32[2,128,128]{2,1,0:T(8,128)S(1)}, f32[2,128,128]{2,1,0:T(8,128)}, u32[]{:S(2)}) copy-start(f32[2,128,128]{2,1,0:T(8,128)} %constant.78.clone.slope_ref) | copy-start | bytes 393220
  90.9 12.9 %copy-start.5 = (bf16[256,256]{1,0:T(8,128)(2,1)S(1)}, bf16[256,256]{1,0:T(8,128)(2,1)}, u32[]{:S(2)}) copy-start(bf16[256,256]{1,0:T(8,128)(2,1)} %constant.74.clone.mat_ref) | copy-start | bytes 393220
  90.9 12.9 %copy-start.6 = (f32[128,128]{1,0:T(8,128)S(1)}, f32[128,128]{1,0:T(8,128)}, u32[]{:S(2)}) copy-start(f32[128,128]{1,0:T(8,128)} %constant.73.clone.turn_ref) | copy-start | bytes 196612
  90.9 12.9 %copy-start.8 = (f32[32,2]{1,0:T(8,128)S(1)}, f32[32,2]{1,0:T(8,128)}, u32[]{:S(2)}) copy-start(f32[32,2]{1,0:T(8,128)} %constant.79.clone.bend_ref) | copy-start | bytes 772
  96.1 60.0 %all-to-all-start = ((f32[16,256,256]{2,1,0:T(8,128)}), f32[16,256,256]{2,1,0:T(8,128)}, u32[]{:S(2)}, u32[]{:S(2)}) async-start(f32[16,256,256]{2,1,0:T(8,128)} %grid_rows_two.1), calls=%async_computation | async-start | bytes 8388608 | tf_op jit(solution)/shard_map/all_to_all | solution.py:1060
  103.8 52.3 %copy-start = (bf16[256,512]{1,0:T(8,128)(2,1)S(1)}, bf16[256,512]{1,0:T(8,128)(2,1)}, u32[]{:S(2)}) copy-start(bf16[256,512]{1,0:T(8,128)(2,1)} %constant.77.clone.mat_g_ref) | copy-start | bytes 786436
  103.8 52.2 %copy-start.1 = (bf16[2,256,256]{2,1,0:T(8,128)(2,1)S(1)}, bf16[2,256,256]{2,1,0:T(8,128)(2,1)}, u32[]{:S(2)}) copy-start(bf16[2,256,256]{2,1,0:T(8,128)(2,1)} %constant.68.clone.mat_r_ref) | copy-start | bytes 786436
  103.8 52.2 %copy-start.2 = (f32[256,128]{1,0:T(8,128)S(1)}, f32[256,128]{1,0:T(8,128)}, u32[]{:S(2)}) copy-start(f32[256,128]{1,0:T(8,128)} %constant.76.clone.turn_g_ref) | copy-start | bytes 393220
  103.8 52.2 %copy-start.3 = (bf16[512,128]{1,0:T(8,128)(2,1)S(1)}, bf16[512,128]{1,0:T(8,128)(2,1)}, u32[]{:S(2)}) copy-start(bf16[512,128]{1,0:T(8,128)(2,1)} %constant.75.clone.mat_f_ref) | copy-start | bytes 393220
  103.8 52.2 %copy-start.7 = (f32[32,2,128]{2,1,0:T(2,128)S(1)}, f32[32,2,128]{2,1,0:T(2,128)}, u32[]{:S(2)}) copy-start(f32[32,2,128]{2,1,0:T(2,128)} %constant.66.clone.turn_ref.turn_r_ref) | copy-start | bytes 98308
  110.5 1.3 copy-start.9
  156.1 1.6 copy-start.10
  157.7 74.1 %copy-start.11 = (f32[128,4096]{1,0:T(8,128)S(1)}, f32[128,4096]{1,0:T(8,128)}, u32[]{:S(2)}) copy-start(f32[128,4096]{1,0:T(8,128)} %amplitude_ref.1) | copy-start | bytes 6291460

commit v6 on v5

--- a/solution.py
+++ b/solution.py
@@ -234,7 +234,7 @@
 
 MESH = pl.DeviceIdType.MESH
 parts = ("base", "half", "quad")
-LANES = 4
+LANES = 6
 
 
 def two_parts(x):
@@ -456,7 +456,7 @@
     tile_col = jnp.where(flip > 0.5, tiles - 1 - tile_col, tile_col)
     line, within = divided(tile_row, ns)
     key = divided(tile_row, 2)[0]
-    code = within * tiles + tile_col
+    code = divided(within, 2)[1] * tiles + tile_col
     keys = ns // 2
     line_down, key_down, flip_down = column(line), column(key), column(flip)
     before = (line_down == line) & ((key_down < key) | ((key_down == key) & (down < across)))
@@ -528,9 +528,9 @@
     )(sent, xi, amplitude, turns, mats)
 
 
-def grid_kernel_two(room, info_ref, codes_ref, first_ref, data_hbm_ref, turn_ref, undo_ref, weight_hbm_ref, away_ref, grid_ref, left_ref, right_ref, out_ref, data_ref, weight_ref, list_ref, sems):
-    quad = info_ref[0]
-    parity = info_ref[1]
+def grid_kernel_two(room, codes_ref, first_ref, data_hbm_ref, turn_ref, undo_ref, weight_hbm_ref, away_ref, grid_ref, left_ref, right_ref, out_ref, data_ref, weight_ref, list_ref, sems):
+    quad = group_of(lax.axis_index("base"), lax.axis_index("quad"))[1]
+    parity = lax.axis_index("half")
     data = pltpu.make_async_copy(data_hbm_ref, data_ref, sems.at[out_ref.shape[0]])
     weight = pltpu.make_async_copy(weight_hbm_ref, weight_ref, sems.at[out_ref.shape[0] + 1])
     data.start()
@@ -567,7 +567,7 @@
 
     def place(k):
         packed = list_ref[k]
-        return packed % 64, packed // 64
+        return packed & (2 * half - 1), lax.shift_right_logical(packed, half.bit_length())
 
     def prepare(k, lane, count):
         col, rest = place(k)
@@ -604,12 +604,17 @@
             grid_ref[1, col, spot, :] += made[lane][:, TILE:]
         return carry
 
+    per = 4 * half
+
     def gather(source, filled):
         start = codes_ref[source, room + quad]
         stop = codes_ref[source, room + quad + 1]
 
+        shift = filled - start
+        first = source * ((room + 1) * per)
+
         def entry(i, carry):
-            list_ref[filled + i - start] = (source * (room + 1) + i) * TILE + codes_ref[source, i] % TILE
+            list_ref[shift + i] = first + i * per + codes_ref[source, i]
             return carry
 
         lax.fori_loop(start, stop, entry, 0)
@@ -719,7 +724,7 @@
     return turns, firsts, undos, np.stack(weights)
 
 
-def grid_rows_two(room, info, codes, first, data, turns, undos, weights):
+def grid_rows_two(room, codes, first, data, turns, undos, weights):
     depth = turns.shape[1]
     rows = 2 * TILE
     smem = pl.BlockSpec(memory_space=pltpu.SMEM)
@@ -728,7 +733,7 @@
     return pl.pallas_call(
         functools.partial(grid_kernel_two, room),
         out_shape=jax.ShapeDtypeStruct((depth, rows, 2 * TILE), jnp.float32),
-        in_specs=[smem, smem, smem, hbm, vmem, vmem, hbm],
+        in_specs=[smem, smem, hbm, vmem, vmem, hbm],
         out_specs=hbm,
         scratch_shapes=[
             pltpu.VMEM((2, 2 * depth, rows, TILE), jnp.float32),
@@ -743,7 +748,7 @@
         compiler_params=pltpu.CompilerParams(vmem_limit_bytes=60 << 20),
         cost_estimate=pl.CostEstimate(flops=2 * 10**10, bytes_accessed=16 * 2**20, transcendentals=0),
         name="grid_rows_two",
-    )(info, codes, first, data, turns, undos, weights)
+    )(codes, first, data, turns, undos, weights)
 
 
 def minus(x):
@@ -1044,12 +1049,10 @@
 
     sources = n_slab * n_base
     codes = got[:, :, room, 0, :].reshape(sources, TILE).astype(jnp.int32)
-    info = jnp.stack([group_of(base, quad)[1], parity]).astype(jnp.int32)
 
     turns, firsts, undos, weights = grid_row_weights(n, size)
     halves = grid_rows_two(
         room,
-        info,
         codes,
         jnp.asarray(firsts),
         got.reshape(sources * (room + 1), 4, TILE),

time: 235 us -> 230 us (0.979)
  waiting for transfers between devices: 49.4 us -> 52.7 us
  starting transfers between devices: 10.4 us -> 7.28 us
  Pallas kernels: 167 us -> 164 us
    all_to_all x1, waiting for transfers between devices: 5.16 us -> 8.63 us  [shared(): lax.all_to_all(spectrum, parts, split_axis=0, concat_axis=0, tiled=True)]
    all_to_all x1, starting transfers between devices: 7.64 us -> 4.54 us  [shared(): lax.all_to_all(halves, ('base', 'quad'), split_axis=0, concat_axis=0, til...]
    pallas_call x1, Pallas kernels: 42.7 us -> 39.9 us  [grid_rows_two(): pl.pallas_call(functools.partial(grid_kernel_two, room), out_shape=jax.Sh...]
  transfers between devices with their start and end apart: 2 -> 2, of which waited for: 2 -> 2; matrix products, arithmetic and copies ran while one was open for 1% -> 1% of each run, Pallas kernels for 21% -> 20%
where the time goes in v6:
time: 230 us
  Pallas kernels  164 us (71%)
  waiting for transfers between devices  52.7 us (23%)
  starting transfers between devices  7.28 us (3%)
  other arithmetic  3.04 us (1%)
  local copies, waits for them, and re-layouts  2.97 us (1%)
    pallas_call x2, Pallas kernels, column_call(): pl.pallas_call(kernel, out_shape=jax.ShapeDtypeStruct(out_shape, jnp.floa...  80.6 us
    all_to_all x1, waiting for transfers between devices, shared(): lax.all_to_all(halves, ('base', 'quad'), split_axis=0, concat_axis=0, til...  44 us
    pallas_call x1, Pallas kernels, exchange(): pl.pallas_call(exchange_kernel, out_shape=(jax.ShapeDtypeStruct((ns,) + s...  40.6 us
    pallas_call x1, Pallas kernels, grid_rows_two(): pl.pallas_call(functools.partial(grid_kernel_two, room), out_shape=jax.Sh...  39.9 us
    all_to_all x1, waiting for transfers between devices, shared(): lax.all_to_all(spectrum, parts, split_axis=0, concat_axis=0, tiled=True)  8.63 us
  transfers between devices with their start and end apart: 2, of which 2 were waited for; matrix products, arithmetic and copies ran while one was open for 1% of the time, Pallas kernels for 20%

profile of v6, /device:TPU:0, one launch (start us, length us, event | category | flops | bytes accessed | tf_op | source)
XLA Modules:
  0.0 229.9 jit_solution(16864347424205347274)
XLA Ops:
  0.0 2.7 %pack.1.send_ref = f32[4,65,4,128]{3,2,1,0:T(4,128)} custom-call(s32[1,128]{1,0:T(1,128)} %bitcast.6, s32[1,128]{1,0:T(1,128)} %bitcast.7, f32[128,2,128]{2,1,0:T(2,128)} %residual_ref.1, f32[128,2,128]{2,1,0:T(2,128)} %position_ref.1), custom_call_target="tpu_custom_call" | custom-call | tf_op jit(solution)/shard_map/pack/pallas_call | solution.py:495
  2.7 40.6 %exchange.1 = (f32[8,4,65,4,128]{4,3,2,1,0:T(4,128)}, f32[32,128,128]{2,1,0:T(8,128)}) custom-call(f32[4,65,4,128]{3,2,1,0:T(4,128)} %pack.1.send_ref, f32[128,4096]{1,0:T(8,128)} %xi_ref.1, f32[128,4096]{1,0:T(8,128)} %amplitude_ref.1, f32[32,2,128]{2,1,0:T(2,128)} %constant.44.clone.turn_ref.turn_r_ref, bf16[2,512,128]{2,1,0:T(8,128)(2,1)} %constant.45.clone.mat_ref), custom_call_target="tpu_custom_call" | custom-call | flops 30000001024 | bytes 16777216 | tf_op jit(solution)/shard_map/exchange/pallas_call | solution.py:511
  43.3 2.7 %all-to-all-start.1 = ((f32[32,128,128]{2,1,0:T(8,128)}), f32[32,128,128]{2,1,0:T(8,128)S(1)}, u32[]{:S(2)}, u32[]{:S(2)}) async-start(f32[32,128,128]{2,1,0:T(8,128)} %get-tuple-element.8), calls=%async_computation.1 | async-start | bytes 4194304 | tf_op jit(solution)/shard_map/all_to_all | solution.py:1048
  46.1 1.5 slice_convert_fusion
  47.5 39.9 %grid_rows_two.1 = f32[16,256,256]{2,1,0:T(8,128)} custom-call(s32[32,128]{1,0:T(8,128)} %bitcast.5, f32[2,16,2]{2,1,0:T(8,128)} %constant.47.clone.first_ref, f32[2080,4,128]{2,1,0:T(4,128)} %bitcast.8, f32[2,16,4,128]{3,2,1,0:T(4,128)} %constant.48.clone.turn_ref, f32[2,16,2,128]{3,2,1,0:T(2,128)} %constant.49.clone.undo_ref, ...), custom_call_target="tpu_custom_call" | custom-call | flops 20000000000 | bytes 16777216 | tf_op jit(solution)/shard_map/grid_rows_two/pallas_call | solution.py:733
  87.4 0.0 copy-start.4
  87.4 0.0 copy-start.5
  87.4 0.0 copy-start.6
  87.4 0.0 copy-start.8
  87.4 8.6 %all-to-all-done.1.field_ref = f32[32,128,128]{2,1,0:T(8,128)S(1)} async-done(((f32[32,128,128]{2,1,0:T(8,128)}), f32[32,128,128]{2,1,0:T(8,128)S(1)}, u32[]{:S(2)}, u32[]{:S(2)}) %all-to-all-start.1) | async-done | bytes 2097184 | tf_op jit(solution)/shard_map/all_to_all | solution.py:1048
  96.1 4.5 %all-to-all-start = ((f32[16,256,256]{2,1,0:T(8,128)}), f32[16,256,256]{2,1,0:T(8,128)}, u32[]{:S(2)}, u32[]{:S(2)}) async-start(f32[16,256,256]{2,1,0:T(8,128)} %grid_rows_two.1), calls=%async_computation | async-start | bytes 8388608 | tf_op jit(solution)/shard_map/all_to_all | solution.py:1063
  100.6 0.0 copy-done.4
  100.6 0.0 copy-done.5
  100.7 0.0 copy-done.6
  100.7 0.0 copy-done.8
  100.7 0.0 copy-start
  100.7 0.0 copy-start.1
  100.7 0.0 copy-start.2
  100.7 0.0 copy-start.3
  100.7 0.0 copy-start.7
  100.7 6.6 %field.1.sky_ref = f32[32,128,128]{2,1,0:T(8,128)S(1)} custom-call(s32[1]{0:T(128)} %bitcast.4.info_ref, f32[32,2]{1,0:T(8,128)S(1)} %copy-done.8, f32[32,128,128]{2,1,0:T(8,128)S(1)} %all-to-all-done.1.field_ref, f32[128,128]{1,0:T(8,128)S(1)} %copy-done.6, bf16[256,256]{1,0:T(8,128)(2,1)S(1)} %copy-done.5, f32[2,128,128]{2,1,0:T(8,128)S(1)} %copy-done.4), custom_call_target="tpu_custom_call" | custom-call | flops 10000000000 | bytes 16777216 | tf_op jit(solution)/shard_map/field/pallas_call | solution.py:1017
  107.4 0.0 copy-start.9
  107.4 1.3 copy-done.9
  108.7 44.0 %all-to-all-done.whole_ref = f32[16,256,256]{2,1,0:T(8,128)} async-done(((f32[16,256,256]{2,1,0:T(8,128)}), f32[16,256,256]{2,1,0:T(8,128)}, u32[]{:S(2)}, u32[]{:S(2)}) %all-to-all-start) | async-done | bytes 4194336 | tf_op jit(solution)/shard_map/all_to_all | solution.py:1063
  152.7 0.0 copy-done
  152.7 0.0 copy-done.1
  152.7 0.0 copy-done.2
  152.8 0.0 copy-done.3
  152.8 0.0 copy-done.7
  152.8 0.0 copy-start.10
  152.8 1.6 copy-done.10
  154.4 0.0 copy-start.11
  154.4 74.0 %image.1 = f32[128,4096]{1,0:T(8,128)S(1)} custom-call(f32[16,256,256]{2,1,0:T(8,128)} %all-to-all-done.whole_ref, f32[32,128,128]{2,1,0:T(8,128)S(1)} %copy-done.10, f32[256,128]{1,0:T(8,128)S(1)} %copy-done.2, bf16[256,512]{1,0:T(8,128)(2,1)S(1)} %copy-done, bf16[512,128]{1,0:T(8,128)(2,1)S(1)} %copy-done.3, f32[128,128]{1,0:T(8,128)S(1)} %copy-done.6, ...), custom_call_target="tpu_custom_call" | custom-call | flops 10000000000 | bytes 16777216 | tf_op jit(solution)/shard_map/image/pallas_call | solution.py:1017
  228.3 0.0 copy-done.11
  228.3 1.6 mul.7
Async XLA Ops:
  43.3 52.8 %all-to-all-start.1 = ((f32[32,128,128]{2,1,0:T(8,128)}), f32[32,128,128]{2,1,0:T(8,128)S(1)}, u32[]{:S(2)}, u32[]{:S(2)}) async-start(f32[32,128,128]{2,1,0:T(8,128)} %get-tuple-element.8), calls=%async_computation.1 | async-start | bytes 4194304 | tf_op jit(solution)/shard_map/all_to_all | solution.py:1048
  87.4 13.2 %copy-start.4 = (f32[2,128,128]{2,1,0:T(8,128)S(1)}, f32[2,128,128]{2,1,0:T(8,128)}, u32[]{:S(2)}) copy-start(f32[2,128,128]{2,1,0:T(8,128)} %constant.56.clone.slope_ref) | copy-start | bytes 393220
  87.4 13.2 %copy-start.5 = (bf16[256,256]{1,0:T(8,128)(2,1)S(1)}, bf16[256,256]{1,0:T(8,128)(2,1)}, u32[]{:S(2)}) copy-start(bf16[256,256]{1,0:T(8,128)(2,1)} %constant.52.clone.mat_ref) | copy-start | bytes 393220
  87.4 13.2 %copy-start.6 = (f32[128,128]{1,0:T(8,128)S(1)}, f32[128,128]{1,0:T(8,128)}, u32[]{:S(2)}) copy-start(f32[128,128]{1,0:T(8,128)} %constant.51.clone.turn_ref) | copy-start | bytes 196612
  87.4 13.2 %copy-start.8 = (f32[32,2]{1,0:T(8,128)S(1)}, f32[32,2]{1,0:T(8,128)}, u32[]{:S(2)}) copy-start(f32[32,2]{1,0:T(8,128)} %constant.57.clone.bend_ref) | copy-start | bytes 772
  96.1 56.7 %all-to-all-start = ((f32[16,256,256]{2,1,0:T(8,128)}), f32[16,256,256]{2,1,0:T(8,128)}, u32[]{:S(2)}, u32[]{:S(2)}) async-start(f32[16,256,256]{2,1,0:T(8,128)} %grid_rows_two.1), calls=%async_computation | async-start | bytes 8388608 | tf_op jit(solution)/shard_map/all_to_all | solution.py:1063
  100.7 52.1 %copy-start = (bf16[256,512]{1,0:T(8,128)(2,1)S(1)}, bf16[256,512]{1,0:T(8,128)(2,1)}, u32[]{:S(2)}) copy-start(bf16[256,512]{1,0:T(8,128)(2,1)} %constant.55.clone.mat_g_ref) | copy-start | bytes 786436
  100.7 52.1 %copy-start.1 = (bf16[2,256,256]{2,1,0:T(8,128)(2,1)S(1)}, bf16[2,256,256]{2,1,0:T(8,128)(2,1)}, u32[]{:S(2)}) copy-start(bf16[2,256,256]{2,1,0:T(8,128)(2,1)} %constant.46.clone.mat_r_ref) | copy-start | bytes 786436
  100.7 52.1 %copy-start.2 = (f32[256,128]{1,0:T(8,128)S(1)}, f32[256,128]{1,0:T(8,128)}, u32[]{:S(2)}) copy-start(f32[256,128]{1,0:T(8,128)} %constant.54.clone.turn_g_ref) | copy-start | bytes 393220
  100.7 52.0 %copy-start.3 = (bf16[512,128]{1,0:T(8,128)(2,1)S(1)}, bf16[512,128]{1,0:T(8,128)(2,1)}, u32[]{:S(2)}) copy-start(bf16[512,128]{1,0:T(8,128)(2,1)} %constant.53.clone.mat_f_ref) | copy-start | bytes 393220
  100.7 52.0 %copy-start.7 = (f32[32,2,128]{2,1,0:T(2,128)S(1)}, f32[32,2,128]{2,1,0:T(2,128)}, u32[]{:S(2)}) copy-start(f32[32,2,128]{2,1,0:T(2,128)} %constant.44.clone.turn_ref.turn_r_ref) | copy-start | bytes 98308
  107.4 1.3 copy-start.9
  152.8 1.6 copy-start.10
  154.4 74.0 %copy-start.11 = (f32[128,4096]{1,0:T(8,128)S(1)}, f32[128,4096]{1,0:T(8,128)}, u32[]{:S(2)}) copy-start(f32[128,4096]{1,0:T(8,128)} %amplitude_ref.1) | copy-start | bytes 6291460

commit v7 on v6

--- a/solution.py
+++ b/solution.py
@@ -1072,7 +1072,7 @@
         [work],
         "field",
     )
-    pieces = 4
+    pieces = 8
     dma = pltpu.SemaphoreType.DMA
     return amplitude * column_call(
         functools.partial(image_kernel, 1.0 / size),

time: 230 us -> 232 us (level)
  no operation moved by 1% of the time
where the time goes in v7:
time: 232 us
  Pallas kernels  164 us (71%)
  waiting for transfers between devices  53.9 us (23%)
  starting transfers between devices  7.28 us (3%)
  other arithmetic  3.04 us (1%)
  local copies, waits for them, and re-layouts  2.97 us (1%)
    pallas_call x2, Pallas kernels, column_call(): pl.pallas_call(kernel, out_shape=jax.ShapeDtypeStruct(out_shape, jnp.floa...  82.5 us
    all_to_all x1, waiting for transfers between devices, shared(): lax.all_to_all(halves, ('base', 'quad'), split_axis=0, concat_axis=0, til...  44 us
    pallas_call x1, Pallas kernels, exchange(): pl.pallas_call(exchange_kernel, out_shape=(jax.ShapeDtypeStruct((ns,) + s...  40.6 us
    pallas_call x1, Pallas kernels, grid_rows_two(): pl.pallas_call(functools.partial(grid_kernel_two, room), out_shape=jax.Sh...  38.6 us
    all_to_all x1, waiting for transfers between devices, shared(): lax.all_to_all(spectrum, parts, split_axis=0, concat_axis=0, tiled=True)  9.87 us
  transfers between devices with their start and end apart: 2, of which 2 were waited for; matrix products, arithmetic and copies ran while one was open for 1% of the time, Pallas kernels for 20%

profile of v7, /device:TPU:0, one launch (start us, length us, event | category | flops | bytes accessed | tf_op | source)
XLA Modules:
  0.0 231.8 jit_solution(3666949513965904201)
XLA Ops:
  0.0 2.7 %pack.1.send_ref = f32[4,65,4,128]{3,2,1,0:T(4,128)} custom-call(s32[1,128]{1,0:T(1,128)} %bitcast.6, s32[1,128]{1,0:T(1,128)} %bitcast.7, f32[128,2,128]{2,1,0:T(2,128)} %residual_ref.1, f32[128,2,128]{2,1,0:T(2,128)} %position_ref.1), custom_call_target="tpu_custom_call" | custom-call | tf_op jit(solution)/shard_map/pack/pallas_call | solution.py:495
  2.7 40.6 %exchange.1 = (f32[8,4,65,4,128]{4,3,2,1,0:T(4,128)}, f32[32,128,128]{2,1,0:T(8,128)}) custom-call(f32[4,65,4,128]{3,2,1,0:T(4,128)} %pack.1.send_ref, f32[128,4096]{1,0:T(8,128)} %xi_ref.1, f32[128,4096]{1,0:T(8,128)} %amplitude_ref.1, f32[32,2,128]{2,1,0:T(2,128)} %constant.44.clone.turn_ref.turn_r_ref, bf16[2,512,128]{2,1,0:T(8,128)(2,1)} %constant.45.clone.mat_ref), custom_call_target="tpu_custom_call" | custom-call | flops 30000001024 | bytes 16777216 | tf_op jit(solution)/shard_map/exchange/pallas_call | solution.py:511
  43.3 2.7 %all-to-all-start.1 = ((f32[32,128,128]{2,1,0:T(8,128)}), f32[32,128,128]{2,1,0:T(8,128)S(1)}, u32[]{:S(2)}, u32[]{:S(2)}) async-start(f32[32,128,128]{2,1,0:T(8,128)} %get-tuple-element.8), calls=%async_computation.1 | async-start | bytes 4194304 | tf_op jit(solution)/shard_map/all_to_all | solution.py:1048
  46.1 1.5 slice_convert_fusion
  47.5 38.6 %grid_rows_two.1 = f32[16,256,256]{2,1,0:T(8,128)} custom-call(s32[32,128]{1,0:T(8,128)} %bitcast.5, f32[2,16,2]{2,1,0:T(8,128)} %constant.47.clone.first_ref, f32[2080,4,128]{2,1,0:T(4,128)} %bitcast.8, f32[2,16,4,128]{3,2,1,0:T(4,128)} %constant.48.clone.turn_ref, f32[2,16,2,128]{3,2,1,0:T(2,128)} %constant.49.clone.undo_ref, ...), custom_call_target="tpu_custom_call" | custom-call | flops 20000000000 | bytes 16777216 | tf_op jit(solution)/shard_map/grid_rows_two/pallas_call | solution.py:733
  86.2 0.0 copy-start.4
  86.2 0.0 copy-start.5
  86.2 0.0 copy-start.6
  86.2 0.0 copy-start.8
  86.2 9.9 %all-to-all-done.1.field_ref = f32[32,128,128]{2,1,0:T(8,128)S(1)} async-done(((f32[32,128,128]{2,1,0:T(8,128)}), f32[32,128,128]{2,1,0:T(8,128)S(1)}, u32[]{:S(2)}, u32[]{:S(2)}) %all-to-all-start.1) | async-done | bytes 2097184 | tf_op jit(solution)/shard_map/all_to_all | solution.py:1048
  96.1 4.5 %all-to-all-start = ((f32[16,256,256]{2,1,0:T(8,128)}), f32[16,256,256]{2,1,0:T(8,128)}, u32[]{:S(2)}, u32[]{:S(2)}) async-start(f32[16,256,256]{2,1,0:T(8,128)} %grid_rows_two.1), calls=%async_computation | async-start | bytes 8388608 | tf_op jit(solution)/shard_map/all_to_all | solution.py:1063
  100.6 0.0 copy-done.4
  100.6 0.0 copy-done.5
  100.7 0.0 copy-done.6
  100.7 0.0 copy-done.8
  100.7 0.0 copy-start
  100.7 0.0 copy-start.1
  100.7 0.0 copy-start.2
  100.7 0.0 copy-start.3
  100.7 0.0 copy-start.7
  100.7 6.6 %field.1.sky_ref = f32[32,128,128]{2,1,0:T(8,128)S(1)} custom-call(s32[1]{0:T(128)} %bitcast.4.info_ref, f32[32,2]{1,0:T(8,128)S(1)} %copy-done.8, f32[32,128,128]{2,1,0:T(8,128)S(1)} %all-to-all-done.1.field_ref, f32[128,128]{1,0:T(8,128)S(1)} %copy-done.6, bf16[256,256]{1,0:T(8,128)(2,1)S(1)} %copy-done.5, f32[2,128,128]{2,1,0:T(8,128)S(1)} %copy-done.4), custom_call_target="tpu_custom_call" | custom-call | flops 10000000000 | bytes 16777216 | tf_op jit(solution)/shard_map/field/pallas_call | solution.py:1017
  107.4 0.0 copy-start.9
  107.4 1.3 copy-done.9
  108.7 44.0 %all-to-all-done.whole_ref = f32[16,256,256]{2,1,0:T(8,128)} async-done(((f32[16,256,256]{2,1,0:T(8,128)}), f32[16,256,256]{2,1,0:T(8,128)}, u32[]{:S(2)}, u32[]{:S(2)}) %all-to-all-start) | async-done | bytes 4194336 | tf_op jit(solution)/shard_map/all_to_all | solution.py:1063
  152.7 0.0 copy-done
  152.7 0.0 copy-done.1
  152.7 0.0 copy-done.2
  152.8 0.0 copy-done.3
  152.8 0.0 copy-done.7
  152.8 0.0 copy-start.10
  152.8 1.6 copy-done.10
  154.4 0.0 copy-start.11
  154.4 75.9 %image.1 = f32[128,4096]{1,0:T(8,128)S(1)} custom-call(f32[16,256,256]{2,1,0:T(8,128)} %all-to-all-done.whole_ref, f32[32,128,128]{2,1,0:T(8,128)S(1)} %copy-done.10, f32[256,128]{1,0:T(8,128)S(1)} %copy-done.2, bf16[256,512]{1,0:T(8,128)(2,1)S(1)} %copy-done, bf16[512,128]{1,0:T(8,128)(2,1)S(1)} %copy-done.3, f32[128,128]{1,0:T(8,128)S(1)} %copy-done.6, ...), custom_call_target="tpu_custom_call" | custom-call | flops 10000000000 | bytes 16777216 | tf_op jit(solution)/shard_map/image/pallas_call | solution.py:1017
  230.2 0.0 copy-done.11
  230.3 1.6 mul.7
Async XLA Ops:
  43.3 52.8 %all-to-all-start.1 = ((f32[32,128,128]{2,1,0:T(8,128)}), f32[32,128,128]{2,1,0:T(8,128)S(1)}, u32[]{:S(2)}, u32[]{:S(2)}) async-start(f32[32,128,128]{2,1,0:T(8,128)} %get-tuple-element.8), calls=%async_computation.1 | async-start | bytes 4194304 | tf_op jit(solution)/shard_map/all_to_all | solution.py:1048
  86.2 14.5 %copy-start.4 = (f32[2,128,128]{2,1,0:T(8,128)S(1)}, f32[2,128,128]{2,1,0:T(8,128)}, u32[]{:S(2)}) copy-start(f32[2,128,128]{2,1,0:T(8,128)} %constant.56.clone.slope_ref) | copy-start | bytes 393220
  86.2 14.5 %copy-start.5 = (bf16[256,256]{1,0:T(8,128)(2,1)S(1)}, bf16[256,256]{1,0:T(8,128)(2,1)}, u32[]{:S(2)}) copy-start(bf16[256,256]{1,0:T(8,128)(2,1)} %constant.52.clone.mat_ref) | copy-start | bytes 393220
  86.2 14.5 %copy-start.6 = (f32[128,128]{1,0:T(8,128)S(1)}, f32[128,128]{1,0:T(8,128)}, u32[]{:S(2)}) copy-start(f32[128,128]{1,0:T(8,128)} %constant.51.clone.turn_ref) | copy-start | bytes 196612
  86.2 14.5 %copy-start.8 = (f32[32,2]{1,0:T(8,128)S(1)}, f32[32,2]{1,0:T(8,128)}, u32[]{:S(2)}) copy-start(f32[32,2]{1,0:T(8,128)} %constant.57.clone.bend_ref) | copy-start | bytes 772
  96.1 56.7 %all-to-all-start = ((f32[16,256,256]{2,1,0:T(8,128)}), f32[16,256,256]{2,1,0:T(8,128)}, u32[]{:S(2)}, u32[]{:S(2)}) async-start(f32[16,256,256]{2,1,0:T(8,128)} %grid_rows_two.1), calls=%async_computation | async-start | bytes 8388608 | tf_op jit(solution)/shard_map/all_to_all | solution.py:1063
  100.7 52.1 %copy-start = (bf16[256,512]{1,0:T(8,128)(2,1)S(1)}, bf16[256,512]{1,0:T(8,128)(2,1)}, u32[]{:S(2)}) copy-start(bf16[256,512]{1,0:T(8,128)(2,1)} %constant.55.clone.mat_g_ref) | copy-start | bytes 786436
  100.7 52.1 %copy-start.1 = (bf16[2,256,256]{2,1,0:T(8,128)(2,1)S(1)}, bf16[2,256,256]{2,1,0:T(8,128)(2,1)}, u32[]{:S(2)}) copy-start(bf16[2,256,256]{2,1,0:T(8,128)(2,1)} %constant.46.clone.mat_r_ref) | copy-start | bytes 786436
  100.7 52.1 %copy-start.2 = (f32[256,128]{1,0:T(8,128)S(1)}, f32[256,128]{1,0:T(8,128)}, u32[]{:S(2)}) copy-start(f32[256,128]{1,0:T(8,128)} %constant.54.clone.turn_g_ref) | copy-start | bytes 393220
  100.7 52.0 %copy-start.3 = (bf16[512,128]{1,0:T(8,128)(2,1)S(1)}, bf16[512,128]{1,0:T(8,128)(2,1)}, u32[]{:S(2)}) copy-start(bf16[512,128]{1,0:T(8,128)(2,1)} %constant.53.clone.mat_f_ref) | copy-start | bytes 393220
  100.7 52.0 %copy-start.7 = (f32[32,2,128]{2,1,0:T(2,128)S(1)}, f32[32,2,128]{2,1,0:T(2,128)}, u32[]{:S(2)}) copy-start(f32[32,2,128]{2,1,0:T(2,128)} %constant.44.clone.turn_ref.turn_r_ref) | copy-start | bytes 98308
  107.4 1.3 copy-start.9
  152.8 1.6 copy-start.10
  154.4 75.9 %copy-start.11 = (f32[128,4096]{1,0:T(8,128)S(1)}, f32[128,4096]{1,0:T(8,128)}, u32[]{:S(2)}) copy-start(f32[128,4096]{1,0:T(8,128)} %amplitude_ref.1) | copy-start | bytes 6291460

commit v8 on v7

--- a/solution.py
+++ b/solution.py
@@ -1072,7 +1072,7 @@
         [work],
         "field",
     )
-    pieces = 8
+    pieces = 2
     dma = pltpu.SemaphoreType.DMA
     return amplitude * column_call(
         functools.partial(image_kernel, 1.0 / size),

time: 232 us -> 229 us (0.987)
  waiting for transfers between devices: 53.9 us -> 50.2 us
    pallas_call x2, Pallas kernels: 82.5 us -> 77.7 us  [column_call(): pl.pallas_call(kernel, out_shape=jax.ShapeDtypeStruct(out_shape, jnp.floa...]
    pallas_call x1, Pallas kernels: 38.6 us -> 42.4 us  [grid_rows_two(): pl.pallas_call(functools.partial(grid_kernel_two, room), out_shape=jax.Sh...]
    all_to_all x1, waiting for transfers between devices: 9.87 us -> 6.16 us  [shared(): lax.all_to_all(spectrum, parts, split_axis=0, concat_axis=0, tiled=True)]
  transfers between devices with their start and end apart: 2 -> 2, of which waited for: 2 -> 2; matrix products, arithmetic and copies ran while one was open for 1% -> 1% of each run, Pallas kernels for 20% -> 22%
where the time goes in v8:
time: 229 us; the launch traced here: 227 us
  Pallas kernels  163 us (71%)
  waiting for transfers between devices  50.2 us (22%)
  starting transfers between devices  7.28 us (3%)
  other arithmetic  3.04 us (1%)
  local copies, waits for them, and re-layouts  2.97 us (1%)
    pallas_call x2, Pallas kernels, column_call(): pl.pallas_call(kernel, out_shape=jax.ShapeDtypeStruct(out_shape, jnp.floa...  77.7 us
    all_to_all x1, waiting for transfers between devices, shared(): lax.all_to_all(halves, ('base', 'quad'), split_axis=0, concat_axis=0, til...  44 us
    pallas_call x1, Pallas kernels, grid_rows_two(): pl.pallas_call(functools.partial(grid_kernel_two, room), out_shape=jax.Sh...  42.4 us
    pallas_call x1, Pallas kernels, exchange(): pl.pallas_call(exchange_kernel, out_shape=(jax.ShapeDtypeStruct((ns,) + s...  40.6 us
    all_to_all x1, waiting for transfers between devices, shared(): lax.all_to_all(spectrum, parts, split_axis=0, concat_axis=0, tiled=True)  6.16 us
  transfers between devices with their start and end apart: 2, of which 2 were waited for; matrix products, arithmetic and copies ran while one was open for 1% of the time, Pallas kernels for 22%

profile of v8, /device:TPU:0, one launch (start us, length us, event | category | flops | bytes accessed | tf_op | source)
XLA Modules:
  0.0 227.0 jit_solution(16105586883851037402)
XLA Ops:
  0.0 2.7 %pack.1.send_ref = f32[4,65,4,128]{3,2,1,0:T(4,128)} custom-call(s32[1,128]{1,0:T(1,128)} %bitcast.6, s32[1,128]{1,0:T(1,128)} %bitcast.7, f32[128,2,128]{2,1,0:T(2,128)} %residual_ref.1, f32[128,2,128]{2,1,0:T(2,128)} %position_ref.1), custom_call_target="tpu_custom_call" | custom-call | tf_op jit(solution)/shard_map/pack/pallas_call | solution.py:495
  2.7 40.6 %exchange.1 = (f32[8,4,65,4,128]{4,3,2,1,0:T(4,128)}, f32[32,128,128]{2,1,0:T(8,128)}) custom-call(f32[4,65,4,128]{3,2,1,0:T(4,128)} %pack.1.send_ref, f32[128,4096]{1,0:T(8,128)} %xi_ref.1, f32[128,4096]{1,0:T(8,128)} %amplitude_ref.1, f32[32,2,128]{2,1,0:T(2,128)} %constant.44.clone.turn_ref.turn_r_ref, bf16[2,512,128]{2,1,0:T(8,128)(2,1)} %constant.45.clone.mat_ref), custom_call_target="tpu_custom_call" | custom-call | flops 30000001024 | bytes 16777216 | tf_op jit(solution)/shard_map/exchange/pallas_call | solution.py:511
  43.3 2.7 %all-to-all-start.1 = ((f32[32,128,128]{2,1,0:T(8,128)}), f32[32,128,128]{2,1,0:T(8,128)S(1)}, u32[]{:S(2)}, u32[]{:S(2)}) async-start(f32[32,128,128]{2,1,0:T(8,128)} %get-tuple-element.8), calls=%async_computation.1 | async-start | bytes 4194304 | tf_op jit(solution)/shard_map/all_to_all | solution.py:1048
  46.1 1.5 slice_convert_fusion
  47.5 42.4 %grid_rows_two.1 = f32[16,256,256]{2,1,0:T(8,128)} custom-call(s32[32,128]{1,0:T(8,128)} %bitcast.5, f32[2,16,2]{2,1,0:T(8,128)} %constant.47.clone.first_ref, f32[2080,4,128]{2,1,0:T(4,128)} %bitcast.8, f32[2,16,4,128]{3,2,1,0:T(4,128)} %constant.48.clone.turn_ref, f32[2,16,2,128]{3,2,1,0:T(2,128)} %constant.49.clone.undo_ref, ...), custom_call_target="tpu_custom_call" | custom-call | flops 20000000000 | bytes 16777216 | tf_op jit(solution)/shard_map/grid_rows_two/pallas_call | solution.py:733
  89.9 0.0 copy-start.4
  89.9 0.0 copy-start.5
  89.9 0.0 copy-start.6
  89.9 0.0 copy-start.8
  89.9 6.2 %all-to-all-done.1.field_ref = f32[32,128,128]{2,1,0:T(8,128)S(1)} async-done(((f32[32,128,128]{2,1,0:T(8,128)}), f32[32,128,128]{2,1,0:T(8,128)S(1)}, u32[]{:S(2)}, u32[]{:S(2)}) %all-to-all-start.1) | async-done | bytes 2097184 | tf_op jit(solution)/shard_map/all_to_all | solution.py:1048
  96.1 4.5 %all-to-all-start = ((f32[16,256,256]{2,1,0:T(8,128)}), f32[16,256,256]{2,1,0:T(8,128)}, u32[]{:S(2)}, u32[]{:S(2)}) async-start(f32[16,256,256]{2,1,0:T(8,128)} %grid_rows_two.1), calls=%async_computation | async-start | bytes 8388608 | tf_op jit(solution)/shard_map/all_to_all | solution.py:1063
  100.6 0.0 copy-done.4
  100.6 0.0 copy-done.5
  100.7 0.0 copy-done.6
  100.7 0.0 copy-done.8
  100.7 0.0 copy-start
  100.7 0.0 copy-start.1
  100.7 0.0 copy-start.2
  100.7 0.0 copy-start.3
  100.7 0.0 copy-start.7
  100.7 6.6 %field.1.sky_ref = f32[32,128,128]{2,1,0:T(8,128)S(1)} custom-call(s32[1]{0:T(128)} %bitcast.4.info_ref, f32[32,2]{1,0:T(8,128)S(1)} %copy-done.8, f32[32,128,128]{2,1,0:T(8,128)S(1)} %all-to-all-done.1.field_ref, f32[128,128]{1,0:T(8,128)S(1)} %copy-done.6, bf16[256,256]{1,0:T(8,128)(2,1)S(1)} %copy-done.5, f32[2,128,128]{2,1,0:T(8,128)S(1)} %copy-done.4), custom_call_target="tpu_custom_call" | custom-call | flops 10000000000 | bytes 16777216 | tf_op jit(solution)/shard_map/field/pallas_call | solution.py:1017
  107.4 0.0 copy-start.9
  107.4 1.3 copy-done.9
  108.7 44.0 %all-to-all-done.whole_ref = f32[16,256,256]{2,1,0:T(8,128)} async-done(((f32[16,256,256]{2,1,0:T(8,128)}), f32[16,256,256]{2,1,0:T(8,128)}, u32[]{:S(2)}, u32[]{:S(2)}) %all-to-all-start) | async-done | bytes 4194336 | tf_op jit(solution)/shard_map/all_to_all | solution.py:1063
  152.7 0.0 copy-done
  152.7 0.0 copy-done.1
  152.7 0.0 copy-done.2
  152.8 0.0 copy-done.3
  152.8 0.0 copy-done.7
  152.8 0.0 copy-start.10
  152.8 1.6 copy-done.10
  154.4 0.0 copy-start.11
  154.4 71.1 %image.1 = f32[128,4096]{1,0:T(8,128)S(1)} custom-call(f32[16,256,256]{2,1,0:T(8,128)} %all-to-all-done.whole_ref, f32[32,128,128]{2,1,0:T(8,128)S(1)} %copy-done.10, f32[256,128]{1,0:T(8,128)S(1)} %copy-done.2, bf16[256,512]{1,0:T(8,128)(2,1)S(1)} %copy-done, bf16[512,128]{1,0:T(8,128)(2,1)S(1)} %copy-done.3, f32[128,128]{1,0:T(8,128)S(1)} %copy-done.6, ...), custom_call_target="tpu_custom_call" | custom-call | flops 10000000000 | bytes 16777216 | tf_op jit(solution)/shard_map/image/pallas_call | solution.py:1017
  225.4 0.0 copy-done.11
  225.4 1.6 mul.7
Async XLA Ops:
  43.3 52.8 %all-to-all-start.1 = ((f32[32,128,128]{2,1,0:T(8,128)}), f32[32,128,128]{2,1,0:T(8,128)S(1)}, u32[]{:S(2)}, u32[]{:S(2)}) async-start(f32[32,128,128]{2,1,0:T(8,128)} %get-tuple-element.8), calls=%async_computation.1 | async-start | bytes 4194304 | tf_op jit(solution)/shard_map/all_to_all | solution.py:1048
  89.9 10.8 %copy-start.4 = (f32[2,128,128]{2,1,0:T(8,128)S(1)}, f32[2,128,128]{2,1,0:T(8,128)}, u32[]{:S(2)}) copy-start(f32[2,128,128]{2,1,0:T(8,128)} %constant.56.clone.slope_ref) | copy-start | bytes 393220
  89.9 10.8 %copy-start.5 = (bf16[256,256]{1,0:T(8,128)(2,1)S(1)}, bf16[256,256]{1,0:T(8,128)(2,1)}, u32[]{:S(2)}) copy-start(bf16[256,256]{1,0:T(8,128)(2,1)} %constant.52.clone.mat_ref) | copy-start | bytes 393220
  89.9 10.8 %copy-start.6 = (f32[128,128]{1,0:T(8,128)S(1)}, f32[128,128]{1,0:T(8,128)}, u32[]{:S(2)}) copy-start(f32[128,128]{1,0:T(8,128)} %constant.51.clone.turn_ref) | copy-start | bytes 196612
  89.9 10.8 %copy-start.8 = (f32[32,2]{1,0:T(8,128)S(1)}, f32[32,2]{1,0:T(8,128)}, u32[]{:S(2)}) copy-start(f32[32,2]{1,0:T(8,128)} %constant.57.clone.bend_ref) | copy-start | bytes 772
  96.1 56.7 %all-to-all-start = ((f32[16,256,256]{2,1,0:T(8,128)}), f32[16,256,256]{2,1,0:T(8,128)}, u32[]{:S(2)}, u32[]{:S(2)}) async-start(f32[16,256,256]{2,1,0:T(8,128)} %grid_rows_two.1), calls=%async_computation | async-start | bytes 8388608 | tf_op jit(solution)/shard_map/all_to_all | solution.py:1063
  100.7 52.1 %copy-start = (bf16[256,512]{1,0:T(8,128)(2,1)S(1)}, bf16[256,512]{1,0:T(8,128)(2,1)}, u32[]{:S(2)}) copy-start(bf16[256,512]{1,0:T(8,128)(2,1)} %constant.55.clone.mat_g_ref) | copy-start | bytes 786436
  100.7 52.1 %copy-start.1 = (bf16[2,256,256]{2,1,0:T(8,128)(2,1)S(1)}, bf16[2,256,256]{2,1,0:T(8,128)(2,1)}, u32[]{:S(2)}) copy-start(bf16[2,256,256]{2,1,0:T(8,128)(2,1)} %constant.46.clone.mat_r_ref) | copy-start | bytes 786436
  100.7 52.1 %copy-start.2 = (f32[256,128]{1,0:T(8,128)S(1)}, f32[256,128]{1,0:T(8,128)}, u32[]{:S(2)}) copy-start(f32[256,128]{1,0:T(8,128)} %constant.54.clone.turn_g_ref) | copy-start | bytes 393220
  100.7 52.0 %copy-start.3 = (bf16[512,128]{1,0:T(8,128)(2,1)S(1)}, bf16[512,128]{1,0:T(8,128)(2,1)}, u32[]{:S(2)}) copy-start(bf16[512,128]{1,0:T(8,128)(2,1)} %constant.53.clone.mat_f_ref) | copy-start | bytes 393220
  100.7 52.0 %copy-start.7 = (f32[32,2,128]{2,1,0:T(2,128)S(1)}, f32[32,2,128]{2,1,0:T(2,128)}, u32[]{:S(2)}) copy-start(f32[32,2,128]{2,1,0:T(2,128)} %constant.44.clone.turn_ref.turn_r_ref) | copy-start | bytes 98308
  107.4 1.3 copy-start.9
  152.8 1.6 copy-start.10
  154.4 71.1 %copy-start.11 = (f32[128,4096]{1,0:T(8,128)S(1)}, f32[128,4096]{1,0:T(8,128)}, u32[]{:S(2)}) copy-start(f32[128,4096]{1,0:T(8,128)} %amplitude_ref.1) | copy-start | bytes 6291460
